TPU v7x, 256 devices: a whole 4x4x8 slice. The times are simulated.
256 devices in a mesh: rep: 4 (over z_hi), exp: 64 (over z_lo, x, y, core).
Axes of the slice: x: 4, y: 4, z: 8 (z_hi: 4, z_lo: 2; z = z_hi * 2 + z_lo), core: 2. Of those that a mesh axis runs over, the one named last changes fastest.
Arguments:
- act_a: bfloat16 [32768, 3584], P(('rep', 'exp')), may hold values from -6 to 6
- grad_a: bfloat16 [32768, 2, 1024], P(('rep', 'exp')), may hold values from -0.125 to 0.125
- route_a: int32 [32768, 2], P(('rep', 'exp')), may hold values from 0 to 63, all different within a row; in each aligned block of 128 rows (0 to 127, 128 to 255, ...) at most 5 rows name the same one
- act_b: bfloat16 [32768, 3584], P(('rep', 'exp')), may hold values from -6 to 6
- grad_b: bfloat16 [32768, 2, 1024], P(('rep', 'exp')), may hold values from -0.125 to 0.125
- route_b: int32 [32768, 2], P(('rep', 'exp')), may hold values from 0 to 31, all different within a row; in each aligned block of 128 rows (0 to 127, 128 to 255, ...) at most 10 rows name the same one
Outputs:
- wgrad_a: bfloat16 [64, 3584, 1024], P('exp', 'rep')
- wgrad_b: bfloat16 [64, 1792, 1024], P('exp', 'rep')
Inputs may be any that keep to these rules, and one draw needn't show every extreme that they name: `route_a`: each token names 2 different experts of layer A; the 128 tokens of one device name any one expert at most 5 times. `route_b`: each token names 2 different experts of layer B; the 128 tokens of one device name any one expert at most 2 * 5 times.
All inputs are finite; a program needn't handle non-finite values.
Results may differ from a plain program's by a relative error of at most 0.013.
Values may be sent and summed in bfloat16 or wider, within the bound.
No kernel may reach another device: no remote copies, remote signals or barrier semaphores. Data moves between devices by JAX's collectives and lax.ppermute only.
A program may use at most 128 MiB of HBM per device.

v0:
```python
import jax
import jax.numpy as jnp
from jax import lax
from jax.sharding import PartitionSpec as P


def sent_together(arrays, axis, split_dim, concat_dim, along):
    ends, at = ([], 0)
    for a in arrays[:-1]:
        at += a.shape[along]
        ends.append(at)
    both = jnp.concatenate(arrays, axis=along)
    return tuple(
        jnp.split(
            lax.all_to_all(both, axis, split_axis=split_dim, concat_axis=concat_dim, tiled=True),
            ends,
            axis=along,
        )
    )


def sent_to_all(array, axis):
    size = lax.axis_size(axis)
    return lax.all_to_all(
        jnp.broadcast_to(array[None], (size, *array.shape)), axis, 0, 0, tiled=True
    )


def joined_along(parts, dim):
    parts = jnp.moveaxis(parts, 0, dim)
    dims = parts.shape
    return parts.reshape(*dims[:dim], dims[dim] * dims[dim + 1], *dims[dim + 2 :])


def gather_directly(array, axis, dim):
    parts = sent_to_all(array, axis)
    return joined_along(parts, dim)


def from_partner(block, axis, apart):
    count = lax.axis_size(axis)
    route = []
    for low in range(count):
        high = low | 1 << apart
        if high != low and high < count:
            route += [(low, high), (high, low)]
    return lax.ppermute(block, axis, route)


def slot_sources(route, experts, stride, slot_count):
    flat_ids = route.reshape(-1)
    onehot = (flat_ids[:, None] == jnp.arange(experts, dtype=jnp.int32)[None, :]).astype(jnp.int32)
    before = jnp.cumsum(onehot, axis=0) - onehot
    position = jnp.sum(before * onehot, axis=1)
    slot_index = flat_ids * stride + position
    pair_ids = jnp.arange(flat_ids.shape[0], dtype=jnp.int32)
    return jnp.full((slot_count,), -1, jnp.int32).at[slot_index].set(pair_ids)


def fill_rows(acts, grads, sources, top_count):
    filled = (sources >= 0)[:, None]
    clamped = jnp.maximum(sources, 0)
    rows_act = jnp.where(filled, acts[clamped // top_count], jnp.zeros((), acts.dtype))
    flat_grads = grads.reshape(-1, grads.shape[-1])
    rows_grad = jnp.where(filled, flat_grads[clamped], jnp.zeros((), grads.dtype))
    return (rows_act, rows_grad)


def contract(left, right):
    return lax.dot_general(
        left, right, (((0,), (0,)), ((), ())), preferred_element_type=jnp.float32
    )


def shards(act_a, grad_a, route_a, act_b, grad_b, route_b):
    exp_count = lax.axis_size("exp")
    token_count = act_a.shape[0]
    top_count = route_a.shape[1]
    features = act_a.shape[1]
    hidden = grad_a.shape[2]
    most_rows = token_count * top_count * 5 // (4 * exp_count)
    sources_a = slot_sources(route_a, exp_count, most_rows, exp_count * most_rows)
    send_act, send_grad = fill_rows(act_a, grad_a, sources_a, top_count)
    recv_act, recv_grad = sent_together((send_act, send_grad), "exp", 0, 0, 1)
    columns_mine = lax.all_to_all(recv_act, "rep", split_axis=1, concat_axis=0, tiled=True)
    owned_a = contract(columns_mine, gather_directly(recv_grad, "rep", 0))
    wgrad_a = owned_a.astype(jnp.bfloat16)[None]
    half_exp = exp_count // 2
    sources_b = slot_sources(route_b, half_exp, 2 * most_rows, exp_count * most_rows)
    send_act_b, send_grad_b = fill_rows(act_b, grad_b, sources_b, top_count)
    recv_act_b, recv_grad_b = sent_together((send_act_b, send_grad_b), "exp", 0, 0, 1)
    partial_value = (
        contract(recv_act_b, recv_grad_b).astype(jnp.bfloat16).reshape(2, features // 2, hidden)
    )
    parity = lax.axis_index("exp") % 2
    kept_half = lax.dynamic_index_in_dim(partial_value, parity, 0, keepdims=False)
    sent_half = lax.dynamic_index_in_dim(partial_value, 1 - parity, 0, keepdims=False)
    arrived = from_partner(sent_half, "exp", 0)
    paired = (kept_half.astype(jnp.float32) + arrived.astype(jnp.float32)).astype(jnp.bfloat16)
    owned_b = lax.psum_scatter(paired, "rep", scatter_dimension=0, tiled=True).astype(jnp.float32)
    wgrad_b = owned_b.astype(jnp.bfloat16)[None]
    return (wgrad_a, wgrad_b)


def solution(mesh):
    return jax.shard_map(
        shards,
        mesh=mesh,
        in_specs=(
            P(("rep", "exp"), None),
            P(("rep", "exp"), None, None),
            P(("rep", "exp"), None),
            P(("rep", "exp"), None),
            P(("rep", "exp"), None, None),
            P(("rep", "exp"), None),
        ),
        out_specs=(P("exp", "rep", None), P("exp", "rep", None)),
        check_vma=False,
    )
```

profile of v0, /device:TPU:34, one launch (start us, length us, event | category | flops | bytes accessed | tf_op | source)
XLA Modules:
  0.0 382.3 jit_solution(356382941867029190)
XLA Ops:
  7.2 0.9 copy.14
  8.2 0.1 eq.60
  8.3 0.7 broadcast_multiply_fusion
  9.0 0.6 reduce-window.16
  9.6 0.2 slice_reduce_fusion.1
  10.0 0.1 mul.44
  10.2 1.4 scatter_custom_fusion.1
  11.7 3.1 gather_fusion.2
  14.8 2.7 gather.25
  17.5 0.1 broadcast_in_dim.79
  17.6 1.2 reshape.147
  18.9 2.1 gather_fusion.3
  21.0 0.3 gather.27
  21.3 2.4 broadcast_select_fusion
  23.7 0.2 broadcast_select_fusion.2
  23.9 3.0 pad_maximum_fusion.1
  26.9 9.4 %all-to-all-start.3 = ((bf16[64,5,4608]{2,1,0:T(8,128)(2,1)}), bf16[64,5,4608]{2,1,0:T(8,128)(2,1)}, u32[]{:S(2)}, u32[]{:S(2)}) async-start(bf16[64,5,4608]{2,1,0:T(8,128)(2,1)} %pad_maximum_fusion.1), calls=%async_computation.3 | async-start | bytes 9437184 | tf_op jit(solution)/shard_map/all_to_all | solution.py:15
  36.4 0.1 eq.56
  36.5 0.1 eq.52
  36.7 0.6 reduce-window.14
  37.3 0.2 slice_reduce_fusion
  37.6 0.1 mul.40
  37.9 1.6 scatter_custom_fusion
  39.5 3.1 gather_fusion
  42.7 2.7 gather.21
  45.4 0.1 broadcast_in_dim.70
  45.5 1.2 reshape.145
  46.8 2.1 gather_fusion.1
  48.9 0.3 gather.23
  49.1 0.2 broadcast_select_fusion.3
  49.3 2.4 broadcast_select_fusion.1
  51.7 3.0 pad_maximum_fusion
  54.7 40.7 %all-to-all-done.3 = bf16[64,5,4608]{2,1,0:T(8,128)(2,1)} async-done(((bf16[64,5,4608]{2,1,0:T(8,128)(2,1)}), bf16[64,5,4608]{2,1,0:T(8,128)(2,1)}, u32[]{:S(2)}, u32[]{:S(2)}) %all-to-all-start.3) | async-done | bytes 2949152 | tf_op jit(solution)/shard_map/all_to_all | solution.py:15
  95.4 8.5 %all-to-all-start = ((bf16[64,5,4608]{2,1,0:T(8,128)(2,1)}), bf16[64,5,4608]{2,1,0:T(8,128)(2,1)}, u32[]{:S(2)}, u32[]{:S(2)}) async-start(bf16[64,5,4608]{2,1,0:T(8,128)(2,1)} %pad_maximum_fusion), calls=%async_computation | async-start | bytes 9437184 | tf_op jit(solution)/shard_map/all_to_all | solution.py:15
  103.9 5.1 %all_to_all.34 = bf16[320,4608]{1,0:T(8,128)(2,1)} reshape(bf16[64,5,4608]{2,1,0:T(8,128)(2,1)} %all-to-all-done.3) | data formatting | bytes 5898240 | tf_op jit(solution)/shard_map/all_to_all | solution.py:15
  108.9 5.8 %convolution_convert_fusion = bf16[3584,1024]{1,0:T(8,128)(2,1)S(1)} fusion(bf16[320,4608]{1,0:T(8,128)(2,1)} %all_to_all.34), kind=kOutput, calls=%fused_computation.6 | convolution fusion | flops 2352480256 | bytes 10289152 | tf_op jit(solution)/shard_map/dot_general | solution.py:70
  114.7 2.5 dynamic-slice_bitcast_fusion
  117.2 1.7 copy-done.3
  119.0 43.9 %all-to-all-done = bf16[64,5,4608]{2,1,0:T(8,128)(2,1)} async-done(((bf16[64,5,4608]{2,1,0:T(8,128)(2,1)}), bf16[64,5,4608]{2,1,0:T(8,128)(2,1)}, u32[]{:S(2)}, u32[]{:S(2)}) %all-to-all-start) | async-done | bytes 2949152 | tf_op jit(solution)/shard_map/all_to_all | solution.py:15
  163.0 5.0 %all_to_all.28 = bf16[320,4608]{1,0:T(8,128)(2,1)} reshape(bf16[64,5,4608]{2,1,0:T(8,128)(2,1)} %all-to-all-done) | data formatting | bytes 5898240 | tf_op jit(solution)/shard_map/all_to_all | solution.py:15
  168.0 1.6 slice-done
  169.6 1.6 copy.23
  171.3 7.6 %all-to-all-start.1 = ((bf16[320,4,896]{2,0,1:T(8,128)(2,1)}), bf16[320,4,896]{2,0,1:T(8,128)(2,1)S(1)}, u32[]{:S(2)}, u32[]{:S(2)}) async-start(bf16[320,4,896]{2,0,1:T(8,128)(2,1)} %bitcast.66), calls=%async_computation.1 | async-start | bytes 4587520 | tf_op jit(solution)/shard_map/all_to_all | solution.py:85
  178.8 6.9 %fusion = bf16[1792,1024]{1,0:T(8,128)(2,1)} fusion(bf16[1792,1024]{1,0:T(8,128)(2,1)} %collective-permute-done, bf16[2,1792,1024]{2,1,0:T(8,128)(2,1)} %bitcast.68, s32[]{:T(128)S(6)} %select_n.79), kind=kLoop, calls=%fused_computation.8 | loop fusion | flops 7340032 | bytes 11010052 | tf_op jit(solution)/shard_map/convert_element_type | solution.py:99
  185.8 130.6 %all-to-all-done.1 = bf16[320,4,896]{2,0,1:T(8,128)(2,1)S(1)} async-done(((bf16[320,4,896]{2,0,1:T(8,128)(2,1)}), bf16[320,4,896]{2,0,1:T(8,128)(2,1)S(1)}, u32[]{:S(2)}, u32[]{:S(2)}) %all-to-all-start.1) | async-done | bytes 2293792 | tf_op jit(solution)/shard_map/all_to_all | solution.py:85
  316.3 0.3 broadcast_in_dim.77
  316.6 55.0 %all_to_all.39 = bf16[4,320,1024]{2,1,0:T(8,128)(2,1)S(1)} all-to-all(bf16[4,320,1024]{2,1,0:T(8,128)(2,1)S(1)} %broadcast_in_dim.77), channel_id=1, replica_groups=mesh['rep'=4,'exp'=64] {'rep'}, dimensions={0} | all-to-all | bytes 5242880 | tf_op jit(solution)/shard_map/all_to_all | solution.py:24
  371.7 3.8 %fusion.4 = bf16[1,896,1024]{2,1,0:T(8,128)(2,1)} fusion(bf16[4,320,1024]{2,1,0:T(8,128)(2,1)S(1)} %all_to_all.39, bf16[320,4,896]{2,0,1:T(8,128)(2,1)S(1)} %all-to-all-done.1), kind=kOutput, calls=%fused_computation.19 | convolution fusion | flops 2349727744 | bytes 6750208 | tf_op jit(solution)/shard_map/dot_general | solution.py:70
  (40 shorter events, 1.0 us)
Async XLA Ops:
  7.2 4.5 %copy-start = (bf16[128,3584]{1,0:T(8,128)(2,1)S(1)}, bf16[128,3584]{1,0:T(8,128)(2,1)}, u32[]{:S(2)}) copy-start(bf16[128,3584]{1,0:T(8,128)(2,1)} %param.9) | copy-start | bytes 2752516
  26.9 9.4 %copy-start.4 = (s32[128,2]{0,1:T(2,128)S(1)}, s32[128,2]{0,1:T(2,128)}, u32[]{:S(2)}) copy-start(s32[128,2]{0,1:T(2,128)} %param.8) | copy-start | bytes 3076
  26.9 12.7 %copy-start.2 = (bf16[128,3584]{1,0:T(8,128)(2,1)S(1)}, bf16[128,3584]{1,0:T(8,128)(2,1)}, u32[]{:S(2)}) copy-start(bf16[128,3584]{1,0:T(8,128)(2,1)} %param.6) | copy-start | bytes 2752516
  26.9 68.5 %all-to-all-start.3 = ((bf16[64,5,4608]{2,1,0:T(8,128)(2,1)}), bf16[64,5,4608]{2,1,0:T(8,128)(2,1)}, u32[]{:S(2)}, u32[]{:S(2)}) async-start(bf16[64,5,4608]{2,1,0:T(8,128)(2,1)} %pad_maximum_fusion.1), calls=%async_computation.3 | async-start | bytes 9437184 | tf_op jit(solution)/shard_map/all_to_all | solution.py:15
  95.4 67.6 %all-to-all-start = ((bf16[64,5,4608]{2,1,0:T(8,128)(2,1)}), bf16[64,5,4608]{2,1,0:T(8,128)(2,1)}, u32[]{:S(2)}, u32[]{:S(2)}) async-start(bf16[64,5,4608]{2,1,0:T(8,128)(2,1)} %pad_maximum_fusion), calls=%async_computation | async-start | bytes 9437184 | tf_op jit(solution)/shard_map/all_to_all | solution.py:15
  114.7 4.2 %copy-start.3 = (bf16[3584,1024]{1,0:T(8,128)(2,1)}, bf16[3584,1024]{1,0:T(8,128)(2,1)S(1)}, u32[]{:S(2)}) copy-start(bf16[3584,1024]{1,0:T(8,128)(2,1)S(1)} %convolution_convert_fusion) | copy-start | bytes 22020100
  118.9 59.9 %collective-permute-start = (bf16[1792,1024]{1,0:T(8,128)(2,1)}, bf16[1792,1024]{1,0:T(8,128)(2,1)}, u32[]{:S(2)}, u32[]{:S(2)}) collective-permute-start(bf16[1792,1024]{1,0:T(8,128)(2,1)} %dynamic-slice_bitcast_fusion), channel_id=1, source_target_pairs={{0,1},{1,0},{2,3},{3,2},{4,5},{5,4},{6,7},{7,6},{8,9},{9,8},{10,11... | collective-permute-start | bytes 11010056 | tf_op jit(solution)/shard_map/ppermute | solution.py:47
  168.0 1.6 slice-start
  171.3 145.0 %all-to-all-start.1 = ((bf16[320,4,896]{2,0,1:T(8,128)(2,1)}), bf16[320,4,896]{2,0,1:T(8,128)(2,1)S(1)}, u32[]{:S(2)}, u32[]{:S(2)}) async-start(bf16[320,4,896]{2,0,1:T(8,128)(2,1)} %bitcast.66), calls=%async_computation.1 | async-start | bytes 4587520 | tf_op jit(solution)/shard_map/all_to_all | solution.py:85
  178.8 196.7 %reduce-scatter.2.cloned.1.call-start = ((), (), s32[]{:S(2)}) async-start(), calls=%async_computation.5 | async-start | bytes 4587520 | tf_op jit(solution)/shard_map/reduce_scatter | solution.py:100
  185.7 130.6 %slice-start.1 = ((bf16[320,4608]{1,0:T(8,128)(2,1)}), bf16[320,1024]{1,0:T(8,128)(2,1)S(1)}, s32[]{:S(2)}) async-start(bf16[320,4608]{1,0:T(8,128)(2,1)} %all_to_all.28), calls=%async_computation.7 | async-start | bytes 1310720 | tf_op jit(solution)/shard_map/split | solution.py:14
  371.7 3.8 %copy-start.1 = (bf16[128,3584]{1,0:T(8,128)(2,1)S(1)}, bf16[128,3584]{1,0:T(8,128)(2,1)}, u32[]{:S(2)}) copy-start(bf16[128,3584]{1,0:T(8,128)(2,1)} %param.9) | copy-start | bytes 2752516
Sparse Core Ops, SparseCore 0:
  185.9 157.8 reduce-scatter.1
where the time goes:
time: 383 us; the launch traced here: 382 us
  waiting for transfers between devices  215 us (56%)
  blocking collectives  55 us (14%)
  local copies, waits for them, and re-layouts  42.4 us (11%)
  starting transfers between devices  25.5 us (7%)
  other arithmetic  20.3 us (5%)
  between operations  14.3 us (4%)
  matrix products  9.62 us (3%)
    all_to_all x1, waiting for transfers between devices, shards(): lax.all_to_all(recv_act, 'rep', split_axis=1, concat_axis=0, tiled=True)  131 us
    all_to_all x2, waiting for transfers between devices, sent_together(): lax.all_to_all(both, axis, split_axis=split_dim, concat_axis=concat_dim,...  84.6 us
    all_to_all x1, blocking collectives, sent_to_all(): lax.all_to_all(jnp.broadcast_to(array[None], (size, *array.shape)), axis,...  55 us
    all_to_all x2, starting transfers between devices, sent_together(): lax.all_to_all(both, axis, split_axis=split_dim, concat_axis=concat_dim,...  17.8 us
    gather x4, local copies, waits for them, and re-layouts, fill_rows(): acts[clamped // top_count]  11.6 us
    all_to_all x2, local copies, waits for them, and re-layouts, sent_together(): lax.all_to_all(both, axis, split_axis=split_dim, concat_axis=concat_dim,...  10.1 us
    dot_general x2, matrix products, contract(): lax.dot_general(left, right, (((0,), (0,)), ((), ())), preferred_element_...  9.62 us
  transfers between devices with their start and end apart: 5, of which 3 were waited for; matrix products, arithmetic and copies ran while one was open for 10% of the time, Pallas kernels for 0%

commit v1 on v0

v1 whole, which is shorter than its diff:
```python
import jax
import jax.numpy as jnp
from jax import lax
from jax.sharding import Mesh, PartitionSpec as P

Z = ("zh", "zl")
PLANE = ("x", "y", "c")
ALL = Z + PLANE
BF = jnp.bfloat16


def contract(left, right, dims):
    return lax.dot_general(left, right, (dims, ((), ())), preferred_element_type=jnp.float32)


def positions(ids):
    order = jnp.arange(ids.shape[0], dtype=jnp.int32)
    same = (ids[:, None] == ids[None, :]) & (order[:, None] < order[None, :])
    return jnp.sum(same.astype(jnp.int32), axis=0)


def one_hot(slots, count):
    return (jnp.arange(count, dtype=jnp.int32)[:, None] == slots[None, :]).astype(BF)


def shards(act_a, grad_a, route_a, act_b, grad_b, route_b):
    tokens, top = route_a.shape
    pairs = tokens * top
    features = act_a.shape[1]
    hidden = grad_a.shape[2]
    planes = lax.axis_size(Z)
    spots = lax.axis_size(PLANE)
    chips = spots // 2
    most = 5
    quarter = features // 4
    half = features // 2
    block = features // 8
    my_zl = lax.axis_index("zl")

    ids_a = route_a.reshape(-1)
    pos_a = positions(ids_a)
    info = jnp.zeros((8, hidden), BF)
    info = info.at[0, :pairs].set(ids_a.astype(BF)).at[1, :pairs].set(pos_a.astype(BF))
    grads_a = jnp.concatenate([grad_a.reshape(pairs, hidden), info], axis=0)
    all_grads = lax.all_gather(grads_a, Z, axis=0, tiled=True)
    my_zh = lax.axis_index("zh")
    my_z = 2 * my_zh + my_zl
    sign = 1 - 2 * my_zl
    quarters = jnp.moveaxis(act_a.reshape(tokens, 4, quarter), 1, 0)

    def mine(which):
        return lax.dynamic_index_in_dim(quarters, lax.rem(which + 8, 4), 0, keepdims=False)

    def along(block_in, step):
        return lax.ppermute(block_in, Z, [(z, (z + step * (1 - 2 * (z % 2))) % planes) for z in range(planes)])

    own = mine(my_zh)
    near = [own]
    for to, step in ((my_zh + 2, -3), (my_zh + sign, 2), (my_zh - sign, -1)):
        near.append(along(mine(to), step))
    offsets = (0, -3, -2, -1, 1, 4, 3, 2)
    origin = lax.rem(jnp.stack([my_z + o * sign for o in offsets]) + planes, planes)

    room = 24
    ids_b = route_b.reshape(-1)
    pos_b = positions(ids_b)
    slots_b = (ids_b % chips) * room + (ids_b // chips) * (room // 2) + pos_b
    pick_b = one_hot(slots_b, chips * room)
    pick_tok = one_hot(slots_b[0::2], chips * room) + one_hot(slots_b[1::2], chips * room)
    rows_g = contract(pick_b, grad_b.reshape(pairs, hidden), ((1,), (0,))).astype(BF)
    rows_a = contract(pick_tok, act_b, ((1,), (0,))).astype(BF)
    rows_g = jnp.broadcast_to(rows_g.reshape(chips, 1, room, hidden), (chips, 2, room, hidden))
    rows_a = jnp.moveaxis(rows_a.reshape(chips, room, 2, half), 2, 1)
    send_b = jnp.concatenate([rows_a, rows_g], axis=-1).reshape(spots, room, half + hidden)
    recv_b = lax.all_to_all(send_b, PLANE, 0, 0, tiled=True).reshape(spots * room, half + hidden)
    recv_b, near = lax.optimization_barrier((recv_b, near))
    far = [along(n, 1) for n in near]
    recv_ba, recv_bg = recv_b[:, :half], recv_b[:, half:]
    which = (jnp.arange(spots * room, dtype=jnp.int32) % room) // (room // 2)
    parts = [
        contract(jnp.where((which == k)[:, None], recv_ba, jnp.zeros((), BF)), recv_bg, ((0,), (0,))).astype(BF)
        for k in range(2)
    ]
    parts = jnp.stack([p.reshape(4, block, hidden) for p in parts], axis=1).reshape(features, hidden)
    parts, far = lax.optimization_barrier((parts, far))
    acts_in = jnp.concatenate(near + far, axis=0)
    wgrad_b = lax.psum_scatter(parts, Z, scatter_dimension=0, tiled=True)[None]

    info_in = all_grads.reshape(planes, pairs + 8, hidden)[:, pairs : pairs + 2, :pairs]
    ids = info_in[:, 0].astype(jnp.int32)
    pos = info_in[:, 1].astype(jnp.int32)
    src = jnp.arange(planes, dtype=jnp.int32)[:, None]
    slots = (ids % spots) * (planes * most) + src * most + pos
    slots = jnp.where(ids // spots == my_zl, slots, -1)
    total = spots * planes * most
    slots_g = jnp.concatenate([slots, jnp.full((planes, 8), -1, jnp.int32)], axis=1).reshape(-1)
    rows_g = contract(one_hot(slots_g, total), all_grads, ((1,), (0,))).astype(BF)
    slots_t = slots[origin]
    pick_tok = one_hot(slots_t[:, 0::2].reshape(-1), total) + one_hot(slots_t[:, 1::2].reshape(-1), total)
    rows_a = contract(pick_tok, acts_in, ((1,), (0,))).astype(BF)
    recv_g = lax.all_to_all(rows_g, PLANE, 0, 0, tiled=True)
    recv_a = lax.all_to_all(rows_a, PLANE, 0, 0, tiled=True)
    wgrad_a = contract(recv_a, recv_g, ((0,), (0,))).astype(BF)[None]
    return wgrad_a, wgrad_b


def solution(mesh):
    fine = Mesh(mesh.devices.reshape(4, 2, 4, 4, 2), ALL)
    return jax.shard_map(
        shards,
        mesh=fine,
        in_specs=tuple(P(ALL, *([None] * n)) for n in (1, 2, 1, 1, 2, 1)),
        out_specs=(P(("zl",) + PLANE, "zh", None),) * 2,
        check_vma=False,
    )
```

time: 383 us -> 217 us (0.57)
  waiting for transfers between devices: 215 us -> 63 us
  matrix products: 9.62 us -> 34.8 us
  blocking collectives: 55 us -> 38.2 us
  local copies, waits for them, and re-layouts: 42.4 us -> 28.4 us
  other arithmetic: 20.3 us -> 7 us
    all_to_all x3 -> x2, waiting for transfers between devices: 215 us -> 33.4 us  [the longest x1 19.9 us: shards(): recv_a = lax.all_to_all(rows_a, PLANE, 0, 0, tiled=True)]
    ppermute x1 -> x7, waiting for transfers between devices: 0.01 us -> 29.6 us  [along(): lax.ppermute(block_in, Z, [(z, (z + step * (1 - 2 * (z % 2))) % planes) f...]
    dot_general x2 -> x7, matrix products: 9.62 us -> 34.8 us  [contract(): lax.dot_general(left, right, (dims, ((), ())), preferred_element_type=jnp...]
    all_to_all x1, blocking collectives: 55 us -> 38.2 us  [shards(): recv_g = lax.all_to_all(rows_g, PLANE, 0, 0, tiled=True)]
    gather x8 -> x1, local copies, waits for them, and re-layouts: 16.3 us -> 0.56 us  [shards(): slots_t = slots[origin]]
    all_to_all x3 -> x0, local copies, waits for them, and re-layouts: 11.7 us -> none  [the longest x2 10.1 us: sent_together(): lax.all_to_all(both, axis, split_axis=split_dim, concat_axis=concat_dim,...]
    ppermute x1 -> x7, starting transfers between devices: 0.12 us -> 11.2 us  [along(): lax.ppermute(block_in, Z, [(z, (z + step * (1 - 2 * (z % 2))) % planes) f...]
    reshape x2 -> x6, local copies, waits for them, and re-layouts: 2.49 us -> 12.2 us  [the longest x2 10.5 us: shards(): rows_a = jnp.moveaxis(rows_a.reshape(chips, room, 2, half), 2, 1)]
  transfers between devices with their start and end apart: 5 -> 11, of which waited for: 3 -> 4; matrix products, arithmetic and copies ran while one was open for 10% -> 30% of each run, Pallas kernels for 0% -> 0%
where the time goes in v1:
time: 217 us; the launch traced here: 214 us
  waiting for transfers between devices  63 us (29%)
  blocking collectives  38.2 us (18%)
  matrix products  34.8 us (16%)
  local copies, waits for them, and re-layouts  28.4 us (13%)
  starting transfers between devices  28.2 us (13%)
  between operations  14.3 us (7%)
  other arithmetic  7 us (3%)
    all_to_all x1, blocking collectives, shards(): recv_g = lax.all_to_all(rows_g, PLANE, 0, 0, tiled=True)  38.2 us
    dot_general x7, matrix products, contract(): lax.dot_general(left, right, (dims, ((), ())), preferred_element_type=jnp...  34.8 us
    ppermute x7, waiting for transfers between devices, along(): lax.ppermute(block_in, Z, [(z, (z + step * (1 - 2 * (z % 2))) % planes) f...  29.6 us
    all_to_all x1, waiting for transfers between devices, shards(): recv_a = lax.all_to_all(rows_a, PLANE, 0, 0, tiled=True)  19.9 us
    all_to_all x1, waiting for transfers between devices, shards(): lax.all_to_all(send_b, PLANE, 0, 0, tiled=True)  13.5 us
    ppermute x7, starting transfers between devices, along(): lax.ppermute(block_in, Z, [(z, (z + step * (1 - 2 * (z % 2))) % planes) f...  11.2 us
    reshape x2, local copies, waits for them, and re-layouts, shards(): rows_a = jnp.moveaxis(rows_a.reshape(chips, room, 2, half), 2, 1)  10.5 us
    all_to_all x1, starting transfers between devices, shards(): recv_a = lax.all_to_all(rows_a, PLANE, 0, 0, tiled=True)  9.15 us
  transfers between devices with their start and end apart: 11, of which 4 were waited for; matrix products, arithmetic and copies ran while one was open for 30% of the time, Pallas kernels for 0%

profile of v1, /device:TPU:34, one launch (start us, length us, event | category | flops | bytes accessed | tf_op | source)
XLA Modules:
  0.0 213.9 jit_solution(16174927159559629472)
XLA Ops:
  7.2 0.9 copy.29
  8.1 0.7 convert_element_type.75
  8.8 1.2 reshape.352
  10.6 0.2 scatter.9
  10.8 0.8 pad_maximum_fusion.2
  12.1 0.2 slice.66
  12.4 0.2 slice.67
  12.6 2.5 %convolution_convert_fusion = bf16[384,3584]{1,0:T(8,128)(2,1)} fusion(bf16[128,3584]{1,0:T(8,128)(2,1)S(1)} %copy-done, s32[128]{0:T(128)S(1)} %slice.67, s32[128]{0:T(128)S(1)} %slice.66), kind=kOutput, calls=%fused_computation.4 | convolution fusion | flops 354091008 | bytes 3671040 | tf_op jit(solution)/shard_map/dot_general | solution.py:13
  15.0 6.8 %reshape.356 = bf16[16,24,2,1792]{3,2,1,0:T(2,128)(2,1)} reshape(bf16[384,3584]{1,0:T(8,128)(2,1)} %convolution_convert_fusion) | data formatting | bytes 5505024 | tf_op jit(solution)/shard_map/reshape | solution.py:73
  21.8 3.7 %copy.49 = bf16[16,24,2,1792]{3,1,2,0:T(8,128)(2,1)} copy(bf16[16,24,2,1792]{3,2,1,0:T(2,128)(2,1)} %reshape.356) | data formatting | bytes 5505024 | tf_op jit(solution)/shard_map/reshape | solution.py:73
  25.5 0.2 reshape.357
  25.8 0.4 convolution_convert_fusion.4
  26.1 0.2 broadcast_in_dim.29
  26.3 1.2 copy-done.2
  27.5 2.4 %pad_maximum_fusion.1 = bf16[16,2,24,2816]{3,2,1,0:T(8,128)(2,1)} fusion(bf16[16,2,24,1024]{3,2,1,0:T(8,128)(2,1)S(1)} %broadcast_in_dim.29, bf16[16,2,24,1792]{3,2,1,0:T(8,128)(2,1)S(1)} %bitcast.54), kind=kLoop, calls=%fused_computation.10 | loop fusion | flops 8650752 | bytes 8650752 | tf_op jit(solution)/shard_map/concatenate | solution.py:74
  29.9 7.8 %all-to-all-start = ((bf16[32,24,2816]{2,1,0:T(8,128)(2,1)}), bf16[32,24,2816]{2,1,0:T(8,128)(2,1)}, u32[]{:S(2)}, u32[]{:S(2)}) async-start(bf16[32,24,2816]{2,1,0:T(8,128)(2,1)} %bitcast.53), calls=%async_computation | async-start | bytes 8650752 | tf_op jit(solution)/shard_map/all_to_all | solution.py:75
  37.8 0.6 copy.34
  38.5 0.2 copy.36
  38.7 5.9 %collective-permute-start = (bf16[128,896]{1,0:T(8,128)(2,1)S(1)}, bf16[128,896]{1,0:T(8,128)(2,1)S(1)}, u32[]{:S(2)}, u32[]{:S(2)}) collective-permute-start(bf16[128,896]{1,0:T(8,128)(2,1)S(1)} %bitcast.62), channel_id=1, source_target_pairs={{0,160},{32,128},{64,224},{96,192},{128,32},{160,0},{192,96},{224,... | collective-permute-start | bytes 688136 | tf_op jit(solution)/shard_map/ppermute | solution.py:55
  44.9 0.2 copy.38
  45.0 1.1 collective-permute-start.2
  46.4 19.2 %collective-permute-done = bf16[128,896]{1,0:T(8,128)(2,1)S(1)} collective-permute-done((bf16[128,896]{1,0:T(8,128)(2,1)S(1)}, bf16[128,896]{1,0:T(8,128)(2,1)S(1)}, u32[]{:S(2)}, u32[]{:S(2)}) %collective-permute-start) | collective-permute-done | bytes 229408 | tf_op jit(solution)/shard_map/ppermute | solution.py:55
  65.6 10.3 %collective-permute-done.2 = bf16[128,896]{1,0:T(8,128)(2,1)S(1)} collective-permute-done((bf16[128,896]{1,0:T(8,128)(2,1)S(1)}, bf16[128,896]{1,0:T(8,128)(2,1)S(1)}, u32[]{:S(2)}, u32[]{:S(2)}) %collective-permute-start.2) | collective-permute-done | bytes 229408 | tf_op jit(solution)/shard_map/ppermute | solution.py:55
  75.9 13.5 %all-to-all-done = bf16[32,24,2816]{2,1,0:T(8,128)(2,1)} async-done(((bf16[32,24,2816]{2,1,0:T(8,128)(2,1)}), bf16[32,24,2816]{2,1,0:T(8,128)(2,1)}, u32[]{:S(2)}, u32[]{:S(2)}) %all-to-all-start) | async-done | bytes 4325408 | tf_op jit(solution)/shard_map/all_to_all | solution.py:75
  89.5 1.9 collective-permute-start.4
  91.5 1.9 collective-permute-start.6
  93.4 5.4 %convolution_convert_fusion.2 = bf16[1792,1024]{1,0:T(8,128)(2,1)S(1)} fusion(pred[768]{0:T(1024)(128)(4,1)S(1)} %broadcast_compare_fusion.1, bf16[768,2816]{1,0:T(8,128)(2,1)} %bitcast.18), kind=kOutput, calls=%fused_computation.12 | convolution fusion | flops 2821783552 | bytes 7996160 | tf_op jit(solution)/shard_map/dot_general | solution.py:13
  98.8 7.3 %convolution_convert_fusion.1 = bf16[1792,1024]{1,0:T(8,128)(2,1)} fusion(pred[768]{0:T(1024)(128)(4,1)S(1)} %broadcast_compare_fusion, bf16[768,2816]{1,0:T(8,128)(2,1)} %bitcast.18), kind=kOutput, calls=%fused_computation.11 | convolution fusion | flops 2821783552 | bytes 7996160 | tf_op jit(solution)/shard_map/dot_general | solution.py:13
  106.1 2.7 %pad_maximum_fusion = bf16[4,2,448,1024]{3,2,0,1:T(8,128)(2,1)S(1)} fusion(bf16[4,1,448,1024]{3,2,0,1:T(8,128)(2,1)} %bitcast.56, bf16[4,1,448,1024]{3,2,0,1:T(8,128)(2,1)S(1)} %bitcast.55), kind=kLoop, calls=%fused_computation.3 | loop fusion | flops 3670016 | bytes 14680064 | tf_op jit(solution)/shard_map/stack | solution.py:84
  108.8 3.8 %copy.39 = bf16[4,2,448,1024]{3,2,1,0:T(8,128)(2,1)} copy(bf16[4,2,448,1024]{3,2,0,1:T(8,128)(2,1)S(1)} %pad_maximum_fusion) | data formatting | bytes 14680064 | tf_op jit(solution)/shard_map/stack | solution.py:84
  112.8 0.7 constant_dynamic-update-slice_fusion.7
  113.5 0.7 constant_dynamic-update-slice_fusion.6
  114.2 0.7 constant_dynamic-update-slice_fusion.5
  114.9 0.7 constant_dynamic-update-slice_fusion.4
  115.6 0.7 constant_dynamic-update-slice_fusion.3
  116.3 0.7 constant_dynamic-update-slice_fusion.2
  117.0 0.7 constant_dynamic-update-slice_fusion.1
  117.7 0.7 constant_dynamic-update-slice_fusion
  118.5 0.8 fusion.52
  119.4 0.6 gather_fusion
  119.9 0.2 slice.64
  120.1 0.2 slice.65
  120.4 5.6 %convolution_convert_fusion.3 = bf16[1280,896]{1,0:T(8,128)(2,1)} fusion(bf16[1024,896]{1,0:T(8,128)(2,1)} %constant_dynamic-update-slice_fusion, s32[1024]{0:T(1024)S(1)} %bitcast.66, s32[1024]{0:T(1024)S(1)} %bitcast.65), kind=kOutput, calls=%fused_computation.15 | convolution fusion | flops 2360442880 | bytes 4136960 | tf_op jit(solution)/shard_map/dot_general | solution.py:13
  126.0 9.2 %all-to-all-start.1 = ((bf16[32,40,896]{2,1,0:T(8,128)(2,1)}), bf16[32,40,896]{2,1,0:T(8,128)(2,1)}, u32[]{:S(2)}, u32[]{:S(2)}) async-start(bf16[32,40,896]{2,1,0:T(8,128)(2,1)} %bitcast.27), calls=%async_computation.1 | async-start | bytes 4587520 | tf_op jit(solution)/shard_map/all_to_all | solution.py:102
  135.2 8.1 %fusion.4 = bf16[1280,1024]{1,0:T(8,128)(2,1)S(1)} fusion(bf16[2112,1024]{1,0:T(8,128)(2,1)} %all-gather.2.cloned.1.call-done, s32[2112]{0:T(1024)S(1)} %eq.166), kind=kOutput, calls=%fused_computation.13 | convolution fusion | flops 5540495360 | bytes 6955264 | tf_op jit(solution)/shard_map/dot_general | solution.py:13
  143.3 19.9 %all-to-all-done.1 = bf16[32,40,896]{2,1,0:T(8,128)(2,1)} async-done(((bf16[32,40,896]{2,1,0:T(8,128)(2,1)}), bf16[32,40,896]{2,1,0:T(8,128)(2,1)}, u32[]{:S(2)}, u32[]{:S(2)}) %all-to-all-start.1) | async-done | bytes 2293792 | tf_op jit(solution)/shard_map/all_to_all | solution.py:102
  163.3 38.2 %all_to_all.23 = bf16[32,40,1024]{2,1,0:T(8,128)(2,1)S(1)} all-to-all(bf16[32,40,1024]{2,1,0:T(8,128)(2,1)S(1)} %bitcast.59), channel_id=1, replica_groups=mesh['zh'=4,'zl'=2,'x'=4,'y'=4,'c'=2] {'x','y','c'}, dimensions={0} | all-to-all | bytes 5242880 | tf_op jit(solution)/shard_map/all_to_all | solution.py:101
  201.5 5.6 %fusion.16 = bf16[1,896,1024]{2,1,0:T(8,128)(2,1)} fusion(bf16[32,40,896]{2,1,0:T(8,128)(2,1)} %all-to-all-done.1, bf16[32,40,1024]{2,1,0:T(8,128)(2,1)S(1)} %all_to_all.23), kind=kOutput, calls=%fused_computation.26 | convolution fusion | flops 2349727744 | bytes 6750208 | tf_op jit(solution)/shard_map/dot_general | solution.py:13
  (48 shorter events, 2.2 us)
Async XLA Ops:
  7.2 5.4 %copy-start = (bf16[128,3584]{1,0:T(8,128)(2,1)S(1)}, bf16[128,3584]{1,0:T(8,128)(2,1)}, u32[]{:S(2)}) copy-start(bf16[128,3584]{1,0:T(8,128)(2,1)} %param.13) | copy-start | bytes 2752516
  7.2 4.5 %copy-start.5 = (s32[128,2]{0,1:T(2,128)S(1)}, s32[128,2]{0,1:T(2,128)}, u32[]{:S(2)}) copy-start(s32[128,2]{0,1:T(2,128)} %param.15) | copy-start | bytes 3076
  7.2 111.3 %all-gather.2.cloned.1.call-start = ((), (), s32[]{:S(2)}) async-start(), calls=%async_computation.4 | async-start | bytes 4866048 | tf_op jit(solution)/shard_map/all_gather | solution.py:45
  21.8 3.7 %copy-start.4 = (bf16[128,2,1024]{2,1,0:T(2,128)(2,1)S(1)}, bf16[128,2,1024]{2,1,0:T(2,128)(2,1)}, u32[]{:S(2)}) copy-start(bf16[128,2,1024]{2,1,0:T(2,128)(2,1)} %param.14) | copy-start | bytes 1572868
  25.7 1.8 copy-start.2
  29.9 7.9 %copy-start.3 = (bf16[128,3584]{1,0:T(8,128)(2,1)S(1)}, bf16[128,3584]{1,0:T(8,128)(2,1)}, u32[]{:S(2)}) copy-start(bf16[128,3584]{1,0:T(8,128)(2,1)} %param.10) | copy-start | bytes 2752516
  29.9 59.5 %all-to-all-start = ((bf16[32,24,2816]{2,1,0:T(8,128)(2,1)}), bf16[32,24,2816]{2,1,0:T(8,128)(2,1)}, u32[]{:S(2)}, u32[]{:S(2)}) async-start(bf16[32,24,2816]{2,1,0:T(8,128)(2,1)} %bitcast.53), calls=%async_computation | async-start | bytes 8650752 | tf_op jit(solution)/shard_map/all_to_all | solution.py:75
  37.7 169.4 %reduce-scatter.2.cloned.1.call-start = ((), (), s32[]{:S(2)}) async-start(), calls=%async_computation.5 | async-start | bytes 8257536 | tf_op jit(solution)/shard_map/reduce_scatter | solution.py:87
  38.7 26.9 %collective-permute-start = (bf16[128,896]{1,0:T(8,128)(2,1)S(1)}, bf16[128,896]{1,0:T(8,128)(2,1)S(1)}, u32[]{:S(2)}, u32[]{:S(2)}) collective-permute-start(bf16[128,896]{1,0:T(8,128)(2,1)S(1)} %bitcast.62), channel_id=1, source_target_pairs={{0,160},{32,128},{64,224},{96,192},{128,32},{160,0},{192,96},{224,... | collective-permute-start | bytes 688136 | tf_op jit(solution)/shard_map/ppermute | solution.py:55
  44.8 20.8 %collective-permute-start.1 = (bf16[128,896]{1,0:T(8,128)(2,1)S(1)}, bf16[128,896]{1,0:T(8,128)(2,1)S(1)}, u32[]{:S(2)}, u32[]{:S(2)}) collective-permute-start(bf16[128,896]{1,0:T(8,128)(2,1)S(1)} %bitcast.63), channel_id=1, source_target_pairs={{0,64},{32,224},{64,128},{96,32},{128,192},{160,96},{192,0},{224,1... | collective-permute-start | bytes 688136 | tf_op jit(solution)/shard_map/ppermute | solution.py:55
  45.0 30.9 %collective-permute-start.2 = (bf16[128,896]{1,0:T(8,128)(2,1)S(1)}, bf16[128,896]{1,0:T(8,128)(2,1)S(1)}, u32[]{:S(2)}, u32[]{:S(2)}) collective-permute-start(bf16[128,896]{1,0:T(8,128)(2,1)S(1)} %bitcast.64), channel_id=1, source_target_pairs={{0,224},{32,64},{64,32},{96,128},{128,96},{160,192},{192,160},{224... | collective-permute-start | bytes 688136 | tf_op jit(solution)/shard_map/ppermute | solution.py:55
  89.4 23.2 %collective-permute-start.3 = (bf16[128,896]{1,0:T(8,128)(2,1)S(1)}, bf16[128,896]{1,0:T(8,128)(2,1)S(1)}, u32[]{:S(2)}, u32[]{:S(2)}) collective-permute-start(bf16[128,896]{1,0:T(8,128)(2,1)S(1)} %bitcast.60), channel_id=1, source_target_pairs={{0,32},{32,0},{64,96},{96,64},{128,160},{160,128},{192,224},{224,1... | collective-permute-start | bytes 688136 | tf_op jit(solution)/shard_map/ppermute | solution.py:55
  89.5 23.1 %collective-permute-start.4 = (bf16[128,896]{1,0:T(8,128)(2,1)S(1)}, bf16[128,896]{1,0:T(8,128)(2,1)S(1)}, u32[]{:S(2)}, u32[]{:S(2)}) collective-permute-start(bf16[128,896]{1,0:T(8,128)(2,1)S(1)} %collective-permute-done), channel_id=1, source_target_pairs={{0,32},{32,0},{64,96},{96,64},{128,160},{160,128},{192,224},{224,1... | collective-permute-start | bytes 688136 | tf_op jit(solution)/shard_map/ppermute | solution.py:55
  91.4 21.2 %collective-permute-start.5 = (bf16[128,896]{1,0:T(8,128)(2,1)S(1)}, bf16[128,896]{1,0:T(8,128)(2,1)S(1)}, u32[]{:S(2)}, u32[]{:S(2)}) collective-permute-start(bf16[128,896]{1,0:T(8,128)(2,1)S(1)} %collective-permute-done.1), channel_id=1, source_target_pairs={{0,32},{32,0},{64,96},{96,64},{128,160},{160,128},{192,224},{224,1... | collective-permute-start | bytes 688136 | tf_op jit(solution)/shard_map/ppermute | solution.py:55
  91.5 21.1 %collective-permute-start.6 = (bf16[128,896]{1,0:T(8,128)(2,1)S(1)}, bf16[128,896]{1,0:T(8,128)(2,1)S(1)}, u32[]{:S(2)}, u32[]{:S(2)}) collective-permute-start(bf16[128,896]{1,0:T(8,128)(2,1)S(1)} %collective-permute-done.2), channel_id=1, source_target_pairs={{0,32},{32,0},{64,96},{96,64},{128,160},{160,128},{192,224},{224,1... | collective-permute-start | bytes 688136 | tf_op jit(solution)/shard_map/ppermute | solution.py:55
  126.0 37.3 %all-to-all-start.1 = ((bf16[32,40,896]{2,1,0:T(8,128)(2,1)}), bf16[32,40,896]{2,1,0:T(8,128)(2,1)}, u32[]{:S(2)}, u32[]{:S(2)}) async-start(bf16[32,40,896]{2,1,0:T(8,128)(2,1)} %bitcast.27), calls=%async_computation.1 | async-start | bytes 4587520 | tf_op jit(solution)/shard_map/all_to_all | solution.py:102
  201.5 5.6 %copy-start.1 = (bf16[128,3584]{1,0:T(8,128)(2,1)S(1)}, bf16[128,3584]{1,0:T(8,128)(2,1)}, u32[]{:S(2)}) copy-start(bf16[128,3584]{1,0:T(8,128)(2,1)} %param.13) | copy-start | bytes 2752516
Sparse Core Ops, SparseCore 0:
  11.8 76.4 all-gather.1
  112.8 87.3 reduce-scatter.1

commit v2 on v1

v2 whole, which is shorter than its diff:
```python
import functools

import jax
import jax.numpy as jnp
from jax import lax
from jax.experimental import pallas as pl
from jax.sharding import Mesh, PartitionSpec as P

Z = ("zh", "zl")
PLANE = ("x", "y", "c")
ALL = Z + PLANE
BF = jnp.bfloat16
ROOM = 24


def contract(left, right, dims):
    return lax.dot_general(left, right, (dims, ((), ())), preferred_element_type=jnp.float32)


def positions(ids):
    order = jnp.arange(ids.shape[0], dtype=jnp.int32)
    same = (ids[:, None] == ids[None, :]) & (order[:, None] < order[None, :])
    return jnp.sum(same.astype(jnp.int32), axis=0)


def one_hot(slots, count):
    return (jnp.arange(count, dtype=jnp.int32)[:, None] == slots[None, :]).astype(BF)


def fill_kernel(half, s_ref, t_ref, act_ref, grad_ref, out_ref):
    chips = out_ref.shape[0]
    rows = chips * ROOM
    pairs = s_ref.shape[1]
    tokens = t_ref.shape[1]
    pick = (lax.broadcasted_iota(jnp.int32, (rows, pairs), 0) == s_ref[...]).astype(BF)
    spot = lax.broadcasted_iota(jnp.int32, (rows, tokens), 0)
    pick_tok = ((spot == t_ref[0:1, :]) | (spot == t_ref[1:2, :])).astype(BF)
    acts = contract(pick_tok, act_ref[...], ((1,), (0,))).astype(BF)
    grads = contract(pick, grad_ref[...], ((1,), (0,))).astype(BF)
    for p in range(chips):
        out_ref[p, 0, :, :half] = acts[p * ROOM : (p + 1) * ROOM]
        out_ref[p, 0, :, half:] = grads[p * ROOM : (p + 1) * ROOM]


def fill(slots, act, grad, chips):
    tokens, features = act.shape
    pairs, hidden = grad.shape
    half = features // 2
    return pl.pallas_call(
        functools.partial(fill_kernel, half),
        grid=(2,),
        in_specs=[
            pl.BlockSpec((1, pairs), lambda c: (0, 0)),
            pl.BlockSpec((2, tokens), lambda c: (0, 0)),
            pl.BlockSpec((tokens, half), lambda c: (0, c)),
            pl.BlockSpec((pairs, hidden), lambda c: (0, 0)),
        ],
        out_specs=pl.BlockSpec((chips, 1, ROOM, half + hidden), lambda c: (0, c, 0, 0)),
        out_shape=jax.ShapeDtypeStruct((chips, 2, ROOM, half + hidden), BF),
        cost_estimate=pl.CostEstimate(flops=2_000_000_000, bytes_accessed=6_000_000, transcendentals=0),
        name="fill_b",
    )(slots.reshape(1, pairs), slots.reshape(tokens, 2).T, act, grad)


def products_kernel(half, block, in_ref, out_ref):
    count = in_ref.shape[0] * 8
    hidden = in_ref.shape[2] - half

    def rows(tile, start, size):
        return in_ref[:, pl.ds(tile * 8, 8), start : start + size].reshape(count, size)

    shared = (lax.broadcasted_iota(jnp.int32, (count, 1), 0) % 8) // 4
    for pair in range(2):
        for k in range(2):

            @pl.when((pl.program_id(0) == pair) & (pl.program_id(1) == k))
            def _():
                start = pair * 2 * block
                last = jnp.where(shared == k, rows(2, half, hidden), jnp.zeros((), BF))
                total = contract(rows(k, start, 2 * block), rows(k, half, hidden), ((0,), (0,)))
                total = total + contract(rows(2, start, 2 * block), last, ((0,), (0,)))
                out_ref[...] = total.astype(BF).reshape(out_ref.shape)


def products(recv, half):
    hidden = recv.shape[2] - half
    block = half // 4
    return pl.pallas_call(
        functools.partial(products_kernel, half, block),
        grid=(2, 2),
        in_specs=[pl.BlockSpec(recv.shape, lambda r, k: (0, 0, 0))],
        out_specs=pl.BlockSpec((2, 1, block, hidden), lambda r, k: (r, k, 0, 0)),
        out_shape=jax.ShapeDtypeStruct((4, 2, block, hidden), BF),
        cost_estimate=pl.CostEstimate(flops=4_000_000_000, bytes_accessed=12_000_000, transcendentals=0),
        name="products_b",
    )(recv)


def shards(act_a, grad_a, route_a, act_b, grad_b, route_b):
    tokens, top = route_a.shape
    pairs = tokens * top
    features = act_a.shape[1]
    hidden = grad_a.shape[2]
    planes = lax.axis_size(Z)
    spots = lax.axis_size(PLANE)
    chips = spots // 2
    most = 5
    quarter = features // 4
    half = features // 2
    my_zh = lax.axis_index("zh")
    my_zl = lax.axis_index("zl")
    my_z = 2 * my_zh + my_zl
    sign = 1 - 2 * my_zl

    all_grads = lax.all_gather(grad_a.reshape(pairs, hidden), Z, axis=0, tiled=True)
    quarters = jnp.moveaxis(act_a.reshape(tokens, 4, quarter), 1, 0)

    def mine(which):
        return lax.dynamic_index_in_dim(quarters, lax.rem(which + 8, 4), 0, keepdims=False)

    def along(block_in, step):
        return lax.ppermute(block_in, Z, [(z, (z + step * (1 - 2 * (z % 2))) % planes) for z in range(planes)])

    near = [mine(my_zh)]
    for to, step in ((my_zh + 2, -3), (my_zh + sign, 2), (my_zh - sign, -1)):
        near.append(along(mine(to), step))
    offsets = (0, -3, -2, -1, 1, 4, 3, 2)
    origin = lax.rem(jnp.stack([my_z + o * sign for o in offsets]) + planes, planes)

    ids_b = route_b.reshape(-1)
    pos_b = positions(ids_b)
    lower = ids_b // chips
    slots_b = (ids_b % chips) * ROOM + jnp.where(pos_b < 8, lower * 8 + pos_b, 16 + lower * 4 + pos_b - 8)
    send_b = fill(slots_b, act_b, grad_b.reshape(pairs, hidden), chips)
    recv_b = lax.all_to_all(send_b.reshape(spots, ROOM, half + hidden), PLANE, 0, 0, tiled=True)

    ids_a = route_a.reshape(-1)
    slots_a = (ids_a % spots) * (planes * most) + my_z * most + positions(ids_a)
    slots_a = slots_a + (ids_a // spots) * 4096
    slots_a, _ = lax.optimization_barrier((slots_a, send_b))
    slots = lax.all_gather(slots_a, Z, axis=0)
    slots = jnp.where(slots // 4096 == my_zl, slots % 4096, -1)

    far = [along(b, 1) for b in near]
    parts = products(recv_b, half).reshape(features, hidden)
    parts, far = lax.optimization_barrier((parts, far))
    wgrad_b = lax.psum_scatter(parts, Z, scatter_dimension=0, tiled=True)[None]

    total = spots * planes * most
    slots_t = slots[origin]
    pick_tok = one_hot(slots_t[:, 0::2].reshape(-1), total) + one_hot(slots_t[:, 1::2].reshape(-1), total)
    rows_a = contract(pick_tok, jnp.concatenate(near + far, axis=0), ((1,), (0,))).astype(BF)
    recv_a = lax.all_to_all(rows_a, PLANE, 0, 0, tiled=True)
    rows_g = contract(one_hot(slots.reshape(-1), total), all_grads, ((1,), (0,))).astype(BF)
    recv_g = lax.all_to_all(rows_g, PLANE, 0, 0, tiled=True)
    wgrad_a = contract(recv_a, recv_g, ((0,), (0,))).astype(BF)[None]
    return wgrad_a, wgrad_b


def solution(mesh):
    fine = Mesh(mesh.devices.reshape(4, 2, 4, 4, 2), ALL)
    return jax.shard_map(
        shards,
        mesh=fine,
        in_specs=tuple(P(ALL, *([None] * n)) for n in (1, 2, 1, 1, 2, 1)),
        out_specs=(P(("zl",) + PLANE, "zh", None),) * 2,
        check_vma=False,
    )
```

time: 217 us -> 203 us (0.935)
  the two profiles are of different devices: /device:TPU:34 before, /device:TPU:1 now
where the time goes in v2:
time: 203 us; the launch traced here: 202 us
  waiting for transfers between devices  63.9 us (31%)
  blocking collectives  52.1 us (26%)
  starting transfers between devices  32.3 us (16%)
  matrix products  17 us (8%)
  between operations  14.3 us (7%)
  Pallas kernels  12.4 us (6%)
  local copies, waits for them, and re-layouts  8.88 us (4%)
    all_to_all x1, blocking collectives, shards(): recv_g = lax.all_to_all(rows_g, PLANE, 0, 0, tiled=True)  37.7 us
    ppermute x7, waiting for transfers between devices, along(): lax.ppermute(block_in, Z, [(z, (z + step * (1 - 2 * (z % 2))) % planes) f...  26.8 us
    all_to_all x1, waiting for transfers between devices, shards(): recv_a = lax.all_to_all(rows_a, PLANE, 0, 0, tiled=True)  23.1 us
    dot_general x3, matrix products, contract(): lax.dot_general(left, right, (dims, ((), ())), preferred_element_type=jnp...  17 us
    all_gather x1, blocking collectives, shards(): slots = lax.all_gather(slots_a, Z, axis=0)  14.4 us
    all_to_all x1, waiting for transfers between devices, shards(): lax.all_to_all(send_b.reshape(spots, ROOM, half + hidden), PLANE, 0, 0, t...  14 us
    ppermute x7, starting transfers between devices, along(): lax.ppermute(block_in, Z, [(z, (z + step * (1 - 2 * (z % 2))) % planes) f...  12.5 us
    all_to_all x1, starting transfers between devices, shards(): recv_a = lax.all_to_all(rows_a, PLANE, 0, 0, tiled=True)  10.9 us
  transfers between devices with their start and end apart: 11, of which 5 were waited for; matrix products, arithmetic and copies ran while one was open for 12% of the time, Pallas kernels for 6%

profile of v2, /device:TPU:1, one launch (start us, length us, event | category | flops | bytes accessed | tf_op | source)
XLA Modules:
  0.0 202.4 jit_solution(10748562003608446121)
XLA Ops:
  7.2 0.0 all-gather.4.cloned.1.call-start
  7.2 2.0 %reshape.324 = bf16[256,1024]{1,0:T(8,128)(2,1)} reshape(bf16[128,2,1024]{2,1,0:T(2,128)(2,1)} %param.7) | data formatting | bytes 1048576 | tf_op jit(solution)/shard_map/reshape | solution.py:115
  9.3 0.8 copy.38
  10.1 0.1 eq.88
  10.2 0.1 reshape.319
  10.3 0.1 convert_reduce_fusion
  10.5 0.1 reduce_sum.25
  10.6 0.1 copy.40
  10.7 2.1 %reshape.320.grad_ref = bf16[256,1024]{1,0:T(8,128)(2,1)} reshape(bf16[128,2,1024]{2,1,0:T(2,128)(2,1)} %param.10) | data formatting | bytes 1048576 | tf_op jit(solution)/shard_map/reshape | solution.py:134
  12.7 0.6 fusion.23.t_ref
  13.3 0.6 fusion.22.s_ref
  13.9 4.0 %fill_b.1 = bf16[16,2,24,2816]{3,2,1,0:T(8,128)(2,1)} custom-call(s32[1,256]{1,0:T(1,128)} %fusion.22.s_ref, s32[2,128]{1,0:T(2,128)} %fusion.23.t_ref, bf16[128,3584]{1,0:T(8,128)(2,1)} %act_ref.1, bf16[256,1024]{1,0:T(8,128)(2,1)} %reshape.320.grad_ref), custom_call_target="tpu_custom_call" | custom-call | flops 2000000000 | bytes 6000000 | tf_op jit(solution)/shard_map/fill_b/pallas_call | solution.py:49
  18.0 8.8 %all-to-all-start = ((bf16[32,24,2816]{2,1,0:T(8,128)(2,1)}), bf16[32,24,2816]{2,1,0:T(8,128)(2,1)}, u32[]{:S(2)}, u32[]{:S(2)}) async-start(bf16[32,24,2816]{2,1,0:T(8,128)(2,1)} %bitcast.61), calls=%async_computation | async-start | bytes 8650752 | tf_op jit(solution)/shard_map/all_to_all | solution.py:135
  26.7 0.0 reduce-scatter.2.cloned.1.call-start
  26.8 0.6 copy.43
  27.5 0.1 constant_dynamic-slice_fusion
  27.6 0.2 copy.45
  27.7 6.6 %collective-permute-start = (bf16[128,896]{1,0:T(8,128)(2,1)S(1)}, bf16[128,896]{1,0:T(8,128)(2,1)S(1)}, u32[]{:S(2)}, u32[]{:S(2)}) collective-permute-start(bf16[128,896]{1,0:T(8,128)(2,1)S(1)} %bitcast.67), channel_id=1, source_target_pairs={{0,160},{32,128},{64,224},{96,192},{128,32},{160,0},{192,96},{224,... | collective-permute-start | bytes 688136 | tf_op jit(solution)/shard_map/ppermute | solution.py:122
  34.3 0.2 copy.46
  34.4 1.3 collective-permute-start.1
  35.7 0.2 copy.47
  35.9 0.1 collective-permute-start.2
  36.0 0.2 copy.44
  36.1 0.4 collective-permute-start.3
  36.5 17.1 %collective-permute-done = bf16[128,896]{1,0:T(8,128)(2,1)S(1)} collective-permute-done((bf16[128,896]{1,0:T(8,128)(2,1)S(1)}, bf16[128,896]{1,0:T(8,128)(2,1)S(1)}, u32[]{:S(2)}, u32[]{:S(2)}) %collective-permute-start) | collective-permute-done | bytes 229408 | tf_op jit(solution)/shard_map/ppermute | solution.py:122
  53.6 2.0 collective-permute-start.4
  55.6 0.0 collective-permute-start.5
  55.6 8.6 %collective-permute-done.2 = bf16[128,896]{1,0:T(8,128)(2,1)S(1)} collective-permute-done((bf16[128,896]{1,0:T(8,128)(2,1)S(1)}, bf16[128,896]{1,0:T(8,128)(2,1)S(1)}, u32[]{:S(2)}, u32[]{:S(2)}) %collective-permute-start.2) | collective-permute-done | bytes 229408 | tf_op jit(solution)/shard_map/ppermute | solution.py:122
  64.2 2.2 %collective-permute-start.6 = (bf16[128,896]{1,0:T(8,128)(2,1)S(1)}, bf16[128,896]{1,0:T(8,128)(2,1)S(1)}, u32[]{:S(2)}, u32[]{:S(2)}) collective-permute-start(bf16[128,896]{1,0:T(8,128)(2,1)S(1)} %collective-permute-done.2), channel_id=1, source_target_pairs={{0,32},{32,0},{64,96},{96,64},{128,160},{160,128},{192,224},{224,1... | collective-permute-start | bytes 688136 | tf_op jit(solution)/shard_map/ppermute | solution.py:122
  66.4 14.0 %all-to-all-done.in_ref = bf16[32,24,2816]{2,1,0:T(8,128)(2,1)} async-done(((bf16[32,24,2816]{2,1,0:T(8,128)(2,1)}), bf16[32,24,2816]{2,1,0:T(8,128)(2,1)}, u32[]{:S(2)}, u32[]{:S(2)}) %all-to-all-start) | async-done | bytes 4325408 | tf_op jit(solution)/shard_map/all_to_all | solution.py:135
  80.4 8.4 %products_b.1 = bf16[4,2,448,1024]{3,2,1,0:T(8,128)(2,1)} custom-call(bf16[32,24,2816]{2,1,0:T(8,128)(2,1)} %all-to-all-done.in_ref), custom_call_target="tpu_custom_call" | custom-call | flops 4000000000 | bytes 12000000 | tf_op jit(solution)/shard_map/products_b/pallas_call | solution.py:88
  88.8 1.2 collective-permute-done.6
  90.0 0.6 copy-done.2
  90.6 0.1 copy.37
  90.7 0.1 reshape.318
  90.9 0.1 convert_reduce_fusion.1
  91.0 0.1 stack.35
  91.1 14.4 %all-gather.1 = s32[8,1,256]{2,1,0:T(1,128)S(1)} all-gather(s32[1,1,256]{2,1,0:T(1,128)S(1)} %bitcast.70), channel_id=2, replica_groups=mesh['zh'=4,'zl'=2,'x'=4,'y'=4,'c'=2] {'zh','zl'}, dimensions={0}, use_global_device_ids=true | all-gather | bytes 9216 | tf_op jit(solution)/shard_map/all_gather | solution.py:141
  105.6 0.6 gather_fusion
  106.2 0.2 slice.6
  106.4 0.2 slice.7
  106.8 4.1 %convolution_convert_fusion = bf16[1280,896]{1,0:T(8,128)(2,1)} fusion(bf16[1024,896]{1,0:T(8,128)(2,1)S(1)} %constant_dynamic-update-slice_fusion, s32[1024]{0:T(1024)S(1)} %bitcast.72, s32[1024]{0:T(1024)S(1)} %bitcast.71), kind=kOutput, calls=%fused_computation.10 | convolution fusion | flops 2360442880 | bytes 4136960 | tf_op jit(solution)/shard_map/dot_general | solution.py:17
  111.0 10.9 %all-to-all-start.1 = ((bf16[32,40,896]{2,1,0:T(8,128)(2,1)}), bf16[32,40,896]{2,1,0:T(8,128)(2,1)}, u32[]{:S(2)}, u32[]{:S(2)}) async-start(bf16[32,40,896]{2,1,0:T(8,128)(2,1)} %bitcast.21), calls=%async_computation.1 | async-start | bytes 4587520 | tf_op jit(solution)/shard_map/all_to_all | solution.py:153
  122.0 0.0 all-gather.4.cloned.1.call-done
  122.0 7.4 %fusion.4 = bf16[1280,1024]{1,0:T(8,128)(2,1)S(1)} fusion(bf16[2048,1024]{1,0:T(8,128)(2,1)} %all-gather.4.cloned.1.call-done, s32[2048]{0:T(1024)S(1)} %bitcast.69), kind=kOutput, calls=%fused_computation.8 | convolution fusion | flops 5372641280 | bytes 6823936 | tf_op jit(solution)/shard_map/dot_general | solution.py:17
  129.4 23.1 %all-to-all-done.1 = bf16[32,40,896]{2,1,0:T(8,128)(2,1)} async-done(((bf16[32,40,896]{2,1,0:T(8,128)(2,1)}), bf16[32,40,896]{2,1,0:T(8,128)(2,1)}, u32[]{:S(2)}, u32[]{:S(2)}) %all-to-all-start.1) | async-done | bytes 2293792 | tf_op jit(solution)/shard_map/all_to_all | solution.py:153
  152.4 37.7 %all_to_all.23 = bf16[32,40,1024]{2,1,0:T(8,128)(2,1)S(1)} all-to-all(bf16[32,40,1024]{2,1,0:T(8,128)(2,1)S(1)} %bitcast.63), channel_id=1, replica_groups=mesh['zh'=4,'zl'=2,'x'=4,'y'=4,'c'=2] {'x','y','c'}, dimensions={0} | all-to-all | bytes 5242880 | tf_op jit(solution)/shard_map/all_to_all | solution.py:155
  190.1 5.5 %fusion.10 = bf16[1,896,1024]{2,1,0:T(8,128)(2,1)} fusion(bf16[32,40,896]{2,1,0:T(8,128)(2,1)} %all-to-all-done.1, bf16[32,40,1024]{2,1,0:T(8,128)(2,1)S(1)} %all_to_all.23), kind=kOutput, calls=%fused_computation.14 | convolution fusion | flops 2349727744 | bytes 6750208 | tf_op jit(solution)/shard_map/dot_general | solution.py:17
  (26 shorter events, 0.3 us)
Async XLA Ops:
  7.2 5.6 %copy-start.1 = (s32[128,2]{0,1:T(2,128)S(1)}, s32[128,2]{0,1:T(2,128)}, u32[]{:S(2)}) copy-start(s32[128,2]{0,1:T(2,128)} %param.11) | copy-start | bytes 3076
  7.2 114.8 %all-gather.4.cloned.1.call-start = ((), (), s32[]{:S(2)}) async-start(), calls=%async_computation.4 | async-start | bytes 4718592 | tf_op jit(solution)/shard_map/all_gather | solution.py:115
  18.0 8.8 %copy-start = (bf16[128,3584]{1,0:T(8,128)(2,1)S(1)}, bf16[128,3584]{1,0:T(8,128)(2,1)}, u32[]{:S(2)}) copy-start(bf16[128,3584]{1,0:T(8,128)(2,1)} %param.6) | copy-start | bytes 2752516
  18.0 62.4 %all-to-all-start = ((bf16[32,24,2816]{2,1,0:T(8,128)(2,1)}), bf16[32,24,2816]{2,1,0:T(8,128)(2,1)}, u32[]{:S(2)}, u32[]{:S(2)}) async-start(bf16[32,24,2816]{2,1,0:T(8,128)(2,1)} %bitcast.61), calls=%async_computation | async-start | bytes 8650752 | tf_op jit(solution)/shard_map/all_to_all | solution.py:135
  26.7 168.8 %reduce-scatter.2.cloned.1.call-start = ((), (), s32[]{:S(2)}) async-start(), calls=%async_computation.5 | async-start | bytes 8257536 | tf_op jit(solution)/shard_map/reduce_scatter | solution.py:147
  27.7 25.8 %collective-permute-start = (bf16[128,896]{1,0:T(8,128)(2,1)S(1)}, bf16[128,896]{1,0:T(8,128)(2,1)S(1)}, u32[]{:S(2)}, u32[]{:S(2)}) collective-permute-start(bf16[128,896]{1,0:T(8,128)(2,1)S(1)} %bitcast.67), channel_id=1, source_target_pairs={{0,160},{32,128},{64,224},{96,192},{128,32},{160,0},{192,96},{224,... | collective-permute-start | bytes 688136 | tf_op jit(solution)/shard_map/ppermute | solution.py:122
  34.4 21.2 %collective-permute-start.1 = (bf16[128,896]{1,0:T(8,128)(2,1)S(1)}, bf16[128,896]{1,0:T(8,128)(2,1)S(1)}, u32[]{:S(2)}, u32[]{:S(2)}) collective-permute-start(bf16[128,896]{1,0:T(8,128)(2,1)S(1)} %bitcast.66), channel_id=1, source_target_pairs={{0,64},{32,224},{64,128},{96,32},{128,192},{160,96},{192,0},{224,1... | collective-permute-start | bytes 688136 | tf_op jit(solution)/shard_map/ppermute | solution.py:122
  35.9 28.3 %collective-permute-start.2 = (bf16[128,896]{1,0:T(8,128)(2,1)S(1)}, bf16[128,896]{1,0:T(8,128)(2,1)S(1)}, u32[]{:S(2)}, u32[]{:S(2)}) collective-permute-start(bf16[128,896]{1,0:T(8,128)(2,1)S(1)} %bitcast.65), channel_id=1, source_target_pairs={{0,224},{32,64},{64,32},{96,128},{128,96},{160,192},{192,160},{224... | collective-permute-start | bytes 688136 | tf_op jit(solution)/shard_map/ppermute | solution.py:122
  36.1 52.6 %collective-permute-start.3 = (bf16[128,896]{1,0:T(8,128)(2,1)S(1)}, bf16[128,896]{1,0:T(8,128)(2,1)S(1)}, u32[]{:S(2)}, u32[]{:S(2)}) collective-permute-start(bf16[128,896]{1,0:T(8,128)(2,1)S(1)} %bitcast.64), channel_id=1, source_target_pairs={{0,32},{32,0},{64,96},{96,64},{128,160},{160,128},{192,224},{224,1... | collective-permute-start | bytes 688136 | tf_op jit(solution)/shard_map/ppermute | solution.py:122
  53.6 35.2 %collective-permute-start.4 = (bf16[128,896]{1,0:T(8,128)(2,1)S(1)}, bf16[128,896]{1,0:T(8,128)(2,1)S(1)}, u32[]{:S(2)}, u32[]{:S(2)}) collective-permute-start(bf16[128,896]{1,0:T(8,128)(2,1)S(1)} %collective-permute-done), channel_id=1, source_target_pairs={{0,32},{32,0},{64,96},{96,64},{128,160},{160,128},{192,224},{224,1... | collective-permute-start | bytes 688136 | tf_op jit(solution)/shard_map/ppermute | solution.py:122
  55.6 33.2 %collective-permute-start.5 = (bf16[128,896]{1,0:T(8,128)(2,1)S(1)}, bf16[128,896]{1,0:T(8,128)(2,1)S(1)}, u32[]{:S(2)}, u32[]{:S(2)}) collective-permute-start(bf16[128,896]{1,0:T(8,128)(2,1)S(1)} %collective-permute-done.1), channel_id=1, source_target_pairs={{0,32},{32,0},{64,96},{96,64},{128,160},{160,128},{192,224},{224,1... | collective-permute-start | bytes 688136 | tf_op jit(solution)/shard_map/ppermute | solution.py:122
  64.2 25.7 %collective-permute-start.6 = (bf16[128,896]{1,0:T(8,128)(2,1)S(1)}, bf16[128,896]{1,0:T(8,128)(2,1)S(1)}, u32[]{:S(2)}, u32[]{:S(2)}) collective-permute-start(bf16[128,896]{1,0:T(8,128)(2,1)S(1)} %collective-permute-done.2), channel_id=1, source_target_pairs={{0,32},{32,0},{64,96},{96,64},{128,160},{160,128},{192,224},{224,1... | collective-permute-start | bytes 688136 | tf_op jit(solution)/shard_map/ppermute | solution.py:122
  89.9 0.7 copy-start.2
  111.0 41.5 %all-to-all-start.1 = ((bf16[32,40,896]{2,1,0:T(8,128)(2,1)}), bf16[32,40,896]{2,1,0:T(8,128)(2,1)}, u32[]{:S(2)}, u32[]{:S(2)}) async-start(bf16[32,40,896]{2,1,0:T(8,128)(2,1)} %bitcast.21), calls=%async_computation.1 | async-start | bytes 4587520 | tf_op jit(solution)/shard_map/all_to_all | solution.py:153
Sparse Core Ops, SparseCore 0:
  10.3 86.1 all-gather.3
  99.7 85.4 reduce-scatter.1

commit v3 on v2

--- a/solution.py
+++ b/solution.py
@@ -10,7 +10,7 @@
 PLANE = ("x", "y", "c")
 ALL = Z + PLANE
 BF = jnp.bfloat16
-ROOM = 24
+TILE = 8
 
 
 def contract(left, right, dims):
@@ -29,23 +29,39 @@
 
 def fill_kernel(half, s_ref, t_ref, act_ref, grad_ref, out_ref):
     chips = out_ref.shape[0]
-    rows = chips * ROOM
+    rows = chips * TILE
     pairs = s_ref.shape[1]
     tokens = t_ref.shape[1]
-    pick = (lax.broadcasted_iota(jnp.int32, (rows, pairs), 0) == s_ref[...]).astype(BF)
-    spot = lax.broadcasted_iota(jnp.int32, (rows, tokens), 0)
-    pick_tok = ((spot == t_ref[0:1, :]) | (spot == t_ref[1:2, :])).astype(BF)
-    acts = contract(pick_tok, act_ref[...], ((1,), (0,))).astype(BF)
-    grads = contract(pick, grad_ref[...], ((1,), (0,))).astype(BF)
-    for p in range(chips):
-        out_ref[p, 0, :, :half] = acts[p * ROOM : (p + 1) * ROOM]
-        out_ref[p, 0, :, half:] = grads[p * ROOM : (p + 1) * ROOM]
+    width = half + grad_ref.shape[1]
+    quarter = half // 2
+    lower = lax.broadcasted_iota(jnp.int32, (rows, 1), 0) % TILE < TILE // 2
+    for tile in range(3):
+
+        def spots(count):
+            row = lax.broadcasted_iota(jnp.int32, (rows, count), 0)
+            if tile == 2:
+                row = row - row % TILE + row % (TILE // 2)
+            return row + tile * rows
+
+        pick = (spots(pairs) == s_ref[...]).astype(BF)
+        spot = spots(tokens)
+        pick_tok = ((spot == t_ref[0:1, :]) | (spot == t_ref[1:2, :])).astype(BF)
+        acts = contract(pick_tok, act_ref[...], ((1,), (0,))).astype(BF)
+        grads = contract(pick, grad_ref[...], ((1,), (0,))).astype(BF)
+        if tile == 2:
+            acts = jnp.where(lower, acts[:, :quarter], acts[:, quarter:])
+        start = tile * width
+        middle = start + acts.shape[1]
+        for p in range(chips):
+            out_ref[p, 0, :, start:middle] = acts[p * TILE : (p + 1) * TILE]
+            out_ref[p, 0, :, middle : middle + grads.shape[1]] = grads[p * TILE : (p + 1) * TILE]
 
 
 def fill(slots, act, grad, chips):
     tokens, features = act.shape
     pairs, hidden = grad.shape
     half = features // 2
+    width = 2 * (half + hidden) + half // 2 + hidden
     return pl.pallas_call(
         functools.partial(fill_kernel, half),
         grid=(2,),
@@ -55,38 +71,38 @@
             pl.BlockSpec((tokens, half), lambda c: (0, c)),
             pl.BlockSpec((pairs, hidden), lambda c: (0, 0)),
         ],
-        out_specs=pl.BlockSpec((chips, 1, ROOM, half + hidden), lambda c: (0, c, 0, 0)),
-        out_shape=jax.ShapeDtypeStruct((chips, 2, ROOM, half + hidden), BF),
+        out_specs=pl.BlockSpec((chips, 1, TILE, width), lambda c: (0, c, 0, 0)),
+        out_shape=jax.ShapeDtypeStruct((chips, 2, TILE, width), BF),
         cost_estimate=pl.CostEstimate(flops=2_000_000_000, bytes_accessed=6_000_000, transcendentals=0),
         name="fill_b",
     )(slots.reshape(1, pairs), slots.reshape(tokens, 2).T, act, grad)
 
 
-def products_kernel(half, block, in_ref, out_ref):
-    count = in_ref.shape[0] * 8
-    hidden = in_ref.shape[2] - half
+def products_kernel(half, hidden, in_ref, out_ref):
+    count = in_ref.shape[0] * TILE
+    quarter = half // 2
+    width = half + hidden
 
-    def rows(tile, start, size):
-        return in_ref[:, pl.ds(tile * 8, 8), start : start + size].reshape(count, size)
+    def rows(start, size):
+        return in_ref[:, :, start : start + size].reshape(count, size)
 
-    shared = (lax.broadcasted_iota(jnp.int32, (count, 1), 0) % 8) // 4
+    row = lax.broadcasted_iota(jnp.int32, (count, 1), 0) % TILE
     for pair in range(2):
         for k in range(2):
 
             @pl.when((pl.program_id(0) == pair) & (pl.program_id(1) == k))
             def _():
-                start = pair * 2 * block
-                last = jnp.where(shared == k, rows(2, half, hidden), jnp.zeros((), BF))
-                total = contract(rows(k, start, 2 * block), rows(k, half, hidden), ((0,), (0,)))
-                total = total + contract(rows(2, start, 2 * block), last, ((0,), (0,)))
+                owner = row // 2 == pair * 2 + k
+                last = jnp.where(owner, rows(2 * width + quarter, hidden), jnp.zeros((), BF))
+                total = contract(rows(k * width + pair * quarter, quarter), rows(k * width + half, hidden), ((0,), (0,)))
+                total = total + contract(rows(2 * width, quarter), last, ((0,), (0,)))
                 out_ref[...] = total.astype(BF).reshape(out_ref.shape)
 
 
-def products(recv, half):
-    hidden = recv.shape[2] - half
+def products(recv, half, hidden):
     block = half // 4
     return pl.pallas_call(
-        functools.partial(products_kernel, half, block),
+        functools.partial(products_kernel, half, hidden),
         grid=(2, 2),
         in_specs=[pl.BlockSpec(recv.shape, lambda r, k: (0, 0, 0))],
         out_specs=pl.BlockSpec((2, 1, block, hidden), lambda r, k: (r, k, 0, 0)),
@@ -130,9 +146,10 @@
     ids_b = route_b.reshape(-1)
     pos_b = positions(ids_b)
     lower = ids_b // chips
-    slots_b = (ids_b % chips) * ROOM + jnp.where(pos_b < 8, lower * 8 + pos_b, 16 + lower * 4 + pos_b - 8)
+    row_b = jnp.where(pos_b < TILE, lower * (chips * TILE) + pos_b, 2 * chips * TILE + lower * 2 + pos_b - TILE)
+    slots_b = (ids_b % chips) * TILE + row_b
     send_b = fill(slots_b, act_b, grad_b.reshape(pairs, hidden), chips)
-    recv_b = lax.all_to_all(send_b.reshape(spots, ROOM, half + hidden), PLANE, 0, 0, tiled=True)
+    recv_b = lax.all_to_all(send_b.reshape(spots, TILE, send_b.shape[-1]), PLANE, 0, 0, tiled=True)
 
     ids_a = route_a.reshape(-1)
     slots_a = (ids_a % spots) * (planes * most) + my_z * most + positions(ids_a)
@@ -142,7 +159,7 @@
     slots = jnp.where(slots // 4096 == my_zl, slots % 4096, -1)
 
     far = [along(b, 1) for b in near]
-    parts = products(recv_b, half).reshape(features, hidden)
+    parts = products(recv_b, half, hidden).reshape(features, hidden)
     parts, far = lax.optimization_barrier((parts, far))
     wgrad_b = lax.psum_scatter(parts, Z, scatter_dimension=0, tiled=True)[None]
 

time: 203 us -> 200 us (0.985)
  blocking collectives: 52.1 us -> 48.7 us
    ppermute x7, waiting for transfers between devices: 26.8 us -> 32.5 us  [along(): lax.ppermute(block_in, Z, [(z, (z + step * (1 - 2 * (z % 2))) % planes) f...]
    all_to_all x1, waiting for transfers between devices: 14 us -> 8.54 us  [shards(): lax.all_to_all(send_b.reshape(spots, TILE, send_b.shape[-1]), PLANE, 0, 0...]
    all_gather x1, blocking collectives: 14.4 us -> 11 us  [shards(): slots = lax.all_gather(slots_a, Z, axis=0)]
where the time goes in v3:
time: 200 us; the launch traced here: 199 us
  waiting for transfers between devices  64.2 us (32%)
  blocking collectives  48.7 us (24%)
  starting transfers between devices  32.8 us (16%)
  matrix products  17 us (8%)
  between operations  14.3 us (7%)
  Pallas kernels  12.1 us (6%)
  local copies, waits for them, and re-layouts  8.88 us (4%)
    all_to_all x1, blocking collectives, shards(): recv_g = lax.all_to_all(rows_g, PLANE, 0, 0, tiled=True)  37.7 us
    ppermute x7, waiting for transfers between devices, along(): lax.ppermute(block_in, Z, [(z, (z + step * (1 - 2 * (z % 2))) % planes) f...  32.5 us
    all_to_all x1, waiting for transfers between devices, shards(): recv_a = lax.all_to_all(rows_a, PLANE, 0, 0, tiled=True)  23.1 us
    dot_general x3, matrix products, contract(): lax.dot_general(left, right, (dims, ((), ())), preferred_element_type=jnp...  17 us
    ppermute x7, starting transfers between devices, along(): lax.ppermute(block_in, Z, [(z, (z + step * (1 - 2 * (z % 2))) % planes) f...  12.5 us
    all_to_all x1, starting transfers between devices, shards(): recv_a = lax.all_to_all(rows_a, PLANE, 0, 0, tiled=True)  11.5 us
    all_gather x1, blocking collectives, shards(): slots = lax.all_gather(slots_a, Z, axis=0)  11 us
    all_to_all x1, starting transfers between devices, shards(): lax.all_to_all(send_b.reshape(spots, TILE, send_b.shape[-1]), PLANE, 0, 0...  8.76 us
  transfers between devices with their start and end apart: 11, of which 5 were waited for; matrix products, arithmetic and copies ran while one was open for 12% of the time, Pallas kernels for 6%

profile of v3, /device:TPU:1, one launch (start us, length us, event | category | flops | bytes accessed | tf_op | source)
XLA Modules:
  0.0 199.5 jit_solution(7718483381922011026)
XLA Ops:
  7.2 0.0 all-gather.4.cloned.1.call-start
  7.2 2.0 %reshape.324 = bf16[256,1024]{1,0:T(8,128)(2,1)} reshape(bf16[128,2,1024]{2,1,0:T(2,128)(2,1)} %param.7) | data formatting | bytes 1048576 | tf_op jit(solution)/shard_map/reshape | solution.py:131
  9.3 0.8 copy.38
  10.1 0.1 eq.88
  10.2 0.1 reshape.319
  10.3 0.1 convert_reduce_fusion
  10.5 0.1 reduce_sum.25
  10.6 0.1 copy.40
  10.7 2.1 %reshape.320.grad_ref = bf16[256,1024]{1,0:T(8,128)(2,1)} reshape(bf16[128,2,1024]{2,1,0:T(2,128)(2,1)} %param.10) | data formatting | bytes 1048576 | tf_op jit(solution)/shard_map/reshape | solution.py:151
  12.7 0.6 fusion.23.t_ref
  13.3 0.6 fusion.22.s_ref
  13.9 3.9 %fill_b.1 = bf16[16,2,8,7552]{3,2,1,0:T(8,128)(2,1)} custom-call(s32[1,256]{1,0:T(1,128)} %fusion.22.s_ref, s32[2,128]{1,0:T(2,128)} %fusion.23.t_ref, bf16[128,3584]{1,0:T(8,128)(2,1)} %act_ref.1, bf16[256,1024]{1,0:T(8,128)(2,1)} %reshape.320.grad_ref), custom_call_target="tpu_custom_call" | custom-call | flops 2000000000 | bytes 6000000 | tf_op jit(solution)/shard_map/fill_b/pallas_call | solution.py:65
  17.9 8.8 %all-to-all-start = ((bf16[32,8,7552]{2,1,0:T(8,128)(2,1)}), bf16[32,8,7552]{2,1,0:T(8,128)(2,1)}, u32[]{:S(2)}, u32[]{:S(2)}) async-start(bf16[32,8,7552]{2,1,0:T(8,128)(2,1)} %bitcast.61), calls=%async_computation | async-start | bytes 7733248 | tf_op jit(solution)/shard_map/all_to_all | solution.py:152
  26.6 0.0 reduce-scatter.2.cloned.1.call-start
  26.7 0.6 copy.43
  27.4 0.1 constant_dynamic-slice_fusion
  27.4 0.2 copy.45
  27.6 6.6 %collective-permute-start = (bf16[128,896]{1,0:T(8,128)(2,1)S(1)}, bf16[128,896]{1,0:T(8,128)(2,1)S(1)}, u32[]{:S(2)}, u32[]{:S(2)}) collective-permute-start(bf16[128,896]{1,0:T(8,128)(2,1)S(1)} %bitcast.67), channel_id=1, source_target_pairs={{0,160},{32,128},{64,224},{96,192},{128,32},{160,0},{192,96},{224,... | collective-permute-start | bytes 688136 | tf_op jit(solution)/shard_map/ppermute | solution.py:138
  34.2 0.2 copy.46
  34.3 1.3 collective-permute-start.1
  35.6 0.2 copy.47
  35.7 0.1 collective-permute-start.2
  35.9 0.2 copy.44
  36.0 0.4 collective-permute-start.3
  36.4 17.0 %collective-permute-done = bf16[128,896]{1,0:T(8,128)(2,1)S(1)} collective-permute-done((bf16[128,896]{1,0:T(8,128)(2,1)S(1)}, bf16[128,896]{1,0:T(8,128)(2,1)S(1)}, u32[]{:S(2)}, u32[]{:S(2)}) %collective-permute-start) | collective-permute-done | bytes 229408 | tf_op jit(solution)/shard_map/ppermute | solution.py:138
  53.4 2.0 %collective-permute-start.4 = (bf16[128,896]{1,0:T(8,128)(2,1)S(1)}, bf16[128,896]{1,0:T(8,128)(2,1)S(1)}, u32[]{:S(2)}, u32[]{:S(2)}) collective-permute-start(bf16[128,896]{1,0:T(8,128)(2,1)S(1)} %collective-permute-done), channel_id=1, source_target_pairs={{0,32},{32,0},{64,96},{96,64},{128,160},{160,128},{192,224},{224,1... | collective-permute-start | bytes 688136 | tf_op jit(solution)/shard_map/ppermute | solution.py:138
  55.4 0.0 collective-permute-start.5
  55.5 8.6 %collective-permute-done.2 = bf16[128,896]{1,0:T(8,128)(2,1)S(1)} collective-permute-done((bf16[128,896]{1,0:T(8,128)(2,1)S(1)}, bf16[128,896]{1,0:T(8,128)(2,1)S(1)}, u32[]{:S(2)}, u32[]{:S(2)}) %collective-permute-start.2) | collective-permute-done | bytes 229408 | tf_op jit(solution)/shard_map/ppermute | solution.py:138
  64.1 2.2 %collective-permute-start.6 = (bf16[128,896]{1,0:T(8,128)(2,1)S(1)}, bf16[128,896]{1,0:T(8,128)(2,1)S(1)}, u32[]{:S(2)}, u32[]{:S(2)}) collective-permute-start(bf16[128,896]{1,0:T(8,128)(2,1)S(1)} %collective-permute-done.2), channel_id=1, source_target_pairs={{0,32},{32,0},{64,96},{96,64},{128,160},{160,128},{192,224},{224,1... | collective-permute-start | bytes 688136 | tf_op jit(solution)/shard_map/ppermute | solution.py:138
  66.3 8.5 %all-to-all-done.in_ref = bf16[32,8,7552]{2,1,0:T(8,128)(2,1)} async-done(((bf16[32,8,7552]{2,1,0:T(8,128)(2,1)}), bf16[32,8,7552]{2,1,0:T(8,128)(2,1)}, u32[]{:S(2)}, u32[]{:S(2)}) %all-to-all-start) | async-done | bytes 3866656 | tf_op jit(solution)/shard_map/all_to_all | solution.py:152
  74.8 8.2 %products_b.1 = bf16[4,2,448,1024]{3,2,1,0:T(8,128)(2,1)} custom-call(bf16[32,8,7552]{2,1,0:T(8,128)(2,1)} %all-to-all-done.in_ref), custom_call_target="tpu_custom_call" | custom-call | flops 4000000000 | bytes 12000000 | tf_op jit(solution)/shard_map/products_b/pallas_call | solution.py:104
  83.0 6.8 %collective-permute-done.6 = bf16[128,896]{1,0:T(8,128)(2,1)S(1)} collective-permute-done((bf16[128,896]{1,0:T(8,128)(2,1)S(1)}, bf16[128,896]{1,0:T(8,128)(2,1)S(1)}, u32[]{:S(2)}, u32[]{:S(2)}) %collective-permute-start.6) | collective-permute-done | bytes 229408 | tf_op jit(solution)/shard_map/ppermute | solution.py:138
  89.9 0.6 copy-done.2
  90.5 0.1 copy.37
  90.6 0.1 reshape.318
  90.7 0.1 convert_reduce_fusion.1
  90.9 0.1 stack.35
  91.0 11.0 %all-gather.1 = s32[8,1,256]{2,1,0:T(1,128)S(1)} all-gather(s32[1,1,256]{2,1,0:T(1,128)S(1)} %bitcast.70), channel_id=2, replica_groups=mesh['zh'=4,'zl'=2,'x'=4,'y'=4,'c'=2] {'zh','zl'}, dimensions={0}, use_global_device_ids=true | all-gather | bytes 9216 | tf_op jit(solution)/shard_map/all_gather | solution.py:158
  102.1 0.6 gather_fusion
  102.6 0.2 slice.6
  102.8 0.2 slice.7
  103.3 4.1 %convolution_convert_fusion = bf16[1280,896]{1,0:T(8,128)(2,1)} fusion(bf16[1024,896]{1,0:T(8,128)(2,1)S(1)} %constant_dynamic-update-slice_fusion, s32[1024]{0:T(1024)S(1)} %bitcast.72, s32[1024]{0:T(1024)S(1)} %bitcast.71), kind=kOutput, calls=%fused_computation.10 | convolution fusion | flops 2360442880 | bytes 4136960 | tf_op jit(solution)/shard_map/dot_general | solution.py:17
  107.5 11.5 %all-to-all-start.1 = ((bf16[32,40,896]{2,1,0:T(8,128)(2,1)}), bf16[32,40,896]{2,1,0:T(8,128)(2,1)}, u32[]{:S(2)}, u32[]{:S(2)}) async-start(bf16[32,40,896]{2,1,0:T(8,128)(2,1)} %bitcast.21), calls=%async_computation.1 | async-start | bytes 4587520 | tf_op jit(solution)/shard_map/all_to_all | solution.py:170
  119.0 0.0 all-gather.4.cloned.1.call-done
  119.0 7.4 %fusion.4 = bf16[1280,1024]{1,0:T(8,128)(2,1)S(1)} fusion(bf16[2048,1024]{1,0:T(8,128)(2,1)} %all-gather.4.cloned.1.call-done, s32[2048]{0:T(1024)S(1)} %bitcast.69), kind=kOutput, calls=%fused_computation.8 | convolution fusion | flops 5372641280 | bytes 6823936 | tf_op jit(solution)/shard_map/dot_general | solution.py:17
  126.5 23.1 %all-to-all-done.1 = bf16[32,40,896]{2,1,0:T(8,128)(2,1)} async-done(((bf16[32,40,896]{2,1,0:T(8,128)(2,1)}), bf16[32,40,896]{2,1,0:T(8,128)(2,1)}, u32[]{:S(2)}, u32[]{:S(2)}) %all-to-all-start.1) | async-done | bytes 2293792 | tf_op jit(solution)/shard_map/all_to_all | solution.py:170
  149.5 37.7 %all_to_all.23 = bf16[32,40,1024]{2,1,0:T(8,128)(2,1)S(1)} all-to-all(bf16[32,40,1024]{2,1,0:T(8,128)(2,1)S(1)} %bitcast.63), channel_id=1, replica_groups=mesh['zh'=4,'zl'=2,'x'=4,'y'=4,'c'=2] {'x','y','c'}, dimensions={0} | all-to-all | bytes 5242880 | tf_op jit(solution)/shard_map/all_to_all | solution.py:172
  187.2 5.5 %fusion.10 = bf16[1,896,1024]{2,1,0:T(8,128)(2,1)} fusion(bf16[32,40,896]{2,1,0:T(8,128)(2,1)} %all-to-all-done.1, bf16[32,40,1024]{2,1,0:T(8,128)(2,1)S(1)} %all_to_all.23), kind=kOutput, calls=%fused_computation.14 | convolution fusion | flops 2349727744 | bytes 6750208 | tf_op jit(solution)/shard_map/dot_general | solution.py:17
  (26 shorter events, 0.3 us)
Async XLA Ops:
  7.2 5.6 %copy-start.1 = (s32[128,2]{0,1:T(2,128)S(1)}, s32[128,2]{0,1:T(2,128)}, u32[]{:S(2)}) copy-start(s32[128,2]{0,1:T(2,128)} %param.11) | copy-start | bytes 3076
  7.2 111.9 %all-gather.4.cloned.1.call-start = ((), (), s32[]{:S(2)}) async-start(), calls=%async_computation.4 | async-start | bytes 4718592 | tf_op jit(solution)/shard_map/all_gather | solution.py:131
  17.9 8.8 %copy-start = (bf16[128,3584]{1,0:T(8,128)(2,1)S(1)}, bf16[128,3584]{1,0:T(8,128)(2,1)}, u32[]{:S(2)}) copy-start(bf16[128,3584]{1,0:T(8,128)(2,1)} %param.6) | copy-start | bytes 2752516
  17.9 56.9 %all-to-all-start = ((bf16[32,8,7552]{2,1,0:T(8,128)(2,1)}), bf16[32,8,7552]{2,1,0:T(8,128)(2,1)}, u32[]{:S(2)}, u32[]{:S(2)}) async-start(bf16[32,8,7552]{2,1,0:T(8,128)(2,1)} %bitcast.61), calls=%async_computation | async-start | bytes 7733248 | tf_op jit(solution)/shard_map/all_to_all | solution.py:152
  26.6 166.0 %reduce-scatter.2.cloned.1.call-start = ((), (), s32[]{:S(2)}) async-start(), calls=%async_computation.5 | async-start | bytes 8257536 | tf_op jit(solution)/shard_map/reduce_scatter | solution.py:164
  27.6 25.8 %collective-permute-start = (bf16[128,896]{1,0:T(8,128)(2,1)S(1)}, bf16[128,896]{1,0:T(8,128)(2,1)S(1)}, u32[]{:S(2)}, u32[]{:S(2)}) collective-permute-start(bf16[128,896]{1,0:T(8,128)(2,1)S(1)} %bitcast.67), channel_id=1, source_target_pairs={{0,160},{32,128},{64,224},{96,192},{128,32},{160,0},{192,96},{224,... | collective-permute-start | bytes 688136 | tf_op jit(solution)/shard_map/ppermute | solution.py:138
  34.3 21.1 %collective-permute-start.1 = (bf16[128,896]{1,0:T(8,128)(2,1)S(1)}, bf16[128,896]{1,0:T(8,128)(2,1)S(1)}, u32[]{:S(2)}, u32[]{:S(2)}) collective-permute-start(bf16[128,896]{1,0:T(8,128)(2,1)S(1)} %bitcast.66), channel_id=1, source_target_pairs={{0,64},{32,224},{64,128},{96,32},{128,192},{160,96},{192,0},{224,1... | collective-permute-start | bytes 688136 | tf_op jit(solution)/shard_map/ppermute | solution.py:138
  35.7 28.3 %collective-permute-start.2 = (bf16[128,896]{1,0:T(8,128)(2,1)S(1)}, bf16[128,896]{1,0:T(8,128)(2,1)S(1)}, u32[]{:S(2)}, u32[]{:S(2)}) collective-permute-start(bf16[128,896]{1,0:T(8,128)(2,1)S(1)} %bitcast.65), channel_id=1, source_target_pairs={{0,224},{32,64},{64,32},{96,128},{128,96},{160,192},{192,160},{224... | collective-permute-start | bytes 688136 | tf_op jit(solution)/shard_map/ppermute | solution.py:138
  36.0 46.9 %collective-permute-start.3 = (bf16[128,896]{1,0:T(8,128)(2,1)S(1)}, bf16[128,896]{1,0:T(8,128)(2,1)S(1)}, u32[]{:S(2)}, u32[]{:S(2)}) collective-permute-start(bf16[128,896]{1,0:T(8,128)(2,1)S(1)} %bitcast.64), channel_id=1, source_target_pairs={{0,32},{32,0},{64,96},{96,64},{128,160},{160,128},{192,224},{224,1... | collective-permute-start | bytes 688136 | tf_op jit(solution)/shard_map/ppermute | solution.py:138
  53.4 29.5 %collective-permute-start.4 = (bf16[128,896]{1,0:T(8,128)(2,1)S(1)}, bf16[128,896]{1,0:T(8,128)(2,1)S(1)}, u32[]{:S(2)}, u32[]{:S(2)}) collective-permute-start(bf16[128,896]{1,0:T(8,128)(2,1)S(1)} %collective-permute-done), channel_id=1, source_target_pairs={{0,32},{32,0},{64,96},{96,64},{128,160},{160,128},{192,224},{224,1... | collective-permute-start | bytes 688136 | tf_op jit(solution)/shard_map/ppermute | solution.py:138
  55.4 27.5 %collective-permute-start.5 = (bf16[128,896]{1,0:T(8,128)(2,1)S(1)}, bf16[128,896]{1,0:T(8,128)(2,1)S(1)}, u32[]{:S(2)}, u32[]{:S(2)}) collective-permute-start(bf16[128,896]{1,0:T(8,128)(2,1)S(1)} %collective-permute-done.1), channel_id=1, source_target_pairs={{0,32},{32,0},{64,96},{96,64},{128,160},{160,128},{192,224},{224,1... | collective-permute-start | bytes 688136 | tf_op jit(solution)/shard_map/ppermute | solution.py:138
  64.1 25.7 %collective-permute-start.6 = (bf16[128,896]{1,0:T(8,128)(2,1)S(1)}, bf16[128,896]{1,0:T(8,128)(2,1)S(1)}, u32[]{:S(2)}, u32[]{:S(2)}) collective-permute-start(bf16[128,896]{1,0:T(8,128)(2,1)S(1)} %collective-permute-done.2), channel_id=1, source_target_pairs={{0,32},{32,0},{64,96},{96,64},{128,160},{160,128},{192,224},{224,1... | collective-permute-start | bytes 688136 | tf_op jit(solution)/shard_map/ppermute | solution.py:138
  89.8 0.7 copy-start.2
  107.5 42.0 %all-to-all-start.1 = ((bf16[32,40,896]{2,1,0:T(8,128)(2,1)}), bf16[32,40,896]{2,1,0:T(8,128)(2,1)}, u32[]{:S(2)}, u32[]{:S(2)}) async-start(bf16[32,40,896]{2,1,0:T(8,128)(2,1)} %bitcast.21), calls=%async_computation.1 | async-start | bytes 4587520 | tf_op jit(solution)/shard_map/all_to_all | solution.py:170
Sparse Core Ops, SparseCore 0:
  10.3 86.0 all-gather.3
  99.6 85.5 reduce-scatter.1

commit v4 on v3

--- a/solution.py
+++ b/solution.py
@@ -112,6 +112,11 @@
     )(recv)
 
 
+def ordered(block_in, target):
+    planes = lax.axis_size(Z)
+    return lax.ppermute(block_in, Z, [(z, target(z) % planes) for z in range(planes)])
+
+
 def shards(act_a, grad_a, route_a, act_b, grad_b, route_b):
     tokens, top = route_a.shape
     pairs = tokens * top
@@ -128,20 +133,35 @@
     my_z = 2 * my_zh + my_zl
     sign = 1 - 2 * my_zl
 
-    all_grads = lax.all_gather(grad_a.reshape(pairs, hidden), Z, axis=0, tiled=True)
+    ids_a = route_a.reshape(-1)
+    info = jnp.stack([ids_a, positions(ids_a)]).astype(BF)
+    info = jnp.pad(info, ((0, 6), (0, hidden - pairs)))
+    grads = jnp.concatenate([grad_a.reshape(pairs, hidden), info], axis=0)
+    up, down = [grads], [grads]
+    for _ in range(1, 4):
+        up.append(ordered(up[-1], lambda z: z + 1))
+        down.append(ordered(down[-1], lambda z: z - 1))
+    cut = pairs // 2
+    across = jnp.concatenate(
+        [ordered(up[3][:cut], lambda z: z + 1), ordered(down[3][cut:], lambda z: z - 1)],
+        axis=0,
+    )
+    ring = (0, -1, -2, -3, 4, 3, 2, 1)
+    all_grads = jnp.concatenate(up + [across] + down[:0:-1], axis=0)
+
     quarters = jnp.moveaxis(act_a.reshape(tokens, 4, quarter), 1, 0)
 
     def mine(which):
         return lax.dynamic_index_in_dim(quarters, lax.rem(which + 8, 4), 0, keepdims=False)
 
     def along(block_in, step):
-        return lax.ppermute(block_in, Z, [(z, (z + step * (1 - 2 * (z % 2))) % planes) for z in range(planes)])
+        return ordered(block_in, lambda z: z + step * (1 - 2 * (z % 2)))
 
     near = [mine(my_zh)]
     for to, step in ((my_zh + 2, -3), (my_zh + sign, 2), (my_zh - sign, -1)):
         near.append(along(mine(to), step))
     offsets = (0, -3, -2, -1, 1, 4, 3, 2)
-    origin = lax.rem(jnp.stack([my_z + o * sign for o in offsets]) + planes, planes)
+    far = [along(b, 1) for b in near]
 
     ids_b = route_b.reshape(-1)
     pos_b = positions(ids_b)
@@ -151,24 +171,22 @@
     send_b = fill(slots_b, act_b, grad_b.reshape(pairs, hidden), chips)
     recv_b = lax.all_to_all(send_b.reshape(spots, TILE, send_b.shape[-1]), PLANE, 0, 0, tiled=True)
 
-    ids_a = route_a.reshape(-1)
-    slots_a = (ids_a % spots) * (planes * most) + my_z * most + positions(ids_a)
-    slots_a = slots_a + (ids_a // spots) * 4096
-    slots_a, _ = lax.optimization_barrier((slots_a, send_b))
-    slots = lax.all_gather(slots_a, Z, axis=0)
-    slots = jnp.where(slots // 4096 == my_zl, slots % 4096, -1)
-
-    far = [along(b, 1) for b in near]
     parts = products(recv_b, half, hidden).reshape(features, hidden)
-    parts, far = lax.optimization_barrier((parts, far))
     wgrad_b = lax.psum_scatter(parts, Z, scatter_dimension=0, tiled=True)[None]
 
     total = spots * planes * most
-    slots_t = slots[origin]
+    told = all_grads.reshape(planes, pairs + 8, hidden)[:, pairs : pairs + 2, :pairs].astype(jnp.int32)
+    origin = lax.rem(jnp.stack([my_z + o for o in ring]) + planes, planes)
+    slots = (told[:, 0] % spots) * (planes * most) + origin[:, None] * most + told[:, 1]
+    slots = jnp.where(told[:, 0] // spots == my_zl, slots, -1)
+    even = slots[jnp.array([ring.index(o) for o in offsets])]
+    odd = slots[jnp.array([ring.index(-o if -o in ring else 4) for o in offsets])]
+    slots_t = jnp.where(my_zl == 0, even, odd)
     pick_tok = one_hot(slots_t[:, 0::2].reshape(-1), total) + one_hot(slots_t[:, 1::2].reshape(-1), total)
     rows_a = contract(pick_tok, jnp.concatenate(near + far, axis=0), ((1,), (0,))).astype(BF)
+    slots_g = jnp.pad(slots, ((0, 0), (0, 8)), constant_values=-1)
+    rows_g = contract(one_hot(slots_g.reshape(-1), total), all_grads, ((1,), (0,))).astype(BF)
     recv_a = lax.all_to_all(rows_a, PLANE, 0, 0, tiled=True)
-    rows_g = contract(one_hot(slots.reshape(-1), total), all_grads, ((1,), (0,))).astype(BF)
     recv_g = lax.all_to_all(rows_g, PLANE, 0, 0, tiled=True)
     wgrad_a = contract(recv_a, recv_g, ((0,), (0,))).astype(BF)[None]
     return wgrad_a, wgrad_b

time: 200 us -> 323 us (1.61)
  the two profiles are of different devices: /device:TPU:1 before, /device:TPU:34 now
where the time goes in v4:
time: 323 us; the launch traced here: 318 us
  waiting for transfers between devices  105 us (33%)
  blocking collectives  91.1 us (28%)
  starting transfers between devices  48.5 us (15%)
  local copies, waits for them, and re-layouts  24.9 us (8%)
  matrix products  19.2 us (6%)
  between operations  14.2 us (4%)
  Pallas kernels  12.1 us (4%)
    ppermute x15, waiting for transfers between devices, ordered(): lax.ppermute(block_in, Z, [(z, target(z) % planes) for z in range(planes)])  84.8 us
    all_to_all x1, blocking collectives, shards(): lax.all_to_all(send_b.reshape(spots, TILE, send_b.shape[-1]), PLANE, 0, 0...  52.9 us
    ppermute x15, starting transfers between devices, ordered(): lax.ppermute(block_in, Z, [(z, target(z) % planes) for z in range(planes)])  41.7 us
    all_to_all x1, blocking collectives, shards(): recv_g = lax.all_to_all(rows_g, PLANE, 0, 0, tiled=True)  38.2 us
    all_to_all x1, waiting for transfers between devices, shards(): recv_a = lax.all_to_all(rows_a, PLANE, 0, 0, tiled=True)  20 us
    dot_general x3, matrix products, contract(): lax.dot_general(left, right, (dims, ((), ())), preferred_element_type=jnp...  19.2 us
    unnamed x28, local copies, waits for them, and re-layouts  14.9 us
    pallas_call x1, Pallas kernels, products(): pl.pallas_call(functools.partial(products_kernel, half, hidden), grid=(2,...  8.14 us
  transfers between devices with their start and end apart: 17, of which 8 were waited for; matrix products, arithmetic and copies ran while one was open for 13% of the time, Pallas kernels for 0%

profile of v4, /device:TPU:34, one launch (start us, length us, event | category | flops | bytes accessed | tf_op | source)
XLA Modules:
  0.0 317.7 jit_solution(3252855316048691596)
XLA Ops:
  7.2 0.8 copy.40
  8.6 1.3 fusion.30.t_ref
  9.9 2.0 reshape.253.grad_ref
  12.5 4.0 %fill_b.1 = bf16[16,2,8,7552]{3,2,1,0:T(8,128)(2,1)} custom-call(s32[1,256]{1,0:T(1,128)} %fusion.29.s_ref, s32[2,128]{1,0:T(2,128)} %fusion.30.t_ref, bf16[128,3584]{1,0:T(8,128)(2,1)} %act_ref.1, bf16[256,1024]{1,0:T(8,128)(2,1)} %reshape.253.grad_ref), custom_call_target="tpu_custom_call" | custom-call | flops 2000000000 | bytes 6000000 | tf_op jit(solution)/shard_map/fill_b/pallas_call | solution.py:65
  16.5 52.9 %all_to_all.23.in_ref = bf16[32,8,7552]{2,1,0:T(8,128)(2,1)} all-to-all(bf16[32,8,7552]{2,1,0:T(8,128)(2,1)} %bitcast.44), channel_id=1, replica_groups=mesh['zh'=4,'zl'=2,'x'=4,'y'=4,'c'=2] {'x','y','c'}, dimensions={0} | all-to-all | bytes 7733248 | tf_op jit(solution)/shard_map/all_to_all | solution.py:172
  69.3 8.1 %products_b.1 = bf16[4,2,448,1024]{3,2,1,0:T(8,128)(2,1)} custom-call(bf16[32,8,7552]{2,1,0:T(8,128)(2,1)} %all_to_all.23.in_ref), custom_call_target="tpu_custom_call" | custom-call | flops 4000000000 | bytes 12000000 | tf_op jit(solution)/shard_map/products_b/pallas_call | solution.py:104
  79.3 0.8 constant_dynamic-update-slice_fusion.9
  80.8 2.0 collective-permute-start
  83.6 0.8 copy.37
  84.4 7.0 %collective-permute-start.8 = (bf16[128,896]{1,0:T(8,128)(2,1)}, bf16[128,896]{1,0:T(8,128)(2,1)}, u32[]{:S(2)}, u32[]{:S(2)}) collective-permute-start(bf16[128,896]{1,0:T(8,128)(2,1)} %bitcast.15), channel_id=1, source_target_pairs={{0,160},{32,128},{64,224},{96,192},{128,32},{160,0},{192,96},{224,... | collective-permute-start | bytes 688136 | tf_op jit(solution)/shard_map/ppermute | solution.py:117
  91.5 0.8 copy.38
  92.3 0.8 copy.39
  94.0 0.7 constant_dynamic-update-slice_fusion.17
  94.7 6.8 %collective-permute-done = bf16[264,1024]{1,0:T(8,128)(2,1)S(1)} collective-permute-done((bf16[264,1024]{1,0:T(8,128)(2,1)S(1)}, bf16[264,1024]{1,0:T(8,128)(2,1)S(1)}, u32[]{:S(2)}, u32[]{:S(2)}) %collective-permute-start) | collective-permute-done | bytes 540704 | tf_op jit(solution)/shard_map/ppermute | solution.py:117
  101.4 3.3 %collective-permute-start.1 = (bf16[264,1024]{1,0:T(8,128)(2,1)S(1)}, bf16[264,1024]{1,0:T(8,128)(2,1)S(1)}, u32[]{:S(2)}, u32[]{:S(2)}) collective-permute-start(bf16[264,1024]{1,0:T(8,128)(2,1)S(1)} %collective-permute-done), channel_id=1, source_target_pairs={{0,32},{32,64},{64,96},{96,128},{128,160},{160,192},{192,224},{224... | collective-permute-start | bytes 1622024 | tf_op jit(solution)/shard_map/ppermute | solution.py:117
  104.8 12.9 %collective-permute-start.5 = (bf16[264,1024]{1,0:T(8,128)(2,1)S(1)}, bf16[264,1024]{1,0:T(8,128)(2,1)S(1)}, u32[]{:S(2)}, u32[]{:S(2)}) collective-permute-start(bf16[264,1024]{1,0:T(8,128)(2,1)S(1)} %collective-permute-done.4), channel_id=1, source_target_pairs={{0,224},{32,0},{64,32},{96,64},{128,96},{160,128},{192,160},{224,1... | collective-permute-start | bytes 1622024 | tf_op jit(solution)/shard_map/ppermute | solution.py:117
  117.7 13.3 %collective-permute-done.8 = bf16[128,896]{1,0:T(8,128)(2,1)} collective-permute-done((bf16[128,896]{1,0:T(8,128)(2,1)}, bf16[128,896]{1,0:T(8,128)(2,1)}, u32[]{:S(2)}, u32[]{:S(2)}) %collective-permute-start.8) | collective-permute-done | bytes 229408 | tf_op jit(solution)/shard_map/ppermute | solution.py:117
  131.0 1.6 constant_dynamic-update-slice_fusion.16
  132.7 2.0 collective-permute-start.12
  135.4 3.2 %collective-permute-start.13 = (bf16[128,896]{1,0:T(8,128)(2,1)S(1)}, bf16[128,896]{1,0:T(8,128)(2,1)S(1)}, u32[]{:S(2)}, u32[]{:S(2)}) collective-permute-start(bf16[128,896]{1,0:T(8,128)(2,1)S(1)} %collective-permute-done.9), channel_id=1, source_target_pairs={{0,32},{32,0},{64,96},{96,64},{128,160},{160,128},{192,224},{224,1... | collective-permute-start | bytes 688136 | tf_op jit(solution)/shard_map/ppermute | solution.py:117
  138.6 15.1 %collective-permute-done.1 = bf16[264,1024]{1,0:T(8,128)(2,1)S(1)} collective-permute-done((bf16[264,1024]{1,0:T(8,128)(2,1)S(1)}, bf16[264,1024]{1,0:T(8,128)(2,1)S(1)}, u32[]{:S(2)}, u32[]{:S(2)}) %collective-permute-start.1) | collective-permute-done | bytes 540704 | tf_op jit(solution)/shard_map/ppermute | solution.py:117
  153.8 2.5 collective-permute-start.2
  157.0 2.1 collective-permute-start.14
  159.1 2.4 collective-permute-start.6
  161.6 0.7 constant_dynamic-update-slice_fusion.13
  162.3 0.7 constant_dynamic-update-slice_fusion.12
  163.0 8.6 %collective-permute-done.13 = bf16[128,896]{1,0:T(8,128)(2,1)S(1)} collective-permute-done((bf16[128,896]{1,0:T(8,128)(2,1)S(1)}, bf16[128,896]{1,0:T(8,128)(2,1)S(1)}, u32[]{:S(2)}, u32[]{:S(2)}) %collective-permute-start.13) | collective-permute-done | bytes 229408 | tf_op jit(solution)/shard_map/ppermute | solution.py:117
  172.3 29.5 %collective-permute-done.14 = bf16[128,896]{1,0:T(8,128)(2,1)S(1)} collective-permute-done((bf16[128,896]{1,0:T(8,128)(2,1)S(1)}, bf16[128,896]{1,0:T(8,128)(2,1)S(1)}, u32[]{:S(2)}, u32[]{:S(2)}) %collective-permute-start.14) | collective-permute-done | bytes 229408 | tf_op jit(solution)/shard_map/ppermute | solution.py:117
  201.7 0.7 constant_dynamic-update-slice_fusion.10
  202.5 2.2 collective-permute-start.3
  204.6 0.9 constant_dynamic-update-slice_fusion.7
  205.5 1.2 collective-permute-start.7
  206.8 0.9 constant_dynamic-update-slice_fusion.6
  207.7 0.8 constant_dynamic-update-slice_fusion.5
  208.5 8.5 %collective-permute-done.3 = bf16[128,1024]{1,0:T(8,128)(2,1)S(1)} collective-permute-done((bf16[128,1024]{1,0:T(8,128)(2,1)S(1)}, bf16[128,1024]{1,0:T(8,128)(2,1)S(1)}, u32[]{:S(2)}, u32[]{:S(2)}) %collective-permute-start.3) | collective-permute-done | bytes 262176 | tf_op jit(solution)/shard_map/ppermute | solution.py:117
  217.0 0.7 constant_dynamic-update-slice_fusion.4
  217.7 3.1 collective-permute-done.7
  220.8 0.7 constant_dynamic-update-slice_fusion.3
  221.6 0.9 constant_dynamic-update-slice_fusion.2
  222.4 0.9 constant_dynamic-update-slice_fusion.1
  223.3 0.8 constant_dynamic-update-slice_fusion
  224.1 0.8 slice.35
  226.5 5.6 %convolution_convert_fusion = bf16[1280,896]{1,0:T(8,128)(2,1)} fusion(bf16[1024,896]{1,0:T(8,128)(2,1)} %constant_dynamic-update-slice_fusion.10, s32[1024]{0:T(1024)S(1)} %bitcast.50, s32[1024]{0:T(1024)S(1)} %bitcast.49), kind=kOutput, calls=%fused_computation.11 | convolution fusion | flops 2360442880 | bytes 4136960 | tf_op jit(solution)/shard_map/dot_general | solution.py:17
  232.1 6.8 %all-to-all-start = ((bf16[32,40,896]{2,1,0:T(8,128)(2,1)}), bf16[32,40,896]{2,1,0:T(8,128)(2,1)}, u32[]{:S(2)}, u32[]{:S(2)}) async-start(bf16[32,40,896]{2,1,0:T(8,128)(2,1)} %bitcast.18), calls=%async_computation | async-start | bytes 4587520 | tf_op jit(solution)/shard_map/all_to_all | solution.py:189
  239.0 8.1 %fusion.4 = bf16[1280,1024]{1,0:T(8,128)(2,1)S(1)} fusion(bf16[2112,1024]{1,0:T(8,128)(2,1)} %constant_dynamic-update-slice_fusion, s32[2112]{0:T(1024)S(1)} %eq.104), kind=kOutput, calls=%fused_computation.9 | convolution fusion | flops 5540495360 | bytes 6955264 | tf_op jit(solution)/shard_map/dot_general | solution.py:17
  247.1 20.0 %all-to-all-done = bf16[32,40,896]{2,1,0:T(8,128)(2,1)} async-done(((bf16[32,40,896]{2,1,0:T(8,128)(2,1)}), bf16[32,40,896]{2,1,0:T(8,128)(2,1)}, u32[]{:S(2)}, u32[]{:S(2)}) %all-to-all-start) | async-done | bytes 2293792 | tf_op jit(solution)/shard_map/all_to_all | solution.py:189
  267.1 38.2 %all_to_all.24 = bf16[32,40,1024]{2,1,0:T(8,128)(2,1)S(1)} all-to-all(bf16[32,40,1024]{2,1,0:T(8,128)(2,1)S(1)} %bitcast.46), channel_id=1, replica_groups=mesh['zh'=4,'zl'=2,'x'=4,'y'=4,'c'=2] {'x','y','c'}, dimensions={0} | all-to-all | bytes 5242880 | tf_op jit(solution)/shard_map/all_to_all | solution.py:190
  305.4 5.5 %fusion.10 = bf16[1,896,1024]{2,1,0:T(8,128)(2,1)} fusion(bf16[32,40,896]{2,1,0:T(8,128)(2,1)} %all-to-all-done, bf16[32,40,1024]{2,1,0:T(8,128)(2,1)S(1)} %all_to_all.24), kind=kOutput, calls=%fused_computation.15 | convolution fusion | flops 2349727744 | bytes 6750208 | tf_op jit(solution)/shard_map/dot_general | solution.py:17
  (62 shorter events, 9.2 us)
Async XLA Ops:
  7.2 303.7 %reduce-scatter.2.cloned.1.call-start = ((), (), s32[]{:S(2)}) async-start(), calls=%async_computation.4 | async-start | bytes 8257536 | tf_op jit(solution)/shard_map/reduce_scatter | solution.py:175
  77.5 0.7 copy-start.2
  77.5 1.1 copy-start.1
  78.1 4.7 %copy-start = (bf16[128,3584]{1,0:T(8,128)(2,1)S(1)}, bf16[128,3584]{1,0:T(8,128)(2,1)}, u32[]{:S(2)}) copy-start(bf16[128,3584]{1,0:T(8,128)(2,1)} %param.8) | copy-start | bytes 2752516
  80.8 20.7 %collective-permute-start = (bf16[264,1024]{1,0:T(8,128)(2,1)S(1)}, bf16[264,1024]{1,0:T(8,128)(2,1)S(1)}, u32[]{:S(2)}, u32[]{:S(2)}) collective-permute-start(bf16[264,1024]{1,0:T(8,128)(2,1)S(1)} %pad_maximum_fusion), channel_id=1, source_target_pairs={{0,32},{32,64},{64,96},{96,128},{128,160},{160,192},{192,224},{224... | collective-permute-start | bytes 1622024 | tf_op jit(solution)/shard_map/ppermute | solution.py:117
  82.8 22.0 %collective-permute-start.4 = (bf16[264,1024]{1,0:T(8,128)(2,1)S(1)}, bf16[264,1024]{1,0:T(8,128)(2,1)S(1)}, u32[]{:S(2)}, u32[]{:S(2)}) collective-permute-start(bf16[264,1024]{1,0:T(8,128)(2,1)S(1)} %pad_maximum_fusion), channel_id=1, source_target_pairs={{0,224},{32,0},{64,32},{96,64},{128,96},{160,128},{192,160},{224,1... | collective-permute-start | bytes 1622024 | tf_op jit(solution)/shard_map/ppermute | solution.py:117
  82.9 34.9 %copy-start.3 = (s32[8]{0:T(128)S(1)}, s32[8]{0:T(128)}, u32[]{:S(2)}) copy-start(s32[8]{0:T(128)} %constant.143) | copy-start | bytes 100
  82.9 34.9 %copy-start.4 = (s32[8]{0:T(128)S(1)}, s32[8]{0:T(128)}, u32[]{:S(2)}) copy-start(s32[8]{0:T(128)} %constant.144) | copy-start | bytes 100
  84.4 46.6 %collective-permute-start.8 = (bf16[128,896]{1,0:T(8,128)(2,1)}, bf16[128,896]{1,0:T(8,128)(2,1)}, u32[]{:S(2)}, u32[]{:S(2)}) collective-permute-start(bf16[128,896]{1,0:T(8,128)(2,1)} %bitcast.15), channel_id=1, source_target_pairs={{0,160},{32,128},{64,224},{96,192},{128,32},{160,0},{192,96},{224,... | collective-permute-start | bytes 688136 | tf_op jit(solution)/shard_map/ppermute | solution.py:117
  92.3 40.4 %collective-permute-start.9 = (bf16[128,896]{1,0:T(8,128)(2,1)}, bf16[128,896]{1,0:T(8,128)(2,1)S(1)}, u32[]{:S(2)}, u32[]{:S(2)}) collective-permute-start(bf16[128,896]{1,0:T(8,128)(2,1)} %bitcast.16), channel_id=1, source_target_pairs={{0,64},{32,224},{64,128},{96,32},{128,192},{160,96},{192,0},{224,1... | collective-permute-start | bytes 688136 | tf_op jit(solution)/shard_map/ppermute | solution.py:117
  93.1 42.3 %collective-permute-start.10 = (bf16[128,896]{1,0:T(8,128)(2,1)}, bf16[128,896]{1,0:T(8,128)(2,1)S(1)}, u32[]{:S(2)}, u32[]{:S(2)}) collective-permute-start(bf16[128,896]{1,0:T(8,128)(2,1)} %bitcast.17), channel_id=1, source_target_pairs={{0,224},{32,64},{64,32},{96,128},{128,96},{160,192},{192,160},{224... | collective-permute-start | bytes 688136 | tf_op jit(solution)/shard_map/ppermute | solution.py:117
  101.4 52.3 %collective-permute-start.1 = (bf16[264,1024]{1,0:T(8,128)(2,1)S(1)}, bf16[264,1024]{1,0:T(8,128)(2,1)S(1)}, u32[]{:S(2)}, u32[]{:S(2)}) collective-permute-start(bf16[264,1024]{1,0:T(8,128)(2,1)S(1)} %collective-permute-done), channel_id=1, source_target_pairs={{0,32},{32,64},{64,96},{96,128},{128,160},{160,192},{192,224},{224... | collective-permute-start | bytes 1622024 | tf_op jit(solution)/shard_map/ppermute | solution.py:117
  104.8 54.3 %collective-permute-start.5 = (bf16[264,1024]{1,0:T(8,128)(2,1)S(1)}, bf16[264,1024]{1,0:T(8,128)(2,1)S(1)}, u32[]{:S(2)}, u32[]{:S(2)}) collective-permute-start(bf16[264,1024]{1,0:T(8,128)(2,1)S(1)} %collective-permute-done.4), channel_id=1, source_target_pairs={{0,224},{32,0},{64,32},{96,64},{128,96},{160,128},{192,160},{224,1... | collective-permute-start | bytes 1622024 | tf_op jit(solution)/shard_map/ppermute | solution.py:117
  131.0 25.9 %collective-permute-start.11 = (bf16[128,896]{1,0:T(8,128)(2,1)S(1)}, bf16[128,896]{1,0:T(8,128)(2,1)S(1)}, u32[]{:S(2)}, u32[]{:S(2)}) collective-permute-start(bf16[128,896]{1,0:T(8,128)(2,1)S(1)} %bitcast.47), channel_id=1, source_target_pairs={{0,32},{32,0},{64,96},{96,64},{128,160},{160,128},{192,224},{224,1... | collective-permute-start | bytes 688136 | tf_op jit(solution)/shard_map/ppermute | solution.py:117
  132.7 29.6 %collective-permute-start.12 = (bf16[128,896]{1,0:T(8,128)(2,1)}, bf16[128,896]{1,0:T(8,128)(2,1)S(1)}, u32[]{:S(2)}, u32[]{:S(2)}) collective-permute-start(bf16[128,896]{1,0:T(8,128)(2,1)} %collective-permute-done.8), channel_id=1, source_target_pairs={{0,32},{32,0},{64,96},{96,64},{128,160},{160,128},{192,224},{224,1... | collective-permute-start | bytes 688136 | tf_op jit(solution)/shard_map/ppermute | solution.py:117
  135.4 36.1 %collective-permute-start.13 = (bf16[128,896]{1,0:T(8,128)(2,1)S(1)}, bf16[128,896]{1,0:T(8,128)(2,1)S(1)}, u32[]{:S(2)}, u32[]{:S(2)}) collective-permute-start(bf16[128,896]{1,0:T(8,128)(2,1)S(1)} %collective-permute-done.9), channel_id=1, source_target_pairs={{0,32},{32,0},{64,96},{96,64},{128,160},{160,128},{192,224},{224,1... | collective-permute-start | bytes 688136 | tf_op jit(solution)/shard_map/ppermute | solution.py:117
  153.8 48.7 %collective-permute-start.2 = (bf16[264,1024]{1,0:T(8,128)(2,1)S(1)}, bf16[264,1024]{1,0:T(8,128)(2,1)S(1)}, u32[]{:S(2)}, u32[]{:S(2)}) collective-permute-start(bf16[264,1024]{1,0:T(8,128)(2,1)S(1)} %collective-permute-done.1), channel_id=1, source_target_pairs={{0,32},{32,64},{64,96},{96,128},{128,160},{160,192},{192,224},{224... | collective-permute-start | bytes 1622024 | tf_op jit(solution)/shard_map/ppermute | solution.py:117
  157.0 44.8 %collective-permute-start.14 = (bf16[128,896]{1,0:T(8,128)(2,1)S(1)}, bf16[128,896]{1,0:T(8,128)(2,1)S(1)}, u32[]{:S(2)}, u32[]{:S(2)}) collective-permute-start(bf16[128,896]{1,0:T(8,128)(2,1)S(1)} %collective-permute-done.10), channel_id=1, source_target_pairs={{0,32},{32,0},{64,96},{96,64},{128,160},{160,128},{192,224},{224,1... | collective-permute-start | bytes 688136 | tf_op jit(solution)/shard_map/ppermute | solution.py:117
  159.1 46.4 %collective-permute-start.6 = (bf16[264,1024]{1,0:T(8,128)(2,1)S(1)}, bf16[264,1024]{1,0:T(8,128)(2,1)S(1)}, u32[]{:S(2)}, u32[]{:S(2)}) collective-permute-start(bf16[264,1024]{1,0:T(8,128)(2,1)S(1)} %collective-permute-done.5), channel_id=1, source_target_pairs={{0,224},{32,0},{64,32},{96,64},{128,96},{160,128},{192,160},{224,1... | collective-permute-start | bytes 1622024 | tf_op jit(solution)/shard_map/ppermute | solution.py:117
  202.5 14.5 %collective-permute-start.3 = (bf16[128,1024]{1,0:T(8,128)(2,1)S(1)}, bf16[128,1024]{1,0:T(8,128)(2,1)S(1)}, u32[]{:S(2)}, u32[]{:S(2)}) collective-permute-start(bf16[128,1024]{1,0:T(8,128)(2,1)S(1)} %slice.33), channel_id=1, source_target_pairs={{0,32},{32,64},{64,96},{96,128},{128,160},{160,192},{192,224},{224... | collective-permute-start | bytes 786440 | tf_op jit(solution)/shard_map/ppermute | solution.py:117
  205.5 15.3 %collective-permute-start.7 = (bf16[136,1024]{1,0:T(8,128)(2,1)S(1)}, bf16[136,1024]{1,0:T(8,128)(2,1)S(1)}, u32[]{:S(2)}, u32[]{:S(2)}) collective-permute-start(bf16[136,1024]{1,0:T(8,128)(2,1)S(1)} %slice.34), channel_id=1, source_target_pairs={{0,224},{32,0},{64,32},{96,64},{128,96},{160,128},{192,160},{224,1... | collective-permute-start | bytes 835592 | tf_op jit(solution)/shard_map/ppermute | solution.py:117
  232.1 35.0 %all-to-all-start = ((bf16[32,40,896]{2,1,0:T(8,128)(2,1)}), bf16[32,40,896]{2,1,0:T(8,128)(2,1)}, u32[]{:S(2)}, u32[]{:S(2)}) async-start(bf16[32,40,896]{2,1,0:T(8,128)(2,1)} %bitcast.18), calls=%async_computation | async-start | bytes 4587520 | tf_op jit(solution)/shard_map/all_to_all | solution.py:189
Sparse Core Ops, SparseCore 0:
  77.6 146.6 reduce-scatter.1

commit v5 on v4

--- a/solution.py
+++ b/solution.py
@@ -4,6 +4,7 @@
 import jax.numpy as jnp
 from jax import lax
 from jax.experimental import pallas as pl
+from jax.experimental.pallas import tpu as pltpu
 from jax.sharding import Mesh, PartitionSpec as P
 
 Z = ("zh", "zl")
@@ -21,10 +22,6 @@
     order = jnp.arange(ids.shape[0], dtype=jnp.int32)
     same = (ids[:, None] == ids[None, :]) & (order[:, None] < order[None, :])
     return jnp.sum(same.astype(jnp.int32), axis=0)
-
-
-def one_hot(slots, count):
-    return (jnp.arange(count, dtype=jnp.int32)[:, None] == slots[None, :]).astype(BF)
 
 
 def fill_kernel(half, s_ref, t_ref, act_ref, grad_ref, out_ref):
@@ -110,6 +107,80 @@
         cost_estimate=pl.CostEstimate(flops=4_000_000_000, bytes_accessed=12_000_000, transcendentals=0),
         name="products_b",
     )(recv)
+
+
+def sort_acts_kernel(spots, most, meta_ref, *refs):
+    blocks, rows_ref, slots_ref, held = refs[:8], refs[8], refs[9], refs[10]
+    tokens = slots_ref.shape[1] // 2
+    base = pl.program_id(0) * rows_ref.shape[0]
+    row = lax.broadcasted_iota(jnp.int32, (rows_ref.shape[0], tokens), 0) + base
+    picks = []
+    for n, block in enumerate(blocks):
+        told = block[tokens : tokens + 8, :tokens].astype(jnp.float32).astype(jnp.int32)
+        pick = None
+        for k in range(2):
+            expert, pos = told[2 * k : 2 * k + 1], told[2 * k + 1 : 2 * k + 2]
+            slot = (expert % spots) * (8 * most) + meta_ref[n] * most + pos
+            slot = jnp.where(expert // spots == meta_ref[8], slot, -1)
+            slots_ref[n : n + 1, k * tokens : (k + 1) * tokens] = slot
+            hit = row == slot
+            pick = hit if pick is None else pick | hit
+        picks.append(pick.astype(BF))
+
+    @pl.when(pl.program_id(0) == 0)
+    def _():
+        for n, block in enumerate(blocks):
+            held[n * tokens : (n + 1) * tokens, :] = block[:tokens, :]
+
+    rows_ref[...] = contract(jnp.concatenate(picks, axis=1), held[...], ((1,), (0,))).astype(BF)
+
+
+def sort_acts(blocks, meta, tokens, spots, most):
+    width = blocks[0].shape[1]
+    total = spots * 8 * most
+    return pl.pallas_call(
+        functools.partial(sort_acts_kernel, spots, most),
+        grid=(2,),
+        in_specs=[pl.BlockSpec(memory_space=pltpu.SMEM)] + [pl.BlockSpec(b.shape, lambda i: (0, 0)) for b in blocks],
+        out_specs=[pl.BlockSpec((total // 2, width), lambda i: (i, 0)), pl.BlockSpec((8, 2 * tokens), lambda i: (0, 0))],
+        out_shape=[jax.ShapeDtypeStruct((total, width), BF), jax.ShapeDtypeStruct((8, 2 * tokens), jnp.int32)],
+        scratch_shapes=[pltpu.VMEM((8 * tokens, width), BF)],
+        cost_estimate=pl.CostEstimate(flops=2_400_000_000, bytes_accessed=5_000_000, transcendentals=0),
+        name="sort_acts",
+    )(meta, *blocks)
+
+
+def sort_grads_kernel(at_ref, slots_ref, *refs):
+    parts, rows_ref, held = refs[:-2], refs[-2], refs[-1]
+    pairs = slots_ref.shape[1]
+    base = pl.program_id(0) * rows_ref.shape[0]
+    row = lax.broadcasted_iota(jnp.int32, (rows_ref.shape[0], pairs), 0) + base
+
+    @pl.when(pl.program_id(0) == 0)
+    def _():
+        start = 0
+        for part in parts:
+            held[start : start + part.shape[0], :] = part[...]
+            start += part.shape[0]
+
+    picks = [(row == slots_ref[pl.ds(at_ref[n], 1), :]).astype(BF) for n in range(8)]
+    rows_ref[...] = contract(jnp.concatenate(picks, axis=1), held[...], ((1,), (0,))).astype(BF)
+
+
+def sort_grads(parts, slots, at, total):
+    width = parts[0].shape[1]
+    pairs = slots.shape[1]
+    return pl.pallas_call(
+        sort_grads_kernel,
+        grid=(2,),
+        in_specs=[pl.BlockSpec(memory_space=pltpu.SMEM), pl.BlockSpec(slots.shape, lambda i: (0, 0))]
+        + [pl.BlockSpec(p.shape, lambda i: (0, 0)) for p in parts],
+        out_specs=pl.BlockSpec((total // 2, width), lambda i: (i, 0)),
+        out_shape=jax.ShapeDtypeStruct((total, width), BF),
+        scratch_shapes=[pltpu.VMEM((8 * pairs, width), BF)],
+        cost_estimate=pl.CostEstimate(flops=5_400_000_000, bytes_accessed=7_000_000, transcendentals=0),
+        name="sort_grads",
+    )(at, slots, *parts)
 
 
 def ordered(block_in, target):
@@ -133,26 +204,23 @@
     my_z = 2 * my_zh + my_zl
     sign = 1 - 2 * my_zl
 
-    ids_a = route_a.reshape(-1)
-    info = jnp.stack([ids_a, positions(ids_a)]).astype(BF)
-    info = jnp.pad(info, ((0, 6), (0, hidden - pairs)))
-    grads = jnp.concatenate([grad_a.reshape(pairs, hidden), info], axis=0)
+    grads = jnp.moveaxis(grad_a, 1, 0).reshape(pairs, hidden)
     up, down = [grads], [grads]
     for _ in range(1, 4):
         up.append(ordered(up[-1], lambda z: z + 1))
         down.append(ordered(down[-1], lambda z: z - 1))
-    cut = pairs // 2
-    across = jnp.concatenate(
-        [ordered(up[3][:cut], lambda z: z + 1), ordered(down[3][cut:], lambda z: z - 1)],
-        axis=0,
-    )
+    across = [ordered(up[3][:tokens], lambda z: z + 1), ordered(down[3][tokens:], lambda z: z - 1)]
     ring = (0, -1, -2, -3, 4, 3, 2, 1)
-    all_grads = jnp.concatenate(up + [across] + down[:0:-1], axis=0)
-
+
+    ids_a = route_a.reshape(-1)
+    info = jnp.stack([ids_a, positions(ids_a)]).reshape(2, tokens, top)
+    info = jnp.moveaxis(info, 2, 0).reshape(2 * top, tokens).astype(BF)
+    info = jnp.pad(info, ((0, 8 - 2 * top), (0, quarter - tokens)))
     quarters = jnp.moveaxis(act_a.reshape(tokens, 4, quarter), 1, 0)
 
     def mine(which):
-        return lax.dynamic_index_in_dim(quarters, lax.rem(which + 8, 4), 0, keepdims=False)
+        rows = lax.dynamic_index_in_dim(quarters, lax.rem(which + 8, 4), 0, keepdims=False)
+        return jnp.concatenate([rows, info], axis=0)
 
     def along(block_in, step):
         return ordered(block_in, lambda z: z + step * (1 - 2 * (z % 2)))
@@ -175,19 +243,16 @@
     wgrad_b = lax.psum_scatter(parts, Z, scatter_dimension=0, tiled=True)[None]
 
     total = spots * planes * most
-    told = all_grads.reshape(planes, pairs + 8, hidden)[:, pairs : pairs + 2, :pairs].astype(jnp.int32)
-    origin = lax.rem(jnp.stack([my_z + o for o in ring]) + planes, planes)
-    slots = (told[:, 0] % spots) * (planes * most) + origin[:, None] * most + told[:, 1]
-    slots = jnp.where(told[:, 0] // spots == my_zl, slots, -1)
-    even = slots[jnp.array([ring.index(o) for o in offsets])]
-    odd = slots[jnp.array([ring.index(-o if -o in ring else 4) for o in offsets])]
-    slots_t = jnp.where(my_zl == 0, even, odd)
-    pick_tok = one_hot(slots_t[:, 0::2].reshape(-1), total) + one_hot(slots_t[:, 1::2].reshape(-1), total)
-    rows_a = contract(pick_tok, jnp.concatenate(near + far, axis=0), ((1,), (0,))).astype(BF)
-    slots_g = jnp.pad(slots, ((0, 0), (0, 8)), constant_values=-1)
-    rows_g = contract(one_hot(slots_g.reshape(-1), total), all_grads, ((1,), (0,))).astype(BF)
-    recv_a = lax.all_to_all(rows_a, PLANE, 0, 0, tiled=True)
-    recv_g = lax.all_to_all(rows_g, PLANE, 0, 0, tiled=True)
+    origin = [lax.rem(my_z + o * sign + planes, planes) for o in offsets]
+    rows_a, slots = sort_acts(near + far, jnp.stack(origin + [my_zl]), tokens, spots, most)
+    even = [offsets.index(o) for o in ring]
+    odd = [offsets.index(-o if -o in offsets else 4) for o in ring]
+    at = jnp.stack([jnp.where(my_zl == 0, e, o).astype(jnp.int32) for e, o in zip(even, odd)])
+    rows_g = sort_grads(up + across + down[:0:-1], slots, at, total)
+    rows_a = rows_a.reshape(spots, planes * most, quarter)
+    rows_g = rows_g.reshape(spots, planes * most, hidden)
+    recv_a = lax.all_to_all(rows_a, PLANE, 0, 0, tiled=True).reshape(total, quarter)
+    recv_g = lax.all_to_all(rows_g, PLANE, 0, 0, tiled=True).reshape(total, hidden)
     wgrad_a = contract(recv_a, recv_g, ((0,), (0,))).astype(BF)[None]
     return wgrad_a, wgrad_b
 

time: 323 us -> 295 us (0.913)
  the two profiles are of different devices: /device:TPU:34 before, /device:TPU:1 now
where the time goes in v5:
time: 295 us; the launch traced here: 294 us
  waiting for transfers between devices  114 us (39%)
  blocking collectives  98.1 us (33%)
  Pallas kernels  28.2 us (10%)
  starting transfers between devices  23.5 us (8%)
  between operations  14.3 us (5%)
  local copies, waits for them, and re-layouts  9.7 us (3%)
  matrix products  3.84 us (1%)
    ppermute x15, waiting for transfers between devices, ordered(): lax.ppermute(block_in, Z, [(z, target(z) % planes) for z in range(planes)])  114 us
    all_to_all x1, blocking collectives, shards(): lax.all_to_all(send_b.reshape(spots, TILE, send_b.shape[-1]), PLANE, 0, 0...  56 us
    all_to_all x1, blocking collectives, shards(): lax.all_to_all(rows_g, PLANE, 0, 0, tiled=True).reshape(total, hidden)  42.2 us
    ppermute x15, starting transfers between devices, ordered(): lax.ppermute(block_in, Z, [(z, target(z) % planes) for z in range(planes)])  18.6 us
    pallas_call x1, Pallas kernels, sort_grads(): pl.pallas_call(sort_grads_kernel, grid=(2,), in_specs=[pl.BlockSpec(memor...  9.38 us
    pallas_call x1, Pallas kernels, products(): pl.pallas_call(functools.partial(products_kernel, half, hidden), grid=(2,...  8.14 us
    pallas_call x1, Pallas kernels, sort_acts(): pl.pallas_call(functools.partial(sort_acts_kernel, spots, most), grid=(2,...  6.7 us
  transfers between devices with their start and end apart: 17, of which 10 were waited for; matrix products, arithmetic and copies ran while one was open for 3% of the time, Pallas kernels for 5%

profile of v5, /device:TPU:1, one launch (start us, length us, event | category | flops | bytes accessed | tf_op | source)
XLA Modules:
  0.0 294.1 jit_solution(17166259537658698290)
XLA Ops:
  7.2 0.8 copy.49
  8.0 0.1 eq.47
  8.1 0.1 reshape.187
  8.3 0.1 convert_reduce_fusion
  8.4 0.1 reduce_sum.25
  8.6 1.3 fusion.12.t_ref
  9.9 2.0 reshape.188.grad_ref
  11.9 0.6 fusion.11.s_ref
  12.5 4.0 %fill_b.1 = bf16[16,2,8,7552]{3,2,1,0:T(8,128)(2,1)} custom-call(s32[1,256]{1,0:T(1,128)} %fusion.11.s_ref, s32[2,128]{1,0:T(2,128)} %fusion.12.t_ref, bf16[128,3584]{1,0:T(8,128)(2,1)} %act_ref.1, bf16[256,1024]{1,0:T(8,128)(2,1)} %reshape.188.grad_ref), custom_call_target="tpu_custom_call" | custom-call | flops 2000000000 | bytes 6000000 | tf_op jit(solution)/shard_map/fill_b/pallas_call | solution.py:62
  16.5 56.0 %all_to_all.15.in_ref = bf16[32,8,7552]{2,1,0:T(8,128)(2,1)} all-to-all(bf16[32,8,7552]{2,1,0:T(8,128)(2,1)} %bitcast.47), channel_id=1, replica_groups=mesh['zh'=4,'zl'=2,'x'=4,'y'=4,'c'=2] {'x','y','c'}, dimensions={0} | all-to-all | bytes 7733248 | tf_op jit(solution)/shard_map/all_to_all | solution.py:240
  72.4 8.1 %products_b.1 = bf16[4,2,448,1024]{3,2,1,0:T(8,128)(2,1)} custom-call(bf16[32,8,7552]{2,1,0:T(8,128)(2,1)} %all_to_all.15.in_ref), custom_call_target="tpu_custom_call" | custom-call | flops 4000000000 | bytes 12000000 | tf_op jit(solution)/shard_map/products_b/pallas_call | solution.py:101
  80.6 0.6 copy-done.6
  81.3 0.1 copy.42
  81.4 0.1 eq.20
  81.5 0.1 convert_reduce_fusion.1
  81.6 0.2 stack.72
  81.9 0.2 reshape.183
  82.2 1.9 constant_dynamic-slice_fusion
  84.2 0.1 fusion.7
  84.3 5.7 %collective-permute-start.2 = (bf16[136,896]{1,0:T(8,128)(2,1)S(1)}, bf16[136,896]{1,0:T(8,128)(2,1)S(1)}, u32[]{:S(2)}, u32[]{:S(2)}) collective-permute-start(bf16[136,896]{1,0:T(8,128)(2,1)S(1)} %get-tuple-element.10), channel_id=1, source_target_pairs={{0,224},{32,64},{64,32},{96,128},{128,96},{160,192},{192,160},{224... | collective-permute-start | bytes 731144 | tf_op jit(solution)/shard_map/ppermute | solution.py:188
  90.0 1.6 collective-permute-start
  91.6 0.6 collective-permute-start.1
  92.2 16.1 %collective-permute-done.2.refs_3_ = bf16[136,896]{1,0:T(8,128)(2,1)S(1)} collective-permute-done((bf16[136,896]{1,0:T(8,128)(2,1)S(1)}, bf16[136,896]{1,0:T(8,128)(2,1)S(1)}, u32[]{:S(2)}, u32[]{:S(2)}) %collective-permute-start.2) | collective-permute-done | bytes 243744 | tf_op jit(solution)/shard_map/ppermute | solution.py:188
  108.3 12.2 %collective-permute-done.refs_1_ = bf16[136,896]{1,0:T(8,128)(2,1)S(1)} collective-permute-done((bf16[136,896]{1,0:T(8,128)(2,1)S(1)}, bf16[136,896]{1,0:T(8,128)(2,1)S(1)}, u32[]{:S(2)}, u32[]{:S(2)}) %collective-permute-start) | collective-permute-done | bytes 243744 | tf_op jit(solution)/shard_map/ppermute | solution.py:188
  120.5 1.5 collective-permute-start.5
  122.0 0.1 copy.48
  122.1 2.8 collective-permute-start.11
  124.9 0.7 stack.70.meta_ref
  125.6 3.6 %collective-permute-done.6.refs_7_ = bf16[136,896]{1,0:T(8,128)(2,1)S(1)} collective-permute-done((bf16[136,896]{1,0:T(8,128)(2,1)S(1)}, bf16[136,896]{1,0:T(8,128)(2,1)S(1)}, u32[]{:S(2)}, u32[]{:S(2)}) %collective-permute-start.6) | collective-permute-done | bytes 243744 | tf_op jit(solution)/shard_map/ppermute | solution.py:188
  129.2 10.4 %collective-permute-done.4.refs_5_ = bf16[136,896]{1,0:T(8,128)(2,1)S(1)} collective-permute-done((bf16[136,896]{1,0:T(8,128)(2,1)S(1)}, bf16[136,896]{1,0:T(8,128)(2,1)S(1)}, u32[]{:S(2)}, u32[]{:S(2)}) %collective-permute-start.4) | collective-permute-done | bytes 243744 | tf_op jit(solution)/shard_map/ppermute | solution.py:188
  139.6 10.4 %collective-permute-done.5.refs_6_ = bf16[136,896]{1,0:T(8,128)(2,1)S(1)} collective-permute-done((bf16[136,896]{1,0:T(8,128)(2,1)S(1)}, bf16[136,896]{1,0:T(8,128)(2,1)S(1)}, u32[]{:S(2)}, u32[]{:S(2)}) %collective-permute-start.5) | collective-permute-done | bytes 243744 | tf_op jit(solution)/shard_map/ppermute | solution.py:188
  150.1 0.7 copy-done.16
  150.8 6.7 %sort_acts.1 = (bf16[1280,896]{1,0:T(8,128)(2,1)}, s32[8,256]{1,0:T(8,128)}) custom-call(s32[9]{0:T(128)} %stack.70.meta_ref, bf16[136,896]{1,0:T(8,128)(2,1)} %copy-done.3, bf16[136,896]{1,0:T(8,128)(2,1)} %copy-done.11, bf16[136,896]{1,0:T(8,128)(2,1)} %copy-done.12, bf16[136,896]{1,0:T(8,128)(2,1)} %copy-done.10, bf16[136,896]{1,0:T(8,128)(2,1)} %copy-done.13, ...), custom_call_target="tpu_custom_call" | custom-call | flops 2400000000 | bytes 5000000 | tf_op jit(solution)/shard_map/sort_acts/pallas_call | solution.py:141
  157.5 4.8 %all-to-all-start = ((bf16[32,40,896]{2,1,0:T(8,128)(2,1)}), bf16[32,40,896]{2,1,0:T(8,128)(2,1)S(1)}, u32[]{:S(2)}, u32[]{:S(2)}) async-start(bf16[32,40,896]{2,1,0:T(8,128)(2,1)} %bitcast.49), calls=%async_computation | async-start | bytes 4587520 | tf_op jit(solution)/shard_map/all_to_all | solution.py:254
  162.3 10.2 %collective-permute-done.11.refs_8_ = bf16[256,1024]{1,0:T(8,128)(2,1)S(1)} collective-permute-done((bf16[256,1024]{1,0:T(8,128)(2,1)S(1)}, bf16[256,1024]{1,0:T(8,128)(2,1)S(1)}, u32[]{:S(2)}, u32[]{:S(2)}) %collective-permute-start.11) | collective-permute-done | bytes 524320 | tf_op jit(solution)/shard_map/ppermute | solution.py:188
  172.5 2.2 collective-permute-start.12
  174.8 22.8 %collective-permute-done.12.refs_7_ = bf16[256,1024]{1,0:T(8,128)(2,1)S(1)} collective-permute-done((bf16[256,1024]{1,0:T(8,128)(2,1)S(1)}, bf16[256,1024]{1,0:T(8,128)(2,1)S(1)}, u32[]{:S(2)}, u32[]{:S(2)}) %collective-permute-start.12) | collective-permute-done | bytes 524320 | tf_op jit(solution)/shard_map/ppermute | solution.py:188
  197.6 2.0 collective-permute-start.13
  199.6 0.2 collective-permute-start.9
  199.8 22.6 %collective-permute-done.13.refs_6_ = bf16[256,1024]{1,0:T(8,128)(2,1)S(1)} collective-permute-done((bf16[256,1024]{1,0:T(8,128)(2,1)S(1)}, bf16[256,1024]{1,0:T(8,128)(2,1)S(1)}, u32[]{:S(2)}, u32[]{:S(2)}) %collective-permute-start.13) | collective-permute-done | bytes 524320 | tf_op jit(solution)/shard_map/ppermute | solution.py:188
  222.4 1.9 collective-permute-start.14
  224.4 0.8 copy-done.5
  225.4 0.7 stack.80.at_ref
  226.0 5.6 %collective-permute-done.14.refs_5_ = bf16[128,1024]{1,0:T(8,128)(2,1)} collective-permute-done((bf16[128,1024]{1,0:T(8,128)(2,1)S(1)}, bf16[128,1024]{1,0:T(8,128)(2,1)}, u32[]{:S(2)}, u32[]{:S(2)}) %collective-permute-start.14) | collective-permute-done | bytes 262176 | tf_op jit(solution)/shard_map/ppermute | solution.py:188
  231.7 0.2 collective-permute-done.10.refs_4_
  231.9 9.4 %sort_grads.1 = bf16[1280,1024]{1,0:T(8,128)(2,1)} custom-call(s32[8]{0:T(128)} %stack.80.at_ref, s32[8,256]{1,0:T(8,128)} %get-tuple-element.5.slots_ref, bf16[256,1024]{1,0:T(8,128)(2,1)} %bitcast.53, bf16[256,1024]{1,0:T(8,128)(2,1)} %collective-permute-done.7.refs_1_, bf16[256,1024]{1,0:T(8,128)(2,1)} %copy-done.9, bf16[256,1024]{1,0:T(8,128)(2,1)} %copy-done.5, ...), custom_call_target="tpu_custom_call" | custom-call | flops 5400000000 | bytes 7000000 | tf_op jit(solution)/shard_map/sort_grads/pallas_call | solution.py:173
  241.3 42.2 %all_to_all.16 = bf16[32,40,1024]{2,1,0:T(8,128)(2,1)S(1)} all-to-all(bf16[32,40,1024]{2,1,0:T(8,128)(2,1)} %bitcast.48), channel_id=1, replica_groups=mesh['zh'=4,'zl'=2,'x'=4,'y'=4,'c'=2] {'x','y','c'}, dimensions={0} | all-to-all | bytes 5242880 | tf_op jit(solution)/shard_map/all_to_all | solution.py:255
  283.4 3.8 %fusion = bf16[1,896,1024]{2,1,0:T(8,128)(2,1)} fusion(bf16[32,40,896]{2,1,0:T(8,128)(2,1)S(1)} %all-to-all-done, bf16[32,40,1024]{2,1,0:T(8,128)(2,1)S(1)} %all_to_all.16), kind=kOutput, calls=%fused_computation.1 | convolution fusion | flops 2349727744 | bytes 6750208 | tf_op jit(solution)/shard_map/dot_general | solution.py:18
  (56 shorter events, 0.6 us)
Async XLA Ops:
  7.2 280.1 %reduce-scatter.2.cloned.1.call-start = ((), (), s32[]{:S(2)}) async-start(), calls=%async_computation.4 | async-start | bytes 8257536 | tf_op jit(solution)/shard_map/reduce_scatter | solution.py:243
  80.6 0.7 copy-start.6
  80.6 1.4 copy-start
  84.1 37.9 %copy-start.1 = (bf16[128,2,1024]{2,1,0:T(2,128)(2,1)S(1)}, bf16[128,2,1024]{2,1,0:T(2,128)(2,1)}, u32[]{:S(2)}) copy-start(bf16[128,2,1024]{2,1,0:T(2,128)(2,1)} %param.7) | copy-start | bytes 1572868
  84.3 65.7 %copy-start.3 = (bf16[136,896]{1,0:T(8,128)(2,1)}, bf16[136,896]{1,0:T(8,128)(2,1)S(1)}, u32[]{:S(2)}) copy-start(bf16[136,896]{1,0:T(8,128)(2,1)S(1)} %get-tuple-element.11.refs_0_) | copy-start | bytes 731140
  84.3 24.0 %collective-permute-start.2 = (bf16[136,896]{1,0:T(8,128)(2,1)S(1)}, bf16[136,896]{1,0:T(8,128)(2,1)S(1)}, u32[]{:S(2)}, u32[]{:S(2)}) collective-permute-start(bf16[136,896]{1,0:T(8,128)(2,1)S(1)} %get-tuple-element.10), channel_id=1, source_target_pairs={{0,224},{32,64},{64,32},{96,128},{128,96},{160,192},{192,160},{224... | collective-permute-start | bytes 731144 | tf_op jit(solution)/shard_map/ppermute | solution.py:188
  90.0 30.5 %collective-permute-start = (bf16[136,896]{1,0:T(8,128)(2,1)S(1)}, bf16[136,896]{1,0:T(8,128)(2,1)S(1)}, u32[]{:S(2)}, u32[]{:S(2)}) collective-permute-start(bf16[136,896]{1,0:T(8,128)(2,1)S(1)} %get-tuple-element.12), channel_id=1, source_target_pairs={{0,160},{32,128},{64,224},{96,192},{128,32},{160,0},{192,96},{224,... | collective-permute-start | bytes 731144 | tf_op jit(solution)/shard_map/ppermute | solution.py:188
  91.6 28.9 %collective-permute-start.1 = (bf16[136,896]{1,0:T(8,128)(2,1)S(1)}, bf16[136,896]{1,0:T(8,128)(2,1)S(1)}, u32[]{:S(2)}, u32[]{:S(2)}) collective-permute-start(bf16[136,896]{1,0:T(8,128)(2,1)S(1)} %get-tuple-element.13), channel_id=1, source_target_pairs={{0,64},{32,224},{64,128},{96,32},{128,192},{160,96},{192,0},{224,1... | collective-permute-start | bytes 731144 | tf_op jit(solution)/shard_map/ppermute | solution.py:188
  92.2 33.4 %collective-permute-start.3 = (bf16[136,896]{1,0:T(8,128)(2,1)S(1)}, bf16[136,896]{1,0:T(8,128)(2,1)S(1)}, u32[]{:S(2)}, u32[]{:S(2)}) collective-permute-start(bf16[136,896]{1,0:T(8,128)(2,1)S(1)} %get-tuple-element.11.refs_0_), channel_id=1, source_target_pairs={{0,32},{32,0},{64,96},{96,64},{128,160},{160,128},{192,224},{224,1... | collective-permute-start | bytes 731144 | tf_op jit(solution)/shard_map/ppermute | solution.py:188
  108.3 41.7 %copy-start.10 = (bf16[136,896]{1,0:T(8,128)(2,1)}, bf16[136,896]{1,0:T(8,128)(2,1)S(1)}, u32[]{:S(2)}) copy-start(bf16[136,896]{1,0:T(8,128)(2,1)S(1)} %collective-permute-done.2.refs_3_) | copy-start | bytes 731140
  108.3 20.8 %collective-permute-start.6 = (bf16[136,896]{1,0:T(8,128)(2,1)S(1)}, bf16[136,896]{1,0:T(8,128)(2,1)S(1)}, u32[]{:S(2)}, u32[]{:S(2)}) collective-permute-start(bf16[136,896]{1,0:T(8,128)(2,1)S(1)} %collective-permute-done.2.refs_3_), channel_id=1, source_target_pairs={{0,32},{32,0},{64,96},{96,64},{128,160},{160,128},{192,224},{224,1... | collective-permute-start | bytes 731144 | tf_op jit(solution)/shard_map/ppermute | solution.py:188
  120.5 29.6 %copy-start.11 = (bf16[136,896]{1,0:T(8,128)(2,1)}, bf16[136,896]{1,0:T(8,128)(2,1)S(1)}, u32[]{:S(2)}) copy-start(bf16[136,896]{1,0:T(8,128)(2,1)S(1)} %collective-permute-done.refs_1_) | copy-start | bytes 731140
  120.5 19.1 %collective-permute-start.4 = (bf16[136,896]{1,0:T(8,128)(2,1)S(1)}, bf16[136,896]{1,0:T(8,128)(2,1)S(1)}, u32[]{:S(2)}, u32[]{:S(2)}) collective-permute-start(bf16[136,896]{1,0:T(8,128)(2,1)S(1)} %collective-permute-done.refs_1_), channel_id=1, source_target_pairs={{0,32},{32,0},{64,96},{96,64},{128,160},{160,128},{192,224},{224,1... | collective-permute-start | bytes 731144 | tf_op jit(solution)/shard_map/ppermute | solution.py:188
  120.5 29.6 %copy-start.12 = (bf16[136,896]{1,0:T(8,128)(2,1)}, bf16[136,896]{1,0:T(8,128)(2,1)S(1)}, u32[]{:S(2)}) copy-start(bf16[136,896]{1,0:T(8,128)(2,1)S(1)} %collective-permute-done.1.refs_2_) | copy-start | bytes 731140
  120.5 29.5 %collective-permute-start.5 = (bf16[136,896]{1,0:T(8,128)(2,1)S(1)}, bf16[136,896]{1,0:T(8,128)(2,1)S(1)}, u32[]{:S(2)}, u32[]{:S(2)}) collective-permute-start(bf16[136,896]{1,0:T(8,128)(2,1)S(1)} %collective-permute-done.1.refs_2_), channel_id=1, source_target_pairs={{0,32},{32,0},{64,96},{96,64},{128,160},{160,128},{192,224},{224,1... | collective-permute-start | bytes 731144 | tf_op jit(solution)/shard_map/ppermute | solution.py:188
  122.1 35.4 %copy-start.2 = (bf16[2,128,1024]{2,1,0:T(8,128)(2,1)}, bf16[2,128,1024]{2,1,0:T(8,128)(2,1)S(1)}, u32[]{:S(2)}) copy-start(bf16[2,128,1024]{2,1,0:T(8,128)(2,1)S(1)} %copy.48) | copy-start | bytes 1572868
  122.1 50.4 %collective-permute-start.11 = (bf16[256,1024]{1,0:T(8,128)(2,1)S(1)}, bf16[256,1024]{1,0:T(8,128)(2,1)S(1)}, u32[]{:S(2)}, u32[]{:S(2)}) collective-permute-start(bf16[256,1024]{1,0:T(8,128)(2,1)S(1)} %bitcast.51), channel_id=1, source_target_pairs={{0,224},{32,0},{64,32},{96,64},{128,96},{160,128},{192,160},{224,1... | collective-permute-start | bytes 1572872 | tf_op jit(solution)/shard_map/ppermute | solution.py:188
  125.6 24.5 %copy-start.13 = (bf16[136,896]{1,0:T(8,128)(2,1)}, bf16[136,896]{1,0:T(8,128)(2,1)S(1)}, u32[]{:S(2)}) copy-start(bf16[136,896]{1,0:T(8,128)(2,1)S(1)} %collective-permute-done.3.refs_4_) | copy-start | bytes 731140
  125.6 49.2 %collective-permute-start.7 = (bf16[256,1024]{1,0:T(8,128)(2,1)S(1)}, bf16[256,1024]{1,0:T(8,128)(2,1)}, u32[]{:S(2)}, u32[]{:S(2)}) collective-permute-start(bf16[256,1024]{1,0:T(8,128)(2,1)S(1)} %bitcast.52), channel_id=1, source_target_pairs={{0,32},{32,64},{64,96},{96,128},{128,160},{160,192},{192,224},{224... | collective-permute-start | bytes 1572872 | tf_op jit(solution)/shard_map/ppermute | solution.py:188
  129.2 20.9 %copy-start.14 = (bf16[136,896]{1,0:T(8,128)(2,1)}, bf16[136,896]{1,0:T(8,128)(2,1)S(1)}, u32[]{:S(2)}) copy-start(bf16[136,896]{1,0:T(8,128)(2,1)S(1)} %collective-permute-done.6.refs_7_) | copy-start | bytes 731140
  139.6 10.5 %copy-start.15 = (bf16[136,896]{1,0:T(8,128)(2,1)}, bf16[136,896]{1,0:T(8,128)(2,1)S(1)}, u32[]{:S(2)}) copy-start(bf16[136,896]{1,0:T(8,128)(2,1)S(1)} %collective-permute-done.4.refs_5_) | copy-start | bytes 731140
  150.1 0.7 copy-start.16
  157.5 83.8 %all-to-all-start = ((bf16[32,40,896]{2,1,0:T(8,128)(2,1)}), bf16[32,40,896]{2,1,0:T(8,128)(2,1)S(1)}, u32[]{:S(2)}, u32[]{:S(2)}) async-start(bf16[32,40,896]{2,1,0:T(8,128)(2,1)} %bitcast.49), calls=%async_computation | async-start | bytes 4587520 | tf_op jit(solution)/shard_map/all_to_all | solution.py:254
  172.5 2.3 copy-start.7
  172.5 25.1 %collective-permute-start.12 = (bf16[256,1024]{1,0:T(8,128)(2,1)S(1)}, bf16[256,1024]{1,0:T(8,128)(2,1)S(1)}, u32[]{:S(2)}, u32[]{:S(2)}) collective-permute-start(bf16[256,1024]{1,0:T(8,128)(2,1)S(1)} %collective-permute-done.11.refs_8_), channel_id=1, source_target_pairs={{0,224},{32,0},{64,32},{96,64},{128,96},{160,128},{192,160},{224,1... | collective-permute-start | bytes 1572872 | tf_op jit(solution)/shard_map/ppermute | solution.py:188
  174.8 24.9 %collective-permute-start.8 = (bf16[256,1024]{1,0:T(8,128)(2,1)}, bf16[256,1024]{1,0:T(8,128)(2,1)S(1)}, u32[]{:S(2)}, u32[]{:S(2)}) collective-permute-start(bf16[256,1024]{1,0:T(8,128)(2,1)} %collective-permute-done.7.refs_1_), channel_id=1, source_target_pairs={{0,32},{32,64},{64,96},{96,128},{128,160},{160,192},{192,224},{224... | collective-permute-start | bytes 1572872 | tf_op jit(solution)/shard_map/ppermute | solution.py:188
  197.6 2.2 copy-start.8
  197.6 24.8 %collective-permute-start.13 = (bf16[256,1024]{1,0:T(8,128)(2,1)S(1)}, bf16[256,1024]{1,0:T(8,128)(2,1)S(1)}, u32[]{:S(2)}, u32[]{:S(2)}) collective-permute-start(bf16[256,1024]{1,0:T(8,128)(2,1)S(1)} %collective-permute-done.12.refs_7_), channel_id=1, source_target_pairs={{0,224},{32,0},{64,32},{96,64},{128,96},{160,128},{192,160},{224,1... | collective-permute-start | bytes 1572872 | tf_op jit(solution)/shard_map/ppermute | solution.py:188
  199.6 25.6 %copy-start.9 = (bf16[256,1024]{1,0:T(8,128)(2,1)}, bf16[256,1024]{1,0:T(8,128)(2,1)S(1)}, u32[]{:S(2)}) copy-start(bf16[256,1024]{1,0:T(8,128)(2,1)S(1)} %collective-permute-done.8.refs_2_) | copy-start | bytes 1572868
  199.6 24.8 %collective-permute-start.9 = (bf16[256,1024]{1,0:T(8,128)(2,1)S(1)}, bf16[256,1024]{1,0:T(8,128)(2,1)S(1)}, u32[]{:S(2)}, u32[]{:S(2)}) collective-permute-start(bf16[256,1024]{1,0:T(8,128)(2,1)S(1)} %collective-permute-done.8.refs_2_), channel_id=1, source_target_pairs={{0,32},{32,64},{64,96},{96,128},{128,160},{160,192},{192,224},{224... | collective-permute-start | bytes 1572872 | tf_op jit(solution)/shard_map/ppermute | solution.py:188
  222.4 9.4 %copy-start.4 = (bf16[256,1024]{1,0:T(8,128)(2,1)}, bf16[256,1024]{1,0:T(8,128)(2,1)S(1)}, u32[]{:S(2)}) copy-start(bf16[256,1024]{1,0:T(8,128)(2,1)S(1)} %collective-permute-done.13.refs_6_) | copy-start | bytes 1572868
  222.4 9.2 %collective-permute-start.14 = (bf16[128,1024]{1,0:T(8,128)(2,1)S(1)}, bf16[128,1024]{1,0:T(8,128)(2,1)}, u32[]{:S(2)}, u32[]{:S(2)}) collective-permute-start(bf16[128,1024]{1,0:T(8,128)(2,1)S(1)} %slice.9), channel_id=1, source_target_pairs={{0,224},{32,0},{64,32},{96,64},{128,96},{160,128},{192,160},{224,1... | collective-permute-start | bytes 786440 | tf_op jit(solution)/shard_map/ppermute | solution.py:188
  224.4 0.8 copy-start.5
  225.2 6.6 %collective-permute-start.10 = (bf16[128,1024]{1,0:T(8,128)(2,1)S(1)}, bf16[128,1024]{1,0:T(8,128)(2,1)}, u32[]{:S(2)}, u32[]{:S(2)}) collective-permute-start(bf16[128,1024]{1,0:T(8,128)(2,1)S(1)} %slice.8), channel_id=1, source_target_pairs={{0,32},{32,64},{64,96},{96,128},{128,160},{160,192},{192,224},{224... | collective-permute-start | bytes 786440 | tf_op jit(solution)/shard_map/ppermute | solution.py:188
Sparse Core Ops, SparseCore 0:
  80.7 148.0 reduce-scatter.1

commit v6 on v5

--- a/solution.py
+++ b/solution.py
@@ -24,27 +24,30 @@
     return jnp.sum(same.astype(jnp.int32), axis=0)
 
 
-def fill_kernel(half, s_ref, t_ref, act_ref, grad_ref, out_ref):
+def fill_kernel(half, ids_ref, act_ref, grad_ref, out_ref):
     chips = out_ref.shape[0]
     rows = chips * TILE
-    pairs = s_ref.shape[1]
-    tokens = t_ref.shape[1]
+    tokens = ids_ref.shape[1]
+    pairs = 2 * tokens
     width = half + grad_ref.shape[1]
     quarter = half // 2
+    ids = jnp.concatenate([ids_ref[0:1, :], ids_ref[1:2, :]], axis=1)
+    named = (lax.broadcasted_iota(jnp.int32, (2 * chips, pairs), 0) == ids).astype(jnp.float32)
+    earlier = lax.broadcasted_iota(jnp.int32, (pairs, pairs), 0) < lax.broadcasted_iota(jnp.int32, (pairs, pairs), 1)
+    before = contract(named.astype(BF), earlier.astype(BF), ((1,), (0,)))
+    pos = jnp.sum(named * before, axis=0, keepdims=True).astype(jnp.int32)
+    expert = ids // chips
+    row = jnp.where(pos < TILE, expert * rows + pos, 2 * rows + expert * 2 + pos - TILE)
+    slots = (ids % chips) * TILE + row
     lower = lax.broadcasted_iota(jnp.int32, (rows, 1), 0) % TILE < TILE // 2
     for tile in range(3):
-
-        def spots(count):
-            row = lax.broadcasted_iota(jnp.int32, (rows, count), 0)
-            if tile == 2:
-                row = row - row % TILE + row % (TILE // 2)
-            return row + tile * rows
-
-        pick = (spots(pairs) == s_ref[...]).astype(BF)
-        spot = spots(tokens)
-        pick_tok = ((spot == t_ref[0:1, :]) | (spot == t_ref[1:2, :])).astype(BF)
+        spot = lax.broadcasted_iota(jnp.int32, (rows, pairs), 0)
+        if tile == 2:
+            spot = spot - spot % TILE + spot % (TILE // 2)
+        pick = (spot + tile * rows == slots).astype(jnp.float32)
+        pick_tok = (pick[:, :tokens] + pick[:, tokens:]).astype(BF)
         acts = contract(pick_tok, act_ref[...], ((1,), (0,))).astype(BF)
-        grads = contract(pick, grad_ref[...], ((1,), (0,))).astype(BF)
+        grads = contract(pick.astype(BF), grad_ref[...], ((1,), (0,))).astype(BF)
         if tile == 2:
             acts = jnp.where(lower, acts[:, :quarter], acts[:, quarter:])
         start = tile * width
@@ -54,7 +57,7 @@
             out_ref[p, 0, :, middle : middle + grads.shape[1]] = grads[p * TILE : (p + 1) * TILE]
 
 
-def fill(slots, act, grad, chips):
+def fill(ids, act, grad, chips):
     tokens, features = act.shape
     pairs, hidden = grad.shape
     half = features // 2
@@ -63,7 +66,6 @@
         functools.partial(fill_kernel, half),
         grid=(2,),
         in_specs=[
-            pl.BlockSpec((1, pairs), lambda c: (0, 0)),
             pl.BlockSpec((2, tokens), lambda c: (0, 0)),
             pl.BlockSpec((tokens, half), lambda c: (0, c)),
             pl.BlockSpec((pairs, hidden), lambda c: (0, 0)),
@@ -72,7 +74,7 @@
         out_shape=jax.ShapeDtypeStruct((chips, 2, TILE, width), BF),
         cost_estimate=pl.CostEstimate(flops=2_000_000_000, bytes_accessed=6_000_000, transcendentals=0),
         name="fill_b",
-    )(slots.reshape(1, pairs), slots.reshape(tokens, 2).T, act, grad)
+    )(ids, act, grad)
 
 
 def products_kernel(half, hidden, in_ref, out_ref):
@@ -212,9 +214,9 @@
     across = [ordered(up[3][:tokens], lambda z: z + 1), ordered(down[3][tokens:], lambda z: z - 1)]
     ring = (0, -1, -2, -3, 4, 3, 2, 1)
 
-    ids_a = route_a.reshape(-1)
-    info = jnp.stack([ids_a, positions(ids_a)]).reshape(2, tokens, top)
-    info = jnp.moveaxis(info, 2, 0).reshape(2 * top, tokens).astype(BF)
+    ids_a = route_a.T
+    pos_a = positions(ids_a.reshape(-1)).reshape(top, tokens)
+    info = jnp.stack([ids_a, pos_a], axis=1).reshape(2 * top, tokens).astype(BF)
     info = jnp.pad(info, ((0, 8 - 2 * top), (0, quarter - tokens)))
     quarters = jnp.moveaxis(act_a.reshape(tokens, 4, quarter), 1, 0)
 
@@ -231,12 +233,8 @@
     offsets = (0, -3, -2, -1, 1, 4, 3, 2)
     far = [along(b, 1) for b in near]
 
-    ids_b = route_b.reshape(-1)
-    pos_b = positions(ids_b)
-    lower = ids_b // chips
-    row_b = jnp.where(pos_b < TILE, lower * (chips * TILE) + pos_b, 2 * chips * TILE + lower * 2 + pos_b - TILE)
-    slots_b = (ids_b % chips) * TILE + row_b
-    send_b = fill(slots_b, act_b, grad_b.reshape(pairs, hidden), chips)
+    grads_b = jnp.moveaxis(grad_b, 1, 0).reshape(pairs, hidden)
+    send_b = fill(route_b.T, act_b, grads_b, chips)
     recv_b = lax.all_to_all(send_b.reshape(spots, TILE, send_b.shape[-1]), PLANE, 0, 0, tiled=True)
 
     parts = products(recv_b, half, hidden).reshape(features, hidden)

time: 295 us -> 291 us (0.986)
  transfers between devices with their start and end apart: 17 -> 17, of which waited for: 10 -> 10; matrix products, arithmetic and copies ran while one was open for 3% -> 3% of each run, Pallas kernels for 5% -> 6%
where the time goes in v6:
time: 291 us
  waiting for transfers between devices  112 us (38%)
  blocking collectives  98 us (34%)
  Pallas kernels  28.5 us (10%)
  starting transfers between devices  26 us (9%)
  between operations  14.3 us (5%)
  local copies, waits for them, and re-layouts  8.18 us (3%)
  matrix products  3.84 us (1%)
    ppermute x15, waiting for transfers between devices, ordered(): lax.ppermute(block_in, Z, [(z, target(z) % planes) for z in range(planes)])  112 us
    all_to_all x1, blocking collectives, shards(): lax.all_to_all(send_b.reshape(spots, TILE, send_b.shape[-1]), PLANE, 0, 0...  56 us
    all_to_all x1, blocking collectives, shards(): lax.all_to_all(rows_g, PLANE, 0, 0, tiled=True).reshape(total, hidden)  42 us
    ppermute x15, starting transfers between devices, ordered(): lax.ppermute(block_in, Z, [(z, target(z) % planes) for z in range(planes)])  20.9 us
    pallas_call x1, Pallas kernels, sort_grads(): pl.pallas_call(sort_grads_kernel, grid=(2,), in_specs=[pl.BlockSpec(memor...  9.37 us
    pallas_call x1, Pallas kernels, products(): pl.pallas_call(functools.partial(products_kernel, half, hidden), grid=(2,...  8.13 us
    pallas_call x1, Pallas kernels, sort_acts(): pl.pallas_call(functools.partial(sort_acts_kernel, spots, most), grid=(2,...  6.7 us
  transfers between devices with their start and end apart: 17, of which 10 were waited for; matrix products, arithmetic and copies ran while one was open for 3% of the time, Pallas kernels for 6%

profile of v6, /device:TPU:1, one launch (start us, length us, event | category | flops | bytes accessed | tf_op | source)
XLA Modules:
  0.0 290.6 jit_solution(10831381557008418697)
XLA Ops:
  7.2 0.0 reduce-scatter.2.cloned.1.call-start
  7.2 2.0 copy.21
  9.2 4.3 %fill_b.1 = bf16[16,2,8,7552]{3,2,1,0:T(8,128)(2,1)} custom-call(s32[2,128]{1,0:T(2,128)} %bitcast.65, bf16[128,3584]{1,0:T(8,128)(2,1)} %act_ref.1, bf16[256,1024]{1,0:T(8,128)(2,1)} %bitcast.61), custom_call_target="tpu_custom_call" | custom-call | flops 2000000000 | bytes 6000000 | tf_op jit(solution)/shard_map/fill_b/pallas_call | solution.py:65
  13.5 56.0 %all_to_all.15.in_ref = bf16[32,8,7552]{2,1,0:T(8,128)(2,1)} all-to-all(bf16[32,8,7552]{2,1,0:T(8,128)(2,1)} %bitcast.53), channel_id=1, replica_groups=mesh['zh'=4,'zl'=2,'x'=4,'y'=4,'c'=2] {'x','y','c'}, dimensions={0} | all-to-all | bytes 7733248 | tf_op jit(solution)/shard_map/all_to_all | solution.py:238
  69.4 8.1 %products_b.1 = bf16[4,2,448,1024]{3,2,1,0:T(8,128)(2,1)} custom-call(bf16[32,8,7552]{2,1,0:T(8,128)(2,1)} %all_to_all.15.in_ref), custom_call_target="tpu_custom_call" | custom-call | flops 4000000000 | bytes 12000000 | tf_op jit(solution)/shard_map/products_b/pallas_call | solution.py:103
  77.6 0.0 reduce-scatter.2.cloned.1.call-update
  77.6 0.6 copy-done.6
  78.3 0.1 convert_reduce_fusion
  78.4 0.4 copy-done
  78.8 0.2 reshape.39
  79.0 1.9 constant_dynamic-slice_fusion
  80.9 0.0 copy-start.1
  80.9 0.1 copy_bitcast_fusion
  81.0 0.1 copy_bitcast_fusion.2
  81.1 0.1 fusion.6
  81.2 5.7 %collective-permute-start.2 = (bf16[136,896]{1,0:T(8,128)(2,1)S(1)}, bf16[136,896]{1,0:T(8,128)(2,1)S(1)}, u32[]{:S(2)}, u32[]{:S(2)}) collective-permute-start(bf16[136,896]{1,0:T(8,128)(2,1)S(1)} %get-tuple-element.10), channel_id=1, source_target_pairs={{0,224},{32,64},{64,32},{96,128},{128,96},{160,192},{192,160},{224... | collective-permute-start | bytes 731144 | tf_op jit(solution)/shard_map/ppermute | solution.py:190
  86.8 1.6 collective-permute-start
  88.5 0.5 collective-permute-start.1
  89.0 0.0 collective-permute-start.3
  89.0 15.9 %collective-permute-done.2.refs_3_ = bf16[136,896]{1,0:T(8,128)(2,1)S(1)} collective-permute-done((bf16[136,896]{1,0:T(8,128)(2,1)S(1)}, bf16[136,896]{1,0:T(8,128)(2,1)S(1)}, u32[]{:S(2)}, u32[]{:S(2)}) %collective-permute-start.2) | collective-permute-done | bytes 243744 | tf_op jit(solution)/shard_map/ppermute | solution.py:190
  104.9 12.2 %collective-permute-done.refs_1_ = bf16[136,896]{1,0:T(8,128)(2,1)S(1)} collective-permute-done((bf16[136,896]{1,0:T(8,128)(2,1)S(1)}, bf16[136,896]{1,0:T(8,128)(2,1)S(1)}, u32[]{:S(2)}, u32[]{:S(2)}) %collective-permute-start) | collective-permute-done | bytes 243744 | tf_op jit(solution)/shard_map/ppermute | solution.py:190
  117.1 0.0 collective-permute-start.4
  117.1 0.0 collective-permute-done.1.refs_2_
  117.1 1.5 collective-permute-start.5
  118.6 0.1 copy.20
  118.7 0.0 copy-start.2
  118.7 3.2 %collective-permute-start.11 = (bf16[256,1024]{1,0:T(8,128)(2,1)S(1)}, bf16[256,1024]{1,0:T(8,128)(2,1)S(1)}, u32[]{:S(2)}, u32[]{:S(2)}) collective-permute-start(bf16[256,1024]{1,0:T(8,128)(2,1)S(1)} %bitcast.58), channel_id=1, source_target_pairs={{0,224},{32,0},{64,32},{96,64},{128,96},{160,128},{192,160},{224,1... | collective-permute-start | bytes 1572872 | tf_op jit(solution)/shard_map/ppermute | solution.py:190
  121.9 0.7 stack.70.meta_ref
  122.6 3.2 %collective-permute-done.6.refs_7_ = bf16[136,896]{1,0:T(8,128)(2,1)S(1)} collective-permute-done((bf16[136,896]{1,0:T(8,128)(2,1)S(1)}, bf16[136,896]{1,0:T(8,128)(2,1)S(1)}, u32[]{:S(2)}, u32[]{:S(2)}) %collective-permute-start.6) | collective-permute-done | bytes 243744 | tf_op jit(solution)/shard_map/ppermute | solution.py:190
  125.7 10.4 %collective-permute-done.4.refs_5_ = bf16[136,896]{1,0:T(8,128)(2,1)S(1)} collective-permute-done((bf16[136,896]{1,0:T(8,128)(2,1)S(1)}, bf16[136,896]{1,0:T(8,128)(2,1)S(1)}, u32[]{:S(2)}, u32[]{:S(2)}) %collective-permute-start.4) | collective-permute-done | bytes 243744 | tf_op jit(solution)/shard_map/ppermute | solution.py:190
  136.2 10.4 %collective-permute-done.5.refs_6_ = bf16[136,896]{1,0:T(8,128)(2,1)S(1)} collective-permute-done((bf16[136,896]{1,0:T(8,128)(2,1)S(1)}, bf16[136,896]{1,0:T(8,128)(2,1)S(1)}, u32[]{:S(2)}, u32[]{:S(2)}) %collective-permute-start.5) | collective-permute-done | bytes 243744 | tf_op jit(solution)/shard_map/ppermute | solution.py:190
  146.7 0.7 copy-done.16
  147.4 6.7 %sort_acts.1 = (bf16[1280,896]{1,0:T(8,128)(2,1)}, s32[8,256]{1,0:T(8,128)}) custom-call(s32[9]{0:T(128)} %stack.70.meta_ref, bf16[136,896]{1,0:T(8,128)(2,1)} %copy-done.3, bf16[136,896]{1,0:T(8,128)(2,1)} %copy-done.11, bf16[136,896]{1,0:T(8,128)(2,1)} %copy-done.12, bf16[136,896]{1,0:T(8,128)(2,1)} %copy-done.10, bf16[136,896]{1,0:T(8,128)(2,1)} %copy-done.13, ...), custom_call_target="tpu_custom_call" | custom-call | flops 2400000000 | bytes 5000000 | tf_op jit(solution)/shard_map/sort_acts/pallas_call | solution.py:143
  154.1 5.1 %all-to-all-start = ((bf16[32,40,896]{2,1,0:T(8,128)(2,1)}), bf16[32,40,896]{2,1,0:T(8,128)(2,1)S(1)}, u32[]{:S(2)}, u32[]{:S(2)}) async-start(bf16[32,40,896]{2,1,0:T(8,128)(2,1)} %bitcast.55), calls=%async_computation | async-start | bytes 4587520 | tf_op jit(solution)/shard_map/all_to_all | solution.py:252
  159.2 9.7 %collective-permute-done.11.refs_8_ = bf16[256,1024]{1,0:T(8,128)(2,1)S(1)} collective-permute-done((bf16[256,1024]{1,0:T(8,128)(2,1)S(1)}, bf16[256,1024]{1,0:T(8,128)(2,1)S(1)}, u32[]{:S(2)}, u32[]{:S(2)}) %collective-permute-start.11) | collective-permute-done | bytes 524320 | tf_op jit(solution)/shard_map/ppermute | solution.py:190
  168.8 2.7 collective-permute-start.12
  171.5 22.2 %collective-permute-done.12.refs_7_ = bf16[256,1024]{1,0:T(8,128)(2,1)S(1)} collective-permute-done((bf16[256,1024]{1,0:T(8,128)(2,1)S(1)}, bf16[256,1024]{1,0:T(8,128)(2,1)S(1)}, u32[]{:S(2)}, u32[]{:S(2)}) %collective-permute-start.12) | collective-permute-done | bytes 524320 | tf_op jit(solution)/shard_map/ppermute | solution.py:190
  193.7 2.9 %collective-permute-start.13 = (bf16[256,1024]{1,0:T(8,128)(2,1)S(1)}, bf16[256,1024]{1,0:T(8,128)(2,1)S(1)}, u32[]{:S(2)}, u32[]{:S(2)}) collective-permute-start(bf16[256,1024]{1,0:T(8,128)(2,1)S(1)} %collective-permute-done.12.refs_7_), channel_id=1, source_target_pairs={{0,224},{32,0},{64,32},{96,64},{128,96},{160,128},{192,160},{224,1... | collective-permute-start | bytes 1572872 | tf_op jit(solution)/shard_map/ppermute | solution.py:190
  196.7 21.7 %collective-permute-done.13.refs_6_ = bf16[256,1024]{1,0:T(8,128)(2,1)S(1)} collective-permute-done((bf16[256,1024]{1,0:T(8,128)(2,1)S(1)}, bf16[256,1024]{1,0:T(8,128)(2,1)S(1)}, u32[]{:S(2)}, u32[]{:S(2)}) %collective-permute-start.13) | collective-permute-done | bytes 524320 | tf_op jit(solution)/shard_map/ppermute | solution.py:190
  218.4 2.7 collective-permute-start.14
  221.1 0.8 copy-done.5
  221.9 0.1 collective-permute-start.10
  222.1 0.7 stack.79.at_ref
  222.7 5.7 %collective-permute-done.14.refs_5_ = bf16[128,1024]{1,0:T(8,128)(2,1)} collective-permute-done((bf16[128,1024]{1,0:T(8,128)(2,1)S(1)}, bf16[128,1024]{1,0:T(8,128)(2,1)}, u32[]{:S(2)}, u32[]{:S(2)}) %collective-permute-start.14) | collective-permute-done | bytes 262176 | tf_op jit(solution)/shard_map/ppermute | solution.py:190
  228.4 0.2 collective-permute-done.10.refs_4_
  228.6 9.4 %sort_grads.1 = bf16[1280,1024]{1,0:T(8,128)(2,1)} custom-call(s32[8]{0:T(128)} %stack.79.at_ref, s32[8,256]{1,0:T(8,128)} %get-tuple-element.5.slots_ref, bf16[256,1024]{1,0:T(8,128)(2,1)} %bitcast.60, bf16[256,1024]{1,0:T(8,128)(2,1)} %collective-permute-done.7.refs_1_, bf16[256,1024]{1,0:T(8,128)(2,1)} %copy-done.9, bf16[256,1024]{1,0:T(8,128)(2,1)} %copy-done.5, ...), custom_call_target="tpu_custom_call" | custom-call | flops 5400000000 | bytes 7000000 | tf_op jit(solution)/shard_map/sort_grads/pallas_call | solution.py:175
  237.9 42.0 %all_to_all.16 = bf16[32,40,1024]{2,1,0:T(8,128)(2,1)S(1)} all-to-all(bf16[32,40,1024]{2,1,0:T(8,128)(2,1)} %bitcast.54), channel_id=1, replica_groups=mesh['zh'=4,'zl'=2,'x'=4,'y'=4,'c'=2] {'x','y','c'}, dimensions={0} | all-to-all | bytes 5242880 | tf_op jit(solution)/shard_map/all_to_all | solution.py:253
  279.9 3.8 %fusion = bf16[1,896,1024]{2,1,0:T(8,128)(2,1)} fusion(bf16[32,40,896]{2,1,0:T(8,128)(2,1)S(1)} %all-to-all-done, bf16[32,40,1024]{2,1,0:T(8,128)(2,1)S(1)} %all_to_all.16), kind=kOutput, calls=%fused_computation.1 | convolution fusion | flops 2349727744 | bytes 6750208 | tf_op jit(solution)/shard_map/dot_general | solution.py:18
  (44 shorter events, 0.1 us)
Async XLA Ops:
  7.2 276.6 %reduce-scatter.2.cloned.1.call-start = ((), (), s32[]{:S(2)}) async-start(), calls=%async_computation.4 | async-start | bytes 8257536 | tf_op jit(solution)/shard_map/reduce_scatter | solution.py:241
  77.6 0.7 copy-start.6
  77.6 1.2 copy-start
  80.9 37.7 %copy-start.1 = (bf16[128,2,1024]{2,1,0:T(2,128)(2,1)S(1)}, bf16[128,2,1024]{2,1,0:T(2,128)(2,1)}, u32[]{:S(2)}) copy-start(bf16[128,2,1024]{2,1,0:T(2,128)(2,1)} %param.7) | copy-start | bytes 1572868
  81.1 65.5 %copy-start.3 = (bf16[136,896]{1,0:T(8,128)(2,1)}, bf16[136,896]{1,0:T(8,128)(2,1)S(1)}, u32[]{:S(2)}) copy-start(bf16[136,896]{1,0:T(8,128)(2,1)S(1)} %get-tuple-element.11.refs_0_) | copy-start | bytes 731140
  81.2 23.7 %collective-permute-start.2 = (bf16[136,896]{1,0:T(8,128)(2,1)S(1)}, bf16[136,896]{1,0:T(8,128)(2,1)S(1)}, u32[]{:S(2)}, u32[]{:S(2)}) collective-permute-start(bf16[136,896]{1,0:T(8,128)(2,1)S(1)} %get-tuple-element.10), channel_id=1, source_target_pairs={{0,224},{32,64},{64,32},{96,128},{128,96},{160,192},{192,160},{224... | collective-permute-start | bytes 731144 | tf_op jit(solution)/shard_map/ppermute | solution.py:190
  86.8 30.3 %collective-permute-start = (bf16[136,896]{1,0:T(8,128)(2,1)S(1)}, bf16[136,896]{1,0:T(8,128)(2,1)S(1)}, u32[]{:S(2)}, u32[]{:S(2)}) collective-permute-start(bf16[136,896]{1,0:T(8,128)(2,1)S(1)} %get-tuple-element.12), channel_id=1, source_target_pairs={{0,160},{32,128},{64,224},{96,192},{128,32},{160,0},{192,96},{224,... | collective-permute-start | bytes 731144 | tf_op jit(solution)/shard_map/ppermute | solution.py:190
  88.5 28.7 %collective-permute-start.1 = (bf16[136,896]{1,0:T(8,128)(2,1)S(1)}, bf16[136,896]{1,0:T(8,128)(2,1)S(1)}, u32[]{:S(2)}, u32[]{:S(2)}) collective-permute-start(bf16[136,896]{1,0:T(8,128)(2,1)S(1)} %get-tuple-element.13), channel_id=1, source_target_pairs={{0,64},{32,224},{64,128},{96,32},{128,192},{160,96},{192,0},{224,1... | collective-permute-start | bytes 731144 | tf_op jit(solution)/shard_map/ppermute | solution.py:190
  89.0 33.6 %collective-permute-start.3 = (bf16[136,896]{1,0:T(8,128)(2,1)S(1)}, bf16[136,896]{1,0:T(8,128)(2,1)S(1)}, u32[]{:S(2)}, u32[]{:S(2)}) collective-permute-start(bf16[136,896]{1,0:T(8,128)(2,1)S(1)} %get-tuple-element.11.refs_0_), channel_id=1, source_target_pairs={{0,32},{32,0},{64,96},{96,64},{128,160},{160,128},{192,224},{224,1... | collective-permute-start | bytes 731144 | tf_op jit(solution)/shard_map/ppermute | solution.py:190
  104.9 41.7 %copy-start.10 = (bf16[136,896]{1,0:T(8,128)(2,1)}, bf16[136,896]{1,0:T(8,128)(2,1)S(1)}, u32[]{:S(2)}) copy-start(bf16[136,896]{1,0:T(8,128)(2,1)S(1)} %collective-permute-done.2.refs_3_) | copy-start | bytes 731140
  104.9 20.8 %collective-permute-start.6 = (bf16[136,896]{1,0:T(8,128)(2,1)S(1)}, bf16[136,896]{1,0:T(8,128)(2,1)S(1)}, u32[]{:S(2)}, u32[]{:S(2)}) collective-permute-start(bf16[136,896]{1,0:T(8,128)(2,1)S(1)} %collective-permute-done.2.refs_3_), channel_id=1, source_target_pairs={{0,32},{32,0},{64,96},{96,64},{128,160},{160,128},{192,224},{224,1... | collective-permute-start | bytes 731144 | tf_op jit(solution)/shard_map/ppermute | solution.py:190
  117.1 29.5 %copy-start.11 = (bf16[136,896]{1,0:T(8,128)(2,1)}, bf16[136,896]{1,0:T(8,128)(2,1)S(1)}, u32[]{:S(2)}) copy-start(bf16[136,896]{1,0:T(8,128)(2,1)S(1)} %collective-permute-done.refs_1_) | copy-start | bytes 731140
  117.1 19.1 %collective-permute-start.4 = (bf16[136,896]{1,0:T(8,128)(2,1)S(1)}, bf16[136,896]{1,0:T(8,128)(2,1)S(1)}, u32[]{:S(2)}, u32[]{:S(2)}) collective-permute-start(bf16[136,896]{1,0:T(8,128)(2,1)S(1)} %collective-permute-done.refs_1_), channel_id=1, source_target_pairs={{0,32},{32,0},{64,96},{96,64},{128,160},{160,128},{192,224},{224,1... | collective-permute-start | bytes 731144 | tf_op jit(solution)/shard_map/ppermute | solution.py:190
  117.1 29.5 %copy-start.12 = (bf16[136,896]{1,0:T(8,128)(2,1)}, bf16[136,896]{1,0:T(8,128)(2,1)S(1)}, u32[]{:S(2)}) copy-start(bf16[136,896]{1,0:T(8,128)(2,1)S(1)} %collective-permute-done.1.refs_2_) | copy-start | bytes 731140
  117.1 29.5 %collective-permute-start.5 = (bf16[136,896]{1,0:T(8,128)(2,1)S(1)}, bf16[136,896]{1,0:T(8,128)(2,1)S(1)}, u32[]{:S(2)}, u32[]{:S(2)}) collective-permute-start(bf16[136,896]{1,0:T(8,128)(2,1)S(1)} %collective-permute-done.1.refs_2_), channel_id=1, source_target_pairs={{0,32},{32,0},{64,96},{96,64},{128,160},{160,128},{192,224},{224,1... | collective-permute-start | bytes 731144 | tf_op jit(solution)/shard_map/ppermute | solution.py:190
  118.7 35.4 %copy-start.2 = (bf16[2,128,1024]{2,1,0:T(8,128)(2,1)}, bf16[2,128,1024]{2,1,0:T(8,128)(2,1)S(1)}, u32[]{:S(2)}) copy-start(bf16[2,128,1024]{2,1,0:T(8,128)(2,1)S(1)} %copy.20) | copy-start | bytes 1572868
  118.7 50.1 %collective-permute-start.11 = (bf16[256,1024]{1,0:T(8,128)(2,1)S(1)}, bf16[256,1024]{1,0:T(8,128)(2,1)S(1)}, u32[]{:S(2)}, u32[]{:S(2)}) collective-permute-start(bf16[256,1024]{1,0:T(8,128)(2,1)S(1)} %bitcast.58), channel_id=1, source_target_pairs={{0,224},{32,0},{64,32},{96,64},{128,96},{160,128},{192,160},{224,1... | collective-permute-start | bytes 1572872 | tf_op jit(solution)/shard_map/ppermute | solution.py:190
  122.6 24.1 %copy-start.13 = (bf16[136,896]{1,0:T(8,128)(2,1)}, bf16[136,896]{1,0:T(8,128)(2,1)S(1)}, u32[]{:S(2)}) copy-start(bf16[136,896]{1,0:T(8,128)(2,1)S(1)} %collective-permute-done.3.refs_4_) | copy-start | bytes 731140
  122.6 48.9 %collective-permute-start.7 = (bf16[256,1024]{1,0:T(8,128)(2,1)S(1)}, bf16[256,1024]{1,0:T(8,128)(2,1)}, u32[]{:S(2)}, u32[]{:S(2)}) collective-permute-start(bf16[256,1024]{1,0:T(8,128)(2,1)S(1)} %bitcast.59), channel_id=1, source_target_pairs={{0,32},{32,64},{64,96},{96,128},{128,160},{160,192},{192,224},{224... | collective-permute-start | bytes 1572872 | tf_op jit(solution)/shard_map/ppermute | solution.py:190
  125.7 20.9 %copy-start.14 = (bf16[136,896]{1,0:T(8,128)(2,1)}, bf16[136,896]{1,0:T(8,128)(2,1)S(1)}, u32[]{:S(2)}) copy-start(bf16[136,896]{1,0:T(8,128)(2,1)S(1)} %collective-permute-done.6.refs_7_) | copy-start | bytes 731140
  136.2 10.5 %copy-start.15 = (bf16[136,896]{1,0:T(8,128)(2,1)}, bf16[136,896]{1,0:T(8,128)(2,1)S(1)}, u32[]{:S(2)}) copy-start(bf16[136,896]{1,0:T(8,128)(2,1)S(1)} %collective-permute-done.4.refs_5_) | copy-start | bytes 731140
  146.7 0.7 copy-start.16
  154.1 83.9 %all-to-all-start = ((bf16[32,40,896]{2,1,0:T(8,128)(2,1)}), bf16[32,40,896]{2,1,0:T(8,128)(2,1)S(1)}, u32[]{:S(2)}, u32[]{:S(2)}) async-start(bf16[32,40,896]{2,1,0:T(8,128)(2,1)} %bitcast.55), calls=%async_computation | async-start | bytes 4587520 | tf_op jit(solution)/shard_map/all_to_all | solution.py:252
  168.8 2.7 copy-start.7
  168.8 24.9 %collective-permute-start.12 = (bf16[256,1024]{1,0:T(8,128)(2,1)S(1)}, bf16[256,1024]{1,0:T(8,128)(2,1)S(1)}, u32[]{:S(2)}, u32[]{:S(2)}) collective-permute-start(bf16[256,1024]{1,0:T(8,128)(2,1)S(1)} %collective-permute-done.11.refs_8_), channel_id=1, source_target_pairs={{0,224},{32,0},{64,32},{96,64},{128,96},{160,128},{192,160},{224,1... | collective-permute-start | bytes 1572872 | tf_op jit(solution)/shard_map/ppermute | solution.py:190
  171.5 25.1 %collective-permute-start.8 = (bf16[256,1024]{1,0:T(8,128)(2,1)}, bf16[256,1024]{1,0:T(8,128)(2,1)S(1)}, u32[]{:S(2)}, u32[]{:S(2)}) collective-permute-start(bf16[256,1024]{1,0:T(8,128)(2,1)} %collective-permute-done.7.refs_1_), channel_id=1, source_target_pairs={{0,32},{32,64},{64,96},{96,128},{128,160},{160,192},{192,224},{224... | collective-permute-start | bytes 1572872 | tf_op jit(solution)/shard_map/ppermute | solution.py:190
  193.7 2.9 %copy-start.8 = (bf16[256,1024]{1,0:T(8,128)(2,1)}, bf16[256,1024]{1,0:T(8,128)(2,1)S(1)}, u32[]{:S(2)}) copy-start(bf16[256,1024]{1,0:T(8,128)(2,1)S(1)} %collective-permute-done.12.refs_7_) | copy-start | bytes 1572868
  193.7 24.6 %collective-permute-start.13 = (bf16[256,1024]{1,0:T(8,128)(2,1)S(1)}, bf16[256,1024]{1,0:T(8,128)(2,1)S(1)}, u32[]{:S(2)}, u32[]{:S(2)}) collective-permute-start(bf16[256,1024]{1,0:T(8,128)(2,1)S(1)} %collective-permute-done.12.refs_7_), channel_id=1, source_target_pairs={{0,224},{32,0},{64,32},{96,64},{128,96},{160,128},{192,160},{224,1... | collective-permute-start | bytes 1572872 | tf_op jit(solution)/shard_map/ppermute | solution.py:190
  196.6 25.3 %copy-start.9 = (bf16[256,1024]{1,0:T(8,128)(2,1)}, bf16[256,1024]{1,0:T(8,128)(2,1)S(1)}, u32[]{:S(2)}) copy-start(bf16[256,1024]{1,0:T(8,128)(2,1)S(1)} %collective-permute-done.8.refs_2_) | copy-start | bytes 1572868
  196.6 24.5 %collective-permute-start.9 = (bf16[256,1024]{1,0:T(8,128)(2,1)S(1)}, bf16[256,1024]{1,0:T(8,128)(2,1)S(1)}, u32[]{:S(2)}, u32[]{:S(2)}) collective-permute-start(bf16[256,1024]{1,0:T(8,128)(2,1)S(1)} %collective-permute-done.8.refs_2_), channel_id=1, source_target_pairs={{0,32},{32,64},{64,96},{96,128},{128,160},{160,192},{192,224},{224... | collective-permute-start | bytes 1572872 | tf_op jit(solution)/shard_map/ppermute | solution.py:190
  218.3 10.2 %copy-start.4 = (bf16[256,1024]{1,0:T(8,128)(2,1)}, bf16[256,1024]{1,0:T(8,128)(2,1)S(1)}, u32[]{:S(2)}) copy-start(bf16[256,1024]{1,0:T(8,128)(2,1)S(1)} %collective-permute-done.13.refs_6_) | copy-start | bytes 1572868
  218.4 10.0 %collective-permute-start.14 = (bf16[128,1024]{1,0:T(8,128)(2,1)S(1)}, bf16[128,1024]{1,0:T(8,128)(2,1)}, u32[]{:S(2)}, u32[]{:S(2)}) collective-permute-start(bf16[128,1024]{1,0:T(8,128)(2,1)S(1)} %slice.9), channel_id=1, source_target_pairs={{0,224},{32,0},{64,32},{96,64},{128,96},{160,128},{192,160},{224,1... | collective-permute-start | bytes 786440 | tf_op jit(solution)/shard_map/ppermute | solution.py:190
  221.1 0.8 copy-start.5
  221.9 6.6 %collective-permute-start.10 = (bf16[128,1024]{1,0:T(8,128)(2,1)S(1)}, bf16[128,1024]{1,0:T(8,128)(2,1)}, u32[]{:S(2)}, u32[]{:S(2)}) collective-permute-start(bf16[128,1024]{1,0:T(8,128)(2,1)S(1)} %slice.8), channel_id=1, source_target_pairs={{0,32},{32,64},{64,96},{96,128},{128,160},{160,192},{192,224},{224... | collective-permute-start | bytes 786440 | tf_op jit(solution)/shard_map/ppermute | solution.py:190
Sparse Core Ops, SparseCore 0:
  77.7 148.4 reduce-scatter.1

commit v7 on v6

--- a/solution.py
+++ b/solution.py
@@ -50,6 +50,7 @@
         grads = contract(pick.astype(BF), grad_ref[...], ((1,), (0,))).astype(BF)
         if tile == 2:
             acts = jnp.where(lower, acts[:, :quarter], acts[:, quarter:])
+            grads = jnp.where(lower, grads[:, : grads.shape[1] // 2], grads[:, grads.shape[1] // 2 :])
         start = tile * width
         middle = start + acts.shape[1]
         for p in range(chips):
@@ -61,7 +62,7 @@
     tokens, features = act.shape
     pairs, hidden = grad.shape
     half = features // 2
-    width = 2 * (half + hidden) + half // 2 + hidden
+    width = 2 * (half + hidden) + (half + hidden) // 2
     return pl.pallas_call(
         functools.partial(fill_kernel, half),
         grid=(2,),
@@ -92,7 +93,12 @@
             @pl.when((pl.program_id(0) == pair) & (pl.program_id(1) == k))
             def _():
                 owner = row // 2 == pair * 2 + k
-                last = jnp.where(owner, rows(2 * width + quarter, hidden), jnp.zeros((), BF))
+                near = rows(2 * width + quarter, hidden // 2).astype(jnp.float32)
+                if pair == 0:
+                    ends = [near, pltpu.roll(near, count - TILE // 2, 0)]
+                else:
+                    ends = [pltpu.roll(near, TILE // 2, 0), near]
+                last = jnp.where(owner, jnp.concatenate(ends, axis=1), 0.0).astype(BF)
                 total = contract(rows(k * width + pair * quarter, quarter), rows(k * width + half, hidden), ((0,), (0,)))
                 total = total + contract(rows(2 * width, quarter), last, ((0,), (0,)))
                 out_ref[...] = total.astype(BF).reshape(out_ref.shape)

time: 291 us -> 288 us (0.990)
  no operation moved by 1% of the time
where the time goes in v7:
time: 288 us
  waiting for transfers between devices  114 us (40%)
  blocking collectives  95.2 us (33%)
  Pallas kernels  28.5 us (10%)
  starting transfers between devices  23.8 us (8%)
  between operations  14.3 us (5%)
  local copies, waits for them, and re-layouts  8.18 us (3%)
  matrix products  3.84 us (1%)
    ppermute x15, waiting for transfers between devices, ordered(): lax.ppermute(block_in, Z, [(z, target(z) % planes) for z in range(planes)])  114 us
    all_to_all x1, blocking collectives, shards(): lax.all_to_all(send_b.reshape(spots, TILE, send_b.shape[-1]), PLANE, 0, 0...  53.3 us
    all_to_all x1, blocking collectives, shards(): lax.all_to_all(rows_g, PLANE, 0, 0, tiled=True).reshape(total, hidden)  41.9 us
    ppermute x15, starting transfers between devices, ordered(): lax.ppermute(block_in, Z, [(z, target(z) % planes) for z in range(planes)])  19 us
    pallas_call x1, Pallas kernels, sort_grads(): pl.pallas_call(sort_grads_kernel, grid=(2,), in_specs=[pl.BlockSpec(memor...  9.38 us
    pallas_call x1, Pallas kernels, products(): pl.pallas_call(functools.partial(products_kernel, half, hidden), grid=(2,...  8.14 us
    pallas_call x1, Pallas kernels, sort_acts(): pl.pallas_call(functools.partial(sort_acts_kernel, spots, most), grid=(2,...  6.71 us
  transfers between devices with their start and end apart: 17, of which 10 were waited for; matrix products, arithmetic and copies ran while one was open for 3% of the time, Pallas kernels for 6%

profile of v7, /device:TPU:1, one launch (start us, length us, event | category | flops | bytes accessed | tf_op | source)
XLA Modules:
  0.0 288.0 jit_solution(8391743037841002304)
XLA Ops:
  7.2 0.0 reduce-scatter.2.cloned.1.call-start
  7.2 2.0 copy.21
  9.2 4.3 %fill_b.1 = bf16[16,2,8,7040]{3,2,1,0:T(8,128)(2,1)} custom-call(s32[2,128]{1,0:T(2,128)} %bitcast.65, bf16[128,3584]{1,0:T(8,128)(2,1)} %act_ref.1, bf16[256,1024]{1,0:T(8,128)(2,1)} %bitcast.61), custom_call_target="tpu_custom_call" | custom-call | flops 2000000000 | bytes 6000000 | tf_op jit(solution)/shard_map/fill_b/pallas_call | solution.py:66
  13.4 53.3 %all_to_all.15.in_ref = bf16[32,8,7040]{2,1,0:T(8,128)(2,1)} all-to-all(bf16[32,8,7040]{2,1,0:T(8,128)(2,1)} %bitcast.53), channel_id=1, replica_groups=mesh['zh'=4,'zl'=2,'x'=4,'y'=4,'c'=2] {'x','y','c'}, dimensions={0} | all-to-all | bytes 7208960 | tf_op jit(solution)/shard_map/all_to_all | solution.py:244
  66.7 8.1 %products_b.1 = bf16[4,2,448,1024]{3,2,1,0:T(8,128)(2,1)} custom-call(bf16[32,8,7040]{2,1,0:T(8,128)(2,1)} %all_to_all.15.in_ref), custom_call_target="tpu_custom_call" | custom-call | flops 4000000000 | bytes 12000000 | tf_op jit(solution)/shard_map/products_b/pallas_call | solution.py:109
  74.9 0.0 reduce-scatter.2.cloned.1.call-update
  74.9 0.6 copy-done.6
  75.6 0.1 convert_reduce_fusion
  75.7 0.4 copy-done
  76.1 0.2 reshape.39
  76.3 1.9 constant_dynamic-slice_fusion
  78.2 0.0 copy-start.1
  78.2 0.1 copy_bitcast_fusion
  78.3 0.1 copy_bitcast_fusion.2
  78.4 0.1 fusion.6
  78.5 5.7 %collective-permute-start.2 = (bf16[136,896]{1,0:T(8,128)(2,1)S(1)}, bf16[136,896]{1,0:T(8,128)(2,1)S(1)}, u32[]{:S(2)}, u32[]{:S(2)}) collective-permute-start(bf16[136,896]{1,0:T(8,128)(2,1)S(1)} %get-tuple-element.10), channel_id=1, source_target_pairs={{0,224},{32,64},{64,32},{96,128},{128,96},{160,192},{192,160},{224... | collective-permute-start | bytes 731144 | tf_op jit(solution)/shard_map/ppermute | solution.py:196
  84.1 1.6 collective-permute-start
  85.8 0.5 collective-permute-start.1
  86.3 16.4 %collective-permute-done.2.refs_3_ = bf16[136,896]{1,0:T(8,128)(2,1)S(1)} collective-permute-done((bf16[136,896]{1,0:T(8,128)(2,1)S(1)}, bf16[136,896]{1,0:T(8,128)(2,1)S(1)}, u32[]{:S(2)}, u32[]{:S(2)}) %collective-permute-start.2) | collective-permute-done | bytes 243744 | tf_op jit(solution)/shard_map/ppermute | solution.py:196
  102.7 0.0 collective-permute-start.6
  102.7 12.1 %collective-permute-done.refs_1_ = bf16[136,896]{1,0:T(8,128)(2,1)S(1)} collective-permute-done((bf16[136,896]{1,0:T(8,128)(2,1)S(1)}, bf16[136,896]{1,0:T(8,128)(2,1)S(1)}, u32[]{:S(2)}, u32[]{:S(2)}) %collective-permute-start) | collective-permute-done | bytes 243744 | tf_op jit(solution)/shard_map/ppermute | solution.py:196
  114.8 0.0 collective-permute-start.4
  114.8 1.5 collective-permute-start.5
  116.3 0.1 copy.20
  116.4 0.0 copy-start.2
  116.4 3.0 %collective-permute-start.11 = (bf16[256,1024]{1,0:T(8,128)(2,1)S(1)}, bf16[256,1024]{1,0:T(8,128)(2,1)S(1)}, u32[]{:S(2)}, u32[]{:S(2)}) collective-permute-start(bf16[256,1024]{1,0:T(8,128)(2,1)S(1)} %bitcast.58), channel_id=1, source_target_pairs={{0,224},{32,0},{64,32},{96,64},{128,96},{160,128},{192,160},{224,1... | collective-permute-start | bytes 1572872 | tf_op jit(solution)/shard_map/ppermute | solution.py:196
  119.4 0.7 stack.70.meta_ref
  120.1 3.2 %collective-permute-done.6.refs_7_ = bf16[136,896]{1,0:T(8,128)(2,1)S(1)} collective-permute-done((bf16[136,896]{1,0:T(8,128)(2,1)S(1)}, bf16[136,896]{1,0:T(8,128)(2,1)S(1)}, u32[]{:S(2)}, u32[]{:S(2)}) %collective-permute-start.6) | collective-permute-done | bytes 243744 | tf_op jit(solution)/shard_map/ppermute | solution.py:196
  123.3 10.4 %collective-permute-done.4.refs_5_ = bf16[136,896]{1,0:T(8,128)(2,1)S(1)} collective-permute-done((bf16[136,896]{1,0:T(8,128)(2,1)S(1)}, bf16[136,896]{1,0:T(8,128)(2,1)S(1)}, u32[]{:S(2)}, u32[]{:S(2)}) %collective-permute-start.4) | collective-permute-done | bytes 243744 | tf_op jit(solution)/shard_map/ppermute | solution.py:196
  133.7 10.4 %collective-permute-done.5.refs_6_ = bf16[136,896]{1,0:T(8,128)(2,1)S(1)} collective-permute-done((bf16[136,896]{1,0:T(8,128)(2,1)S(1)}, bf16[136,896]{1,0:T(8,128)(2,1)S(1)}, u32[]{:S(2)}, u32[]{:S(2)}) %collective-permute-start.5) | collective-permute-done | bytes 243744 | tf_op jit(solution)/shard_map/ppermute | solution.py:196
  144.2 0.7 copy-done.16
  144.9 6.7 %sort_acts.1 = (bf16[1280,896]{1,0:T(8,128)(2,1)}, s32[8,256]{1,0:T(8,128)}) custom-call(s32[9]{0:T(128)} %stack.70.meta_ref, bf16[136,896]{1,0:T(8,128)(2,1)} %copy-done.3, bf16[136,896]{1,0:T(8,128)(2,1)} %copy-done.11, bf16[136,896]{1,0:T(8,128)(2,1)} %copy-done.12, bf16[136,896]{1,0:T(8,128)(2,1)} %copy-done.10, bf16[136,896]{1,0:T(8,128)(2,1)} %copy-done.13, ...), custom_call_target="tpu_custom_call" | custom-call | flops 2400000000 | bytes 5000000 | tf_op jit(solution)/shard_map/sort_acts/pallas_call | solution.py:149
  151.6 4.7 %all-to-all-start = ((bf16[32,40,896]{2,1,0:T(8,128)(2,1)}), bf16[32,40,896]{2,1,0:T(8,128)(2,1)S(1)}, u32[]{:S(2)}, u32[]{:S(2)}) async-start(bf16[32,40,896]{2,1,0:T(8,128)(2,1)} %bitcast.55), calls=%async_computation | async-start | bytes 4587520 | tf_op jit(solution)/shard_map/all_to_all | solution.py:258
  156.4 10.3 %collective-permute-done.11.refs_8_ = bf16[256,1024]{1,0:T(8,128)(2,1)S(1)} collective-permute-done((bf16[256,1024]{1,0:T(8,128)(2,1)S(1)}, bf16[256,1024]{1,0:T(8,128)(2,1)S(1)}, u32[]{:S(2)}, u32[]{:S(2)}) %collective-permute-start.11) | collective-permute-done | bytes 524320 | tf_op jit(solution)/shard_map/ppermute | solution.py:196
  166.6 2.3 collective-permute-start.12
  168.9 22.8 %collective-permute-done.12.refs_7_ = bf16[256,1024]{1,0:T(8,128)(2,1)S(1)} collective-permute-done((bf16[256,1024]{1,0:T(8,128)(2,1)S(1)}, bf16[256,1024]{1,0:T(8,128)(2,1)S(1)}, u32[]{:S(2)}, u32[]{:S(2)}) %collective-permute-start.12) | collective-permute-done | bytes 524320 | tf_op jit(solution)/shard_map/ppermute | solution.py:196
  191.7 2.1 collective-permute-start.13
  193.8 0.2 collective-permute-start.9
  194.0 22.5 %collective-permute-done.13.refs_6_ = bf16[256,1024]{1,0:T(8,128)(2,1)S(1)} collective-permute-done((bf16[256,1024]{1,0:T(8,128)(2,1)S(1)}, bf16[256,1024]{1,0:T(8,128)(2,1)S(1)}, u32[]{:S(2)}, u32[]{:S(2)}) %collective-permute-start.13) | collective-permute-done | bytes 524320 | tf_op jit(solution)/shard_map/ppermute | solution.py:196
  216.6 2.0 collective-permute-start.14
  218.6 0.8 copy-done.5
  219.4 0.1 collective-permute-start.10
  219.5 0.7 stack.79.at_ref
  220.2 5.6 %collective-permute-done.14.refs_5_ = bf16[128,1024]{1,0:T(8,128)(2,1)} collective-permute-done((bf16[128,1024]{1,0:T(8,128)(2,1)S(1)}, bf16[128,1024]{1,0:T(8,128)(2,1)}, u32[]{:S(2)}, u32[]{:S(2)}) %collective-permute-start.14) | collective-permute-done | bytes 262176 | tf_op jit(solution)/shard_map/ppermute | solution.py:196
  225.8 0.2 collective-permute-done.10.refs_4_
  226.0 9.4 %sort_grads.1 = bf16[1280,1024]{1,0:T(8,128)(2,1)} custom-call(s32[8]{0:T(128)} %stack.79.at_ref, s32[8,256]{1,0:T(8,128)} %get-tuple-element.5.slots_ref, bf16[256,1024]{1,0:T(8,128)(2,1)} %bitcast.60, bf16[256,1024]{1,0:T(8,128)(2,1)} %collective-permute-done.7.refs_1_, bf16[256,1024]{1,0:T(8,128)(2,1)} %copy-done.9, bf16[256,1024]{1,0:T(8,128)(2,1)} %copy-done.5, ...), custom_call_target="tpu_custom_call" | custom-call | flops 5400000000 | bytes 7000000 | tf_op jit(solution)/shard_map/sort_grads/pallas_call | solution.py:181
  235.4 41.9 %all_to_all.16 = bf16[32,40,1024]{2,1,0:T(8,128)(2,1)S(1)} all-to-all(bf16[32,40,1024]{2,1,0:T(8,128)(2,1)} %bitcast.54), channel_id=1, replica_groups=mesh['zh'=4,'zl'=2,'x'=4,'y'=4,'c'=2] {'x','y','c'}, dimensions={0} | all-to-all | bytes 5242880 | tf_op jit(solution)/shard_map/all_to_all | solution.py:259
  277.3 3.8 %fusion = bf16[1,896,1024]{2,1,0:T(8,128)(2,1)} fusion(bf16[32,40,896]{2,1,0:T(8,128)(2,1)S(1)} %all-to-all-done, bf16[32,40,1024]{2,1,0:T(8,128)(2,1)S(1)} %all_to_all.16), kind=kOutput, calls=%fused_computation.1 | convolution fusion | flops 2349727744 | bytes 6750208 | tf_op jit(solution)/shard_map/dot_general | solution.py:18
  (44 shorter events, 0.1 us)
Async XLA Ops:
  7.2 274.0 %reduce-scatter.2.cloned.1.call-start = ((), (), s32[]{:S(2)}) async-start(), calls=%async_computation.4 | async-start | bytes 8257536 | tf_op jit(solution)/shard_map/reduce_scatter | solution.py:247
  74.9 0.7 copy-start.6
  74.9 1.2 copy-start
  78.2 38.0 %copy-start.1 = (bf16[128,2,1024]{2,1,0:T(2,128)(2,1)S(1)}, bf16[128,2,1024]{2,1,0:T(2,128)(2,1)}, u32[]{:S(2)}) copy-start(bf16[128,2,1024]{2,1,0:T(2,128)(2,1)} %param.7) | copy-start | bytes 1572868
  78.5 65.7 %copy-start.3 = (bf16[136,896]{1,0:T(8,128)(2,1)}, bf16[136,896]{1,0:T(8,128)(2,1)S(1)}, u32[]{:S(2)}) copy-start(bf16[136,896]{1,0:T(8,128)(2,1)S(1)} %get-tuple-element.11.refs_0_) | copy-start | bytes 731140
  78.5 24.3 %collective-permute-start.2 = (bf16[136,896]{1,0:T(8,128)(2,1)S(1)}, bf16[136,896]{1,0:T(8,128)(2,1)S(1)}, u32[]{:S(2)}, u32[]{:S(2)}) collective-permute-start(bf16[136,896]{1,0:T(8,128)(2,1)S(1)} %get-tuple-element.10), channel_id=1, source_target_pairs={{0,224},{32,64},{64,32},{96,128},{128,96},{160,192},{192,160},{224... | collective-permute-start | bytes 731144 | tf_op jit(solution)/shard_map/ppermute | solution.py:196
  84.1 30.7 %collective-permute-start = (bf16[136,896]{1,0:T(8,128)(2,1)S(1)}, bf16[136,896]{1,0:T(8,128)(2,1)S(1)}, u32[]{:S(2)}, u32[]{:S(2)}) collective-permute-start(bf16[136,896]{1,0:T(8,128)(2,1)S(1)} %get-tuple-element.12), channel_id=1, source_target_pairs={{0,160},{32,128},{64,224},{96,192},{128,32},{160,0},{192,96},{224,... | collective-permute-start | bytes 731144 | tf_op jit(solution)/shard_map/ppermute | solution.py:196
  85.8 29.0 %collective-permute-start.1 = (bf16[136,896]{1,0:T(8,128)(2,1)S(1)}, bf16[136,896]{1,0:T(8,128)(2,1)S(1)}, u32[]{:S(2)}, u32[]{:S(2)}) collective-permute-start(bf16[136,896]{1,0:T(8,128)(2,1)S(1)} %get-tuple-element.13), channel_id=1, source_target_pairs={{0,64},{32,224},{64,128},{96,32},{128,192},{160,96},{192,0},{224,1... | collective-permute-start | bytes 731144 | tf_op jit(solution)/shard_map/ppermute | solution.py:196
  86.3 33.8 %collective-permute-start.3 = (bf16[136,896]{1,0:T(8,128)(2,1)S(1)}, bf16[136,896]{1,0:T(8,128)(2,1)S(1)}, u32[]{:S(2)}, u32[]{:S(2)}) collective-permute-start(bf16[136,896]{1,0:T(8,128)(2,1)S(1)} %get-tuple-element.11.refs_0_), channel_id=1, source_target_pairs={{0,32},{32,0},{64,96},{96,64},{128,160},{160,128},{192,224},{224,1... | collective-permute-start | bytes 731144 | tf_op jit(solution)/shard_map/ppermute | solution.py:196
  102.7 41.4 %copy-start.10 = (bf16[136,896]{1,0:T(8,128)(2,1)}, bf16[136,896]{1,0:T(8,128)(2,1)S(1)}, u32[]{:S(2)}) copy-start(bf16[136,896]{1,0:T(8,128)(2,1)S(1)} %collective-permute-done.2.refs_3_) | copy-start | bytes 731140
  102.7 20.5 %collective-permute-start.6 = (bf16[136,896]{1,0:T(8,128)(2,1)S(1)}, bf16[136,896]{1,0:T(8,128)(2,1)S(1)}, u32[]{:S(2)}, u32[]{:S(2)}) collective-permute-start(bf16[136,896]{1,0:T(8,128)(2,1)S(1)} %collective-permute-done.2.refs_3_), channel_id=1, source_target_pairs={{0,32},{32,0},{64,96},{96,64},{128,160},{160,128},{192,224},{224,1... | collective-permute-start | bytes 731144 | tf_op jit(solution)/shard_map/ppermute | solution.py:196
  114.8 29.4 %copy-start.11 = (bf16[136,896]{1,0:T(8,128)(2,1)}, bf16[136,896]{1,0:T(8,128)(2,1)S(1)}, u32[]{:S(2)}) copy-start(bf16[136,896]{1,0:T(8,128)(2,1)S(1)} %collective-permute-done.refs_1_) | copy-start | bytes 731140
  114.8 18.9 %collective-permute-start.4 = (bf16[136,896]{1,0:T(8,128)(2,1)S(1)}, bf16[136,896]{1,0:T(8,128)(2,1)S(1)}, u32[]{:S(2)}, u32[]{:S(2)}) collective-permute-start(bf16[136,896]{1,0:T(8,128)(2,1)S(1)} %collective-permute-done.refs_1_), channel_id=1, source_target_pairs={{0,32},{32,0},{64,96},{96,64},{128,160},{160,128},{192,224},{224,1... | collective-permute-start | bytes 731144 | tf_op jit(solution)/shard_map/ppermute | solution.py:196
  114.8 29.4 %copy-start.12 = (bf16[136,896]{1,0:T(8,128)(2,1)}, bf16[136,896]{1,0:T(8,128)(2,1)S(1)}, u32[]{:S(2)}) copy-start(bf16[136,896]{1,0:T(8,128)(2,1)S(1)} %collective-permute-done.1.refs_2_) | copy-start | bytes 731140
  114.8 29.4 %collective-permute-start.5 = (bf16[136,896]{1,0:T(8,128)(2,1)S(1)}, bf16[136,896]{1,0:T(8,128)(2,1)S(1)}, u32[]{:S(2)}, u32[]{:S(2)}) collective-permute-start(bf16[136,896]{1,0:T(8,128)(2,1)S(1)} %collective-permute-done.1.refs_2_), channel_id=1, source_target_pairs={{0,32},{32,0},{64,96},{96,64},{128,160},{160,128},{192,224},{224,1... | collective-permute-start | bytes 731144 | tf_op jit(solution)/shard_map/ppermute | solution.py:196
  116.4 35.3 %copy-start.2 = (bf16[2,128,1024]{2,1,0:T(8,128)(2,1)}, bf16[2,128,1024]{2,1,0:T(8,128)(2,1)S(1)}, u32[]{:S(2)}) copy-start(bf16[2,128,1024]{2,1,0:T(8,128)(2,1)S(1)} %copy.20) | copy-start | bytes 1572868
  116.4 50.2 %collective-permute-start.11 = (bf16[256,1024]{1,0:T(8,128)(2,1)S(1)}, bf16[256,1024]{1,0:T(8,128)(2,1)S(1)}, u32[]{:S(2)}, u32[]{:S(2)}) collective-permute-start(bf16[256,1024]{1,0:T(8,128)(2,1)S(1)} %bitcast.58), channel_id=1, source_target_pairs={{0,224},{32,0},{64,32},{96,64},{128,96},{160,128},{192,160},{224,1... | collective-permute-start | bytes 1572872 | tf_op jit(solution)/shard_map/ppermute | solution.py:196
  120.1 24.1 %copy-start.13 = (bf16[136,896]{1,0:T(8,128)(2,1)}, bf16[136,896]{1,0:T(8,128)(2,1)S(1)}, u32[]{:S(2)}) copy-start(bf16[136,896]{1,0:T(8,128)(2,1)S(1)} %collective-permute-done.3.refs_4_) | copy-start | bytes 731140
  120.1 48.8 %collective-permute-start.7 = (bf16[256,1024]{1,0:T(8,128)(2,1)S(1)}, bf16[256,1024]{1,0:T(8,128)(2,1)}, u32[]{:S(2)}, u32[]{:S(2)}) collective-permute-start(bf16[256,1024]{1,0:T(8,128)(2,1)S(1)} %bitcast.59), channel_id=1, source_target_pairs={{0,32},{32,64},{64,96},{96,128},{128,160},{160,192},{192,224},{224... | collective-permute-start | bytes 1572872 | tf_op jit(solution)/shard_map/ppermute | solution.py:196
  123.3 20.9 %copy-start.14 = (bf16[136,896]{1,0:T(8,128)(2,1)}, bf16[136,896]{1,0:T(8,128)(2,1)S(1)}, u32[]{:S(2)}) copy-start(bf16[136,896]{1,0:T(8,128)(2,1)S(1)} %collective-permute-done.6.refs_7_) | copy-start | bytes 731140
  133.7 10.5 %copy-start.15 = (bf16[136,896]{1,0:T(8,128)(2,1)}, bf16[136,896]{1,0:T(8,128)(2,1)S(1)}, u32[]{:S(2)}) copy-start(bf16[136,896]{1,0:T(8,128)(2,1)S(1)} %collective-permute-done.4.refs_5_) | copy-start | bytes 731140
  144.2 0.7 copy-start.16
  151.6 83.8 %all-to-all-start = ((bf16[32,40,896]{2,1,0:T(8,128)(2,1)}), bf16[32,40,896]{2,1,0:T(8,128)(2,1)S(1)}, u32[]{:S(2)}, u32[]{:S(2)}) async-start(bf16[32,40,896]{2,1,0:T(8,128)(2,1)} %bitcast.55), calls=%async_computation | async-start | bytes 4587520 | tf_op jit(solution)/shard_map/all_to_all | solution.py:258
  166.6 2.3 copy-start.7
  166.6 25.1 %collective-permute-start.12 = (bf16[256,1024]{1,0:T(8,128)(2,1)S(1)}, bf16[256,1024]{1,0:T(8,128)(2,1)S(1)}, u32[]{:S(2)}, u32[]{:S(2)}) collective-permute-start(bf16[256,1024]{1,0:T(8,128)(2,1)S(1)} %collective-permute-done.11.refs_8_), channel_id=1, source_target_pairs={{0,224},{32,0},{64,32},{96,64},{128,96},{160,128},{192,160},{224,1... | collective-permute-start | bytes 1572872 | tf_op jit(solution)/shard_map/ppermute | solution.py:196
  168.9 24.9 %collective-permute-start.8 = (bf16[256,1024]{1,0:T(8,128)(2,1)}, bf16[256,1024]{1,0:T(8,128)(2,1)S(1)}, u32[]{:S(2)}, u32[]{:S(2)}) collective-permute-start(bf16[256,1024]{1,0:T(8,128)(2,1)} %collective-permute-done.7.refs_1_), channel_id=1, source_target_pairs={{0,32},{32,64},{64,96},{96,128},{128,160},{160,192},{192,224},{224... | collective-permute-start | bytes 1572872 | tf_op jit(solution)/shard_map/ppermute | solution.py:196
  191.7 2.3 copy-start.8
  191.7 24.8 %collective-permute-start.13 = (bf16[256,1024]{1,0:T(8,128)(2,1)S(1)}, bf16[256,1024]{1,0:T(8,128)(2,1)S(1)}, u32[]{:S(2)}, u32[]{:S(2)}) collective-permute-start(bf16[256,1024]{1,0:T(8,128)(2,1)S(1)} %collective-permute-done.12.refs_7_), channel_id=1, source_target_pairs={{0,224},{32,0},{64,32},{96,64},{128,96},{160,128},{192,160},{224,1... | collective-permute-start | bytes 1572872 | tf_op jit(solution)/shard_map/ppermute | solution.py:196
  193.8 25.6 %copy-start.9 = (bf16[256,1024]{1,0:T(8,128)(2,1)}, bf16[256,1024]{1,0:T(8,128)(2,1)S(1)}, u32[]{:S(2)}) copy-start(bf16[256,1024]{1,0:T(8,128)(2,1)S(1)} %collective-permute-done.8.refs_2_) | copy-start | bytes 1572868
  193.8 24.8 %collective-permute-start.9 = (bf16[256,1024]{1,0:T(8,128)(2,1)S(1)}, bf16[256,1024]{1,0:T(8,128)(2,1)S(1)}, u32[]{:S(2)}, u32[]{:S(2)}) collective-permute-start(bf16[256,1024]{1,0:T(8,128)(2,1)S(1)} %collective-permute-done.8.refs_2_), channel_id=1, source_target_pairs={{0,32},{32,64},{64,96},{96,128},{128,160},{160,192},{192,224},{224... | collective-permute-start | bytes 1572872 | tf_op jit(solution)/shard_map/ppermute | solution.py:196
  216.5 9.5 %copy-start.4 = (bf16[256,1024]{1,0:T(8,128)(2,1)}, bf16[256,1024]{1,0:T(8,128)(2,1)S(1)}, u32[]{:S(2)}) copy-start(bf16[256,1024]{1,0:T(8,128)(2,1)S(1)} %collective-permute-done.13.refs_6_) | copy-start | bytes 1572868
  216.6 9.3 %collective-permute-start.14 = (bf16[128,1024]{1,0:T(8,128)(2,1)S(1)}, bf16[128,1024]{1,0:T(8,128)(2,1)}, u32[]{:S(2)}, u32[]{:S(2)}) collective-permute-start(bf16[128,1024]{1,0:T(8,128)(2,1)S(1)} %slice.9), channel_id=1, source_target_pairs={{0,224},{32,0},{64,32},{96,64},{128,96},{160,128},{192,160},{224,1... | collective-permute-start | bytes 786440 | tf_op jit(solution)/shard_map/ppermute | solution.py:196
  218.6 0.8 copy-start.5
  219.4 6.6 %collective-permute-start.10 = (bf16[128,1024]{1,0:T(8,128)(2,1)S(1)}, bf16[128,1024]{1,0:T(8,128)(2,1)}, u32[]{:S(2)}, u32[]{:S(2)}) collective-permute-start(bf16[128,1024]{1,0:T(8,128)(2,1)S(1)} %slice.8), channel_id=1, source_target_pairs={{0,32},{32,64},{64,96},{96,128},{128,160},{160,192},{192,224},{224... | collective-permute-start | bytes 786440 | tf_op jit(solution)/shard_map/ppermute | solution.py:196
Sparse Core Ops, SparseCore 0:
  75.0 147.9 reduce-scatter.1
